TPU v7x, 32 devices: a whole 2x2x4 slice. The times are simulated.
32 devices in a mesh: dp: 8 (over z, y), tensor: 4 (over x, core).
Axes of the slice: x: 2, y: 2, z: 4, core: 2. Of those that a mesh axis runs over, the one named last changes fastest.
Arguments:
- resid_in: float32 [8, 2048, 1536], P('dp', 'tensor'), may hold values from -32 to 32
- norm_gain: float32 [1536], P(('dp', 'tensor')), may hold values from 0.5 to 1.5
- proj_zx: bfloat16 [1536, 2, 3072], P('dp', None, 'tensor'), may hold values from -0.15625 to 0.15625
- proj_dt: bfloat16 [1536, 48], P('dp', 'tensor'), may hold values from -0.15625 to 0.15625
- proj_bc: bfloat16 [1536, 256], P(('dp', 'tensor')), may hold values from -0.15625 to 0.15625
- conv_x_weight: float32 [4, 3072], P(None, 'tensor'), may hold values from -0.5 to 0.5
- conv_x_bias: float32 [3072], P('tensor'), may hold values from -0.5 to 0.5
- conv_bc_weight: float32 [4, 256], P(None, ('dp', 'tensor')), may hold values from -0.5 to 0.5
- conv_bc_bias: float32 [256], P(('dp', 'tensor')), may hold values from -0.5 to 0.5
- dt_bias: float32 [48], P('tensor'), may hold values from -5 to -2
- a_log: float32 [48], P('tensor'), may hold values from -4.6 to 0.5
- skip_gain: float32 [48], P('tensor'), may hold values from 0.25 to 1.75
- gate_gain: float32 [3072], P('tensor'), may hold values from 0.5 to 1.5
- proj_out: bfloat16 [3072, 1536], P('tensor', 'dp'), may hold values from -0.109375 to 0.109375
- cotangent: float32 [8, 2048, 1536], P('dp', 'tensor'), may hold values from -23 to 23
Outputs:
- block_out: float32 [8, 2048, 1536], P('dp', 'tensor')
- grad_resid_in: float32 [8, 2048, 1536], P('dp', 'tensor')
- grad_norm_gain: float32 [1536], P(('dp', 'tensor'))
- grad_proj_zx: float32 [1536, 2, 3072], P('dp', None, 'tensor')
- grad_proj_dt: float32 [1536, 48], P('dp', 'tensor')
- grad_proj_bc: float32 [1536, 256], P(('dp', 'tensor'))
- grad_conv_x_weight: float32 [4, 3072], P(None, 'tensor')
- grad_conv_x_bias: float32 [3072], P('tensor')
- grad_conv_bc_weight: float32 [4, 256], P(None, ('dp', 'tensor'))
- grad_conv_bc_bias: float32 [256], P(('dp', 'tensor'))
- grad_dt_bias: float32 [48], P('tensor')
- grad_a_log: float32 [48], P('tensor')
- grad_skip_gain: float32 [48], P('tensor')
- grad_gate_gain: float32 [3072], P('tensor')
- grad_proj_out: float32 [3072, 1536], P('tensor', 'dp')
All inputs are finite; a program needn't handle non-finite values.
Results may differ from a plain program's by a relative error of at most 0.012.
The roundings to bfloat16 on the way count: a program that leaves them out, or rounds other values in their place, can miss the bound.
Values may be sent and summed in bfloat16 or wider, within the bound.
A program may use at most 320 MiB of HBM per device.

v0:
```python
import jax
import jax.numpy as jnp
from jax import lax
from jax.sharding import PartitionSpec as P

K = 4
BLK = 256
DI = 3072


EPSILON = 1e-05


def causal_conv(values, weight, offset_bias):
    length = values.shape[0]
    padded = jnp.pad(values, ((K - 1, 0), (0, 0)))
    summed = jnp.zeros(values.shape, jnp.float32) + offset_bias[None, :]
    for offset in range(K):
        summed = summed + weight[offset][None, :] * padded[offset : offset + length]
    return summed


def state_space(x_act, bc_act, dt_raw, dt_bias, a_log, skip_gain):
    maximum_precision = lax.Precision.HIGHEST
    length = x_act.shape[0]
    head_count = a_log.shape[0]
    head_width = x_act.shape[1] // head_count
    state_size = bc_act.shape[1] // 2
    blocks = length // BLK
    step_sizes = jax.nn.softplus(dt_raw + dt_bias[None, :])
    log_rates = step_sizes * (-jnp.exp(a_log))[None, :]
    x_blocks = x_act.reshape(blocks, BLK, head_count, head_width)
    dt_blocks = step_sizes.reshape(blocks, BLK, head_count)
    log_cum = jnp.cumsum(log_rates.reshape(blocks, BLK, head_count), axis=1)
    b_in = bc_act[:, :state_size].reshape(blocks, BLK, state_size)
    c_out = bc_act[:, state_size:].reshape(blocks, BLK, state_size)
    scores = jnp.einsum("bin,bjn->bij", c_out, b_in, precision=maximum_precision)
    log_gaps = log_cum[:, :, None, :] - log_cum[:, None, :, :]
    position = jnp.arange(BLK, dtype=jnp.int32)
    causal = position[:, None] >= position[None, :]
    kernel = jnp.exp(jnp.where(causal[None, :, :, None], log_gaps, -jnp.inf))
    kernel = kernel * scores[..., None] * dt_blocks[:, None, :, :]
    inner_out = jnp.einsum("bijh,bjhp->bihp", kernel, x_blocks, precision=maximum_precision)
    tail_weight = jnp.exp(log_cum[:, -1:, :] - log_cum) * dt_blocks
    states = jnp.einsum(
        "bjn,bjh,bjhp->bhnp", b_in, tail_weight, x_blocks, precision=maximum_precision
    )
    block_decay = jnp.exp(log_cum[:, -1, :])

    def carry_state(entering, inputs):
        block_factor, block_state = inputs
        return (block_factor[:, None, None] * entering + block_state, entering)

    start_state = jnp.zeros((head_count, state_size, head_width), jnp.float32)
    unused, entering = lax.scan(carry_state, start_state, (block_decay, states))
    outer_out = (
        jnp.einsum("bin,bhnp->bihp", c_out, entering, precision=maximum_precision)
        * jnp.exp(log_cum)[..., None]
    )
    result = inner_out + outer_out + skip_gain[None, None, :, None] * x_blocks
    return result.reshape(length, head_count * head_width)


def scan_core(
    x_in,
    bc_in,
    dt_raw,
    conv_x_weight,
    conv_x_bias,
    conv_bc_weight,
    conv_bc_bias,
    dt_bias,
    a_log,
    skip_gain,
):
    x_act = jax.nn.silu(causal_conv(x_in, conv_x_weight, conv_x_bias))
    bc_act = jax.nn.silu(causal_conv(bc_in, conv_bc_weight, conv_bc_bias))
    return state_space(x_act, bc_act, dt_raw, dt_bias, a_log, skip_gain)


def pre_norm(seq_rows, gain):
    return (
        seq_rows * lax.rsqrt(jnp.mean(seq_rows * seq_rows, axis=-1, keepdims=True) + EPSILON) * gain
    )


def on_device(
    resid_in,
    norm_gain,
    proj_zx,
    proj_dt,
    proj_bc,
    conv_x_weight,
    conv_x_bias,
    conv_bc_weight,
    conv_bc_bias,
    dt_bias,
    a_log,
    skip_gain,
    gate_gain,
    proj_out,
    cotangent,
):
    maximum_precision = lax.Precision.HIGHEST
    full_gain, key_query_wide, full_conv_weight, full_conv_bias = (
        lax.all_gather(norm_gain, ("dp", "tensor"), axis=0, tiled=True),
        lax.all_gather(proj_bc.astype(jnp.float32), ("dp", "tensor"), axis=0, tiled=True),
        lax.all_gather(conv_bc_weight, ("dp", "tensor"), axis=1, tiled=True),
        lax.all_gather(conv_bc_bias, ("dp", "tensor"), axis=0, tiled=True),
    )
    key_query_weight = key_query_wide.astype(jnp.bfloat16)
    forward_gate_input_weight, forward_step_weight, forward_output_weight = (
        lax.all_gather(proj_zx, "dp", axis=0, tiled=True),
        lax.all_gather(proj_dt, "dp", axis=0, tiled=True),
        lax.all_gather(proj_out, "dp", axis=1, tiled=True),
    )
    normed, norm_back = jax.vjp(pre_norm, resid_in, full_gain)
    normed_half = normed.astype(jnp.bfloat16)
    row_segment = lax.all_gather(normed_half, "tensor", axis=1, tiled=True)
    gate_input_slice = jnp.einsum(
        "ugq,qpj->ugpj", row_segment, forward_gate_input_weight, preferred_element_type=jnp.float32
    )
    step_size_slice = jnp.einsum(
        "avm,mu->avu", row_segment, forward_step_weight, preferred_element_type=jnp.float32
    )
    key_query_slice = jnp.einsum(
        "etk,kw->etw", row_segment, key_query_weight, preferred_element_type=jnp.float32
    )
    collected_rows = row_segment
    gate_pre = gate_input_slice[:, :, 0]
    x_in = gate_input_slice[:, :, 1]
    core_fn = jax.vmap(scan_core, in_axes=(0, 0, 0, None, None, None, None, None, None, None))
    y_vals, core_back = jax.vjp(
        core_fn,
        x_in,
        key_query_slice,
        step_size_slice,
        conv_x_weight,
        conv_x_bias,
        full_conv_weight,
        full_conv_bias,
        dt_bias,
        a_log,
        skip_gain,
    )
    gate_act = jax.nn.silu(gate_pre)
    product = y_vals * gate_act
    square_sums = lax.psum(jnp.sum(product * product, axis=-1), "tensor")
    inv_gate = lax.rsqrt(square_sums / DI + EPSILON)[..., None]
    quotient = product * inv_gate
    gated_values = (quotient * gate_gain).astype(jnp.bfloat16)
    partial_output_sum = jnp.einsum(
        "gxw,wy->gxy", gated_values, forward_output_weight, preferred_element_type=jnp.float32
    )
    block_out = resid_in + lax.psum_scatter(
        partial_output_sum, "tensor", scatter_dimension=1, tiled=True
    )
    backward_gate_input_weight, backward_step_weight, backward_output_weight = (
        lax.all_gather(proj_zx, "dp", axis=0, tiled=True),
        lax.all_gather(proj_dt, "dp", axis=0, tiled=True),
        lax.all_gather(proj_out, "dp", axis=1, tiled=True),
    )
    row_segment = lax.all_gather(cotangent.astype(jnp.bfloat16), "tensor", axis=1, tiled=True)
    gated_output_gradient = jnp.einsum(
        "foz,wz->fow", row_segment, backward_output_weight, preferred_element_type=jnp.float32
    )
    output_weight_gradient = jnp.einsum(
        "vux,vuh->xh", gated_values, row_segment, preferred_element_type=jnp.float32
    )
    grad_gate = jnp.sum(gated_output_gradient * quotient, axis=(0, 1))
    d_quot = gated_output_gradient * gate_gain
    dot_sums = lax.psum(jnp.sum(d_quot * quotient, axis=-1), "tensor")
    d_prod = inv_gate * (d_quot - quotient * (dot_sums / DI)[..., None])
    d_y = d_prod * gate_act
    sigmoid_gate = jax.nn.sigmoid(gate_pre)
    d_gate = d_prod * y_vals * sigmoid_gate * (1.0 + gate_pre * (1.0 - sigmoid_gate))
    core_grads = core_back(d_y)
    d_x_in = core_grads[0]
    key_query_input_gradient = core_grads[1]
    d_dt_raw = core_grads[2]
    gate_input_gradient = jnp.stack([d_gate, d_x_in], axis=2).astype(jnp.bfloat16)
    step_size_gradient = d_dt_raw.astype(jnp.bfloat16)
    normalized_gradient = jnp.einsum(
        "xham,uam->xhu",
        gate_input_gradient,
        backward_gate_input_weight,
        preferred_element_type=jnp.float32,
    )
    normalized_gradient = normalized_gradient + jnp.einsum(
        "zap,qp->zaq", step_size_gradient, backward_step_weight, preferred_element_type=jnp.float32
    )
    normalized_gradient = normalized_gradient + jnp.einsum(
        "rta,ua->rtu", key_query_input_gradient, key_query_wide, precision=maximum_precision
    )
    d_local = lax.psum_scatter(normalized_gradient, "tensor", scatter_dimension=1, tiled=True)
    d_rows, grad_gain = norm_back(d_local)
    grad_resid = d_rows + cotangent
    gate_input_weight_gradient = jnp.einsum(
        "qex,qepz->xpz", collected_rows, gate_input_gradient, preferred_element_type=jnp.float32
    )
    step_weight_gradient = jnp.einsum(
        "aje,ajk->ek", collected_rows, step_size_gradient, preferred_element_type=jnp.float32
    )
    key_query_weight_gradient = jnp.einsum(
        "xjy,xjm->ym",
        collected_rows.astype(jnp.float32),
        key_query_input_gradient,
        precision=maximum_precision,
    )
    owned_zx, owned_dt, owned_out = (
        lax.psum_scatter(gate_input_weight_gradient, "dp", scatter_dimension=0, tiled=True),
        lax.psum_scatter(step_weight_gradient, "dp", scatter_dimension=0, tiled=True),
        lax.psum_scatter(output_weight_gradient, "dp", scatter_dimension=1, tiled=True),
    )
    owned_gain, owned_bc, owned_conv_weight, owned_conv_bias = (
        lax.psum_scatter(grad_gain, ("dp", "tensor"), scatter_dimension=0, tiled=True),
        lax.psum_scatter(
            key_query_weight_gradient, ("dp", "tensor"), scatter_dimension=0, tiled=True
        ),
        lax.psum_scatter(core_grads[5], ("dp", "tensor"), scatter_dimension=1, tiled=True),
        lax.psum_scatter(core_grads[6], ("dp", "tensor"), scatter_dimension=0, tiled=True),
    )
    summed_cxw, summed_cxb, summed_dtb, summed_alog, summed_skip, summed_gate = lax.psum(
        (core_grads[3], core_grads[4], core_grads[7], core_grads[8], core_grads[9], grad_gate), "dp"
    )
    return (
        block_out,
        grad_resid,
        owned_gain,
        owned_zx,
        owned_dt,
        owned_bc,
        summed_cxw,
        summed_cxb,
        owned_conv_weight,
        owned_conv_bias,
        summed_dtb,
        summed_alog,
        summed_skip,
        summed_gate,
        owned_out,
    )


def solution(mesh):
    return jax.shard_map(
        on_device,
        mesh=mesh,
        in_specs=(
            P("dp", "tensor", None),
            P(("dp", "tensor")),
            P("dp", None, "tensor"),
            P("dp", "tensor"),
            P(("dp", "tensor"), None),
            P(None, "tensor"),
            P("tensor"),
            P(None, ("dp", "tensor")),
            P(("dp", "tensor")),
            P("tensor"),
            P("tensor"),
            P("tensor"),
            P("tensor"),
            P("tensor", "dp"),
            P("dp", "tensor", None),
        ),
        out_specs=(
            P("dp", "tensor", None),
            P("dp", "tensor", None),
            P(("dp", "tensor")),
            P("dp", None, "tensor"),
            P("dp", "tensor"),
            P(("dp", "tensor"), None),
            P(None, "tensor"),
            P("tensor"),
            P(None, ("dp", "tensor")),
            P(("dp", "tensor")),
            P("tensor"),
            P("tensor"),
            P("tensor"),
            P("tensor"),
            P("tensor", "dp"),
        ),
        check_vma=False,
    )
```

profile of v0, /device:TPU:0, one launch (start us, length us, event | category | flops | bytes accessed | tf_op | source)
XLA Modules:
  0.0 1311.9 jit_solution(16323796765738089239)
XLA Ops:
  11.3 42.1 %all-reduce.28 = (f32[1536]{0:T(1024)S(1)}, f32[256]{0:T(256)S(1)}) all-reduce(f32[1536]{0:T(1024)S(1)} %dynamic-update-slice, f32[256]{0:T(256)S(1)} %dynamic-update-slice.1), channel_id=1, replica_groups=mesh['dp'=8,'tensor'=4] {'dp','tensor'}, use_global_device_ids=true, to_apply=%add.22 | all-reduce | flops 1792 | bytes 14336
  61.9 30.5 %all-gather = bf16[8,192,12]{1,2,0:T(8,128)(2,1)S(1)} all-gather(bf16[1,192,12]{1,2,0:T(8,128)(2,1)S(1)} %bitcast.509), channel_id=1, replica_groups=mesh['dp'=8,'tensor'=4] {'dp'}, dimensions={0}, use_global_device_ids=true | all-gather | bytes 41472 | tf_op jit(solution)/shard_map/all_gather | solution.py:114
  92.6 40.5 %all-gather.1 = f32[32,8,4]{1,2,0:T(4,128)S(1)} all-gather(f32[1,8,4]{1,2,0:T(4,128)S(1)} %bitcast.517), channel_id=1, replica_groups=mesh['dp'=8,'tensor'=4] {'dp','tensor'}, dimensions={0}, use_global_device_ids=true | all-gather | bytes 4224 | tf_op jit(solution)/shard_map/all_gather | solution.py:108
  144.7 17.0 %all-gather.12.cloned.1.call-done = f32[1536,256]{1,0:T(8,128)} async-done(((f32[48,256]{1,0:T(8,128)}), f32[1536,256]{1,0:T(8,128)}) %all-gather.12.cloned.1.call-update) | async-done | bytes 1572880 | tf_op jit(solution)/shard_map/all_gather | solution.py:107
  172.0 70.9 %all-gather.10.cloned.1.call-done = bf16[1536,2,768]{2,0,1:T(8,128)(2,1)} async-done(((bf16[192,2,768]{2,0,1:T(8,128)(2,1)}), bf16[1536,2,768]{2,0,1:T(8,128)(2,1)}) %all-gather.10.cloned.1.call-update) | async-done | bytes 4718608 | tf_op jit(solution)/shard_map/all_gather | solution.py:113
  242.9 16.0 %fusion.64 = f32[1,2048,2,768]{3,1,2,0:T(8,128)} fusion(bf16[1536,2,768]{2,0,1:T(8,128)(2,1)} %all-gather.10.cloned.1.call-done, bf16[1,2048,1536]{2,1,0:T(8,128)(2,1)} %all-gather.8.cloned.1.call-done), kind=kOutput, calls=%fused_computation.114 | convolution fusion | flops 9663676416 | bytes 23592960 | tf_op jit(solution)/shard_map/ugq,qpj->ugpj/dot_general | solution.py:120
  258.9 10.0 fusion.151
  316.5 19.7 %while.34 = (s32[]{:T(128)}, f32[1,12,128,64]{3,2,1,0:T(8,128)S(1)}, f32[8,1,12,128,64]{4,3,2,1,0:T(8,128)}, f32[8,1,12,1,1]{2,4,3,1,0:T(1,128)S(1)}, f32[8,1,12...) while((s32[]{:T(128)}, f32[1,12,128,64]{3,2,1,0:T(8,128)S(1)}, ...), condition=%wide.region_4.5_spmd.clone, body=%wide.region_3.4_spmd.clone.sunk | while | flops 393219 | bytes 3933448 | solution.py:55
  350.1 37.5 %multiply_reduce_fusion.9 = (f32[8,256]{1,0:T(8,128)S(1)}, f32[1,8,256,12,64]{2,4,3,1,0:T(8,128)}, f32[1,8,256,12,64]{2,4,3,1,0:T(8,128)S(1)}) fusion(f32[1,8,256,12,64]{2,1,4,3,0:T(8,128)} %bitcast.473, f32[1,8,256,12,64]{2,1,4,3,0:T(8,128)S(1)} %bitcast.443, f32[12]{0:T(128)S(1)} %copy-done.84, f32[8,256,12,64]{1,3,2,0:T(8,128)S(1)} %bitcast.464, ...), kind=kOutput, calls=%fused_computation.96 | convolution fusion | flops 4874303488 | bytes 40214576 | tf_op jit(solution)/shard_map/jvp(vmap(bijh,bjhp->bihp))/dot_general | solution.py:43
  411.8 15.1 %multiply_reduce_fusion.2 = (f32[768]{0:T(1024)}, f32[2048]{0:T(1024)S(1)}, f32[2048,768]{1,0:T(8,128)}, f32[2048,768]{1,0:T(8,128)}) fusion(f32[768]{0:T(1024)S(1)} %copy-done.49, f32[2048]{0:T(1024)S(1)} %bitcast.492, f32[2048,768]{1,0:T(8,128)} %copy.324, f32[1,2048,2,768]{3,1,2,0:T(8,128)} %fusion.64, ...), kind=kOutput, calls=%fused_computation.87 | convolution fusion | flops 4849136640 | bytes 33839104 | tf_op jit(solution)/shard_map/foz,wz->fow/dot_general | solution.py:164
  433.6 12.1 fusion.81
  446.6 10.7 fusion.26
  474.5 42.5 %fusion.7 = (f32[8,256,12]{1,2,0:T(8,128)S(1)}, f32[8,256,12]{1,2,0:T(8,128)S(1)}, f32[8,256,12]{1,2,0:T(8,128)}, f32[8,256,256]{2,1,0:T(8,128)}) fusion(f32[8,256,12]{1,2,0:T(8,128)S(1)} %copy-done.39, f32[8,256,256]{2,1,0:T(8,128)S(1)} %copy-done.28, f32[8,256,12]{1,2,0:T(8,128)S(1)} %copy-done.42, pred[256,256]{1,0:T(8,128)(4,1)S(1)} %copy-done.47, ...), kind=kOutput, calls=%fused_computation.24 | convolution fusion | flops 4913029120 | bytes 17334272 | tf_op jit(solution)/shard_map/transpose(jvp(vmap(bijh,bjhp->bihp)))/dot_general | solution.py:43
  529.3 29.8 %while.35 = (s32[]{:T(128)}, f32[1,12,128,64]{3,2,1,0:T(8,128)S(1)}, f32[8,1,12]{2,1,0:T(1,128)S(1)}, f32[8,1,12,128,64]{4,3,2,1,0:T(8,128)}, f32[8,1,12,128,64]...) while((s32[]{:T(128)}, ...), condition=%wide.region_12.13_spmd.clone, body=%wide.region_10.12_spmd.clone.sunk | while | flops 589816 | bytes 4326744 | solution.py:55
  559.1 13.0 fusion.83
  579.5 25.7 %bitcast_add_fusion.3 = f32[1,8,256,12,64]{2,4,3,1,0:T(8,128)S(1)} fusion(f32[8,256,12,64]{1,3,2,0:T(8,128)S(1)} %fusion.83, f32[8,256,12,64]{1,0,3,2:T(8,128)S(1)} %bitcast.452, f32[12]{0:T(128)S(1)} %copy-done.84, f32[8,256,12]{1,2,0:T(8,128)S(1)} %copy-done.31, f32[8,256,12]{1,2,0:T(8,128)S(1)} %copy-done.40, f32[8,256,256]{2,1,0:T(8,128)S(1)} %copy-done.29, ...), kind=kOutput, calls=%fused_computation.50 | convolution fusion | flops 4863295488 | bytes 27623472 | tf_op jit(solution)/shard_map/transpose(jvp(vmap(bijh,bjhp->bihp)))/dot_general | solution.py:43
  626.2 17.6 %multiply_reduce_fusion.5 = (f32[768]{0:T(1024)}, f32[768]{0:T(1024)S(1)}, f32[768]{0:T(1024)S(1)}, f32[768]{0:T(1024)}, f32[768]{0:T(1024)S(1)}, /*index=5*/f32[1,2048,768]{2,1,0:T(8,128)}) fusion(f32[1,2048,768]{2,1,0:T(8,128)} %get-tuple-element.486, f32[1,2048,2,768]{3,1,2,0:T(8,128)} %fusion.64, f32[1,2048,768]{2,1,0:T(8,128)} %get-tuple-element.482, ...), kind=kLoop, calls=%fused_computation.90 | loop fusion | flops 28307712 | bytes 31472640 | tf_op jit(solution)/shard_map/transpose(jvp(vmap()))/reduce_sum | solution.py:19
  644.7 19.9 %reduce-window.16 = f32[1,8,12,2,128]{4,2,3,1,0:T(8,128)S(1)} reduce-window(f32[1,8,12,2,128]{4,2,3,1,0:T(8,128)S(1)} %copy.352, f32[]{:T(128)} %constant.101.clone.1), window={size=1x1x1x1x128 pad=0_0x0_0x0_0x0_0x0_127}, to_apply=%region_18.19 | reduce-window | flops 3121152 | bytes 196612 | tf_op jit(solution)/shard_map/reduce-window.2
  682.1 14.6 %fusion.41 = f32[1536,2,768]{2,0,1:T(8,128)} fusion(bf16[1,2048,1536]{2,1,0:T(8,128)(2,1)} %all-gather.8.cloned.1.call-done, bf16[2048,1,768]{2,0,1:T(8,128)(2,1)} %fusion.75, bf16[2048,1,768]{2,0,1:T(8,128)(2,1)S(1)} %copy-done.20), kind=kOutput, calls=%fused_computation.72 | convolution fusion | flops 9676259328 | bytes 22020096 | tf_op jit(solution)/shard_map/qex,qepz->xpz/dot_general | solution.py:198
  700.4 15.6 %fusion.111 = f32[1,8,256,128]{2,3,1,0:T(8,128)S(1)} fusion(f32[1,8,256,128]{2,3,1,0:T(8,128)S(1)} %convolution_bitcast_fusion.1, f32[8,256,12,64]{1,0,3,2:T(8,128)} %bitcast.439, f32[8,256,12]{1,2,0:T(8,128)S(1)} %copy-done.31, f32[8,1,12,128,64]{4,3,2,1,0:T(8,128)} %get-tuple-element.192), kind=kOutput, calls=%fused_computation.162 | convolution fusion | flops 2417754112 | bytes 11632640 | tf_op jit(solution)/shard_map/transpose(jvp(vmap(bjn,bjh,bjhp->bhnp)))/dot_general | solution.py:45
  716.4 24.0 %fusion.103 = f32[8,256,128]{2,1,0:T(8,128)S(1)} fusion(f32[8,256,12,64]{1,0,3,2:T(8,128)} %bitcast.450, f32[8,256,12]{1,2,0:T(8,128)S(1)} %copy.320, f32[8,1,12,128,64]{4,3,2,1,0:T(8,128)} %get-tuple-element.665), kind=kOutput, calls=%fused_computation.158 | convolution fusion | flops 2417491968 | bytes 10584064 | tf_op jit(solution)/shard_map/transpose(jvp(vmap(bin,bhnp->bihp)))/dot_general | solution.py:57
  750.1 14.8 %fusion.73 = f32[2048,1536,1]{1,0,2:T(8,128)} fusion(bf16[1536,2,768]{2,0,1:T(8,128)(2,1)} %all-gather.10.cloned.1.call-done, bf16[2048,1,768]{2,0,1:T(8,128)(2,1)S(1)} %copy-done.22, bf16[2048,1,768]{2,0,1:T(8,128)(2,1)S(1)} %copy-done.21), kind=kOutput, calls=%fused_computation.122 | convolution fusion | flops 9666822144 | bytes 23592960 | tf_op jit(solution)/shard_map/xham,uam->xhu/dot_general | solution.py:183
  764.9 17.5 %fusion.9 = f32[1,2048,1536]{2,1,0:T(8,128)} fusion(f32[2048,1536]{1,0:T(8,128)S(1)} %fusion.130, f32[2048,1536,1]{1,0,2:T(8,128)} %fusion.73, f32[2048,256]{1,0:T(8,128)} %fusion.91, f32[1536,256]{1,0:T(8,128)} %all-gather.12.cloned.1.call-done), kind=kOutput, calls=%fused_computation.27 | convolution fusion | flops 9669967872 | bytes 41418752 | tf_op jit(solution)/shard_map/rta,ua->rtu/dot_general | solution.py:192
  783.1 10.7 convolution_bitcast_fusion
  795.5 10.1 fusion.51
  820.4 36.2 %all-reduce.29 = (f32[4,768]{1,0:T(4,128)}, f32[768]{0:T(1024)}, f32[12]{0:T(128)}, f32[12]{0:T(128)}, f32[12]{0:T(128)}, /*index=5*/f32[768]{0:T(1024)}) all-reduce(f32[4,768]{1,0:T(4,128)S(1)} %pad_add_fusion.6, f32[768]{0:T(1024)S(1)} %copy-done.67, f32[12]{0:T(128)S(1)} %get-tuple-element.470, ...), channel_id=1, replica_groups=mesh['dp'=8,'tensor'=4] {'dp'}, use_global_device_ids=true, to_apply=%region_32.33 | all-reduce | flops 4644 | bytes 37152 | tf_op jit(solution)/shard_map/psum | solution.py:223
  858.3 39.7 %reduce-scatter.14.cloned.1.call-done = f32[192,2,768]{2,0,1:T(8,128)} async-done(((f32[1536,2,768]{2,0,1:T(8,128)}), f32[192,2,768]{2,0,1:T(8,128)}) %reduce-scatter.14.cloned.1.call-update) | async-done | bytes 1179664 | tf_op jit(solution)/shard_map/reduce_scatter | solution.py:211
  901.2 98.3 %reduce-scatter.12.cloned.1.call-done = f32[1,512,1536]{2,1,0:T(8,128)} async-done(((f32[1,2048,1536]{2,1,0:T(8,128)}), f32[1,512,1536]{2,1,0:T(8,128)}) %reduce-scatter.12.cloned.1.call-update) | async-done | bytes 3145744 | tf_op jit(solution)/shard_map/reduce_scatter | solution.py:195
  1002.2 40.1 %all-reduce.27 = (f32[1536]{0:T(1024)S(1)}, f32[4,256]{1,0:T(4,128)S(1)}, f32[256]{0:T(256)S(1)}) all-reduce(f32[1536]{0:T(1024)S(1)} %get-tuple-element.418, f32[4,256]{1,0:T(4,128)S(1)} %pad_add_fusion.7, f32[256]{0:T(256)S(1)} %get-tuple-element.423), channel_id=4, replica_groups=mesh['dp'=8,'tensor'=4] {'dp','tensor'}, use_global_device_ids=true, to_apply=%region_24.25.clone | all-reduce | flops 2816 | bytes 22528
  1044.1 58.5 %reduce-scatter.10.cloned.1.call-done = f32[1,512,1536]{2,1,0:T(8,128)} async-done(((f32[1,2048,1536]{2,1,0:T(8,128)}), f32[1,512,1536]{2,1,0:T(8,128)}) %reduce-scatter.10.cloned.1.call-update) | async-done | bytes 3145744 | tf_op jit(solution)/shard_map/reduce_scatter | solution.py:155
  1109.9 96.2 %reduce-scatter.16.cloned.1.call-done = f32[48,256]{1,0:T(8,128)} async-done(((f32[1536,256]{1,0:T(8,128)}), f32[48,256]{1,0:T(8,128)}) %reduce-scatter.16.cloned.1.call-update) | async-done | bytes 49168 | tf_op jit(solution)/shard_map/reduce_scatter | solution.py:217
  1206.1 99.0 %reduce-scatter.18.cloned.1.call-done = f32[768,192]{0,1:T(8,128)} async-done(((f32[768,1536]{0,1:T(8,128)}), f32[768,192]{0,1:T(8,128)}) %reduce-scatter.18.cloned.1.call-update) | async-done | bytes 589840 | tf_op jit(solution)/shard_map/reduce_scatter | solution.py:213
  (435 shorter events, 298.9 us)
Async XLA Ops:
  7.2 49.7 %copy-start.62 = (bf16[48,256]{1,0:T(8,128)(2,1)S(1)}, bf16[48,256]{1,0:T(8,128)(2,1)}, u32[]{:S(2)}) copy-start(bf16[48,256]{1,0:T(8,128)(2,1)} %param.23) | copy-start | bytes 73732
  7.2 53.1 %copy-start.15 = (f32[1,512,1536]{2,1,0:T(8,128)S(1)}, f32[1,512,1536]{2,1,0:T(8,128)}, u32[]{:S(2)}) copy-start(f32[1,512,1536]{2,1,0:T(8,128)} %param.33) | copy-start | bytes 9437188
  7.2 126.0 %all-gather.8.cloned.1.call-start = ((), (), s32[]{:S(2)}) async-start(), calls=%async_computation.6 | async-start | bytes 7864320 | tf_op jit(solution)/shard_map/all_gather | solution.py:119
  9.6 52.0 %copy-start.59 = (f32[512]{0:T(512)}, f32[512]{0:T(512)S(1)}, u32[]{:S(2)}) copy-start(f32[512]{0:T(512)S(1)} %fusion.137) | copy-start | bytes 6148
  56.8 76.4 %copy-start.82 = (f32[12]{0:T(128)S(1)}, f32[12]{0:T(128)}, u32[]{:S(2)}) copy-start(f32[12]{0:T(128)} %param.28) | copy-start | bytes 148
  56.9 104.9 %all-gather.12.cloned.1.call-start = ((), (), s32[]{:S(2)}) async-start(), calls=%async_computation.8 | async-start | bytes 1622016 | tf_op jit(solution)/shard_map/all_gather | solution.py:107
  57.6 185.2 %all-gather.10.cloned.1.call-start = ((), (), s32[]{:S(2)}) async-start(), calls=%async_computation.7 | async-start | bytes 5308416 | tf_op jit(solution)/shard_map/all_gather | solution.py:113
  59.6 352.2 %all-gather.14.cloned.1.call-start = ((), (), s32[]{:S(2)}) async-start(), calls=%async_computation.9 | async-start | bytes 2654208 | tf_op jit(solution)/shard_map/all_gather | solution.py:115
  60.2 351.6 %all-gather.16.cloned.1.call-start = ((), (), s32[]{:S(2)}) async-start(), calls=%async_computation.11 | async-start | bytes 7864320 | tf_op jit(solution)/shard_map/all_gather | solution.py:163
  61.6 795.1 %reduce-scatter.20.cloned.1.call-start = ((), (), s32[]{:S(2)}) async-start(), calls=%async_computation.16 | async-start | bytes 884736
  61.7 288.3 %copy-start.46 = (pred[256,256]{1,0:T(8,128)(4,1)}, pred[256,256]{1,0:T(8,128)(4,1)S(1)}, u32[]{:S(2)}) copy-start(pred[256,256]{1,0:T(8,128)(4,1)S(1)} %iota_compare_fusion) | copy-start | bytes 196612
  61.8 82.2 %copy-start.78 = (f32[12]{0:T(128)}, f32[12]{0:T(128)S(1)}, u32[]{:S(2)}) copy-start(f32[12]{0:T(128)S(1)} %exponential_negate_fusion) | copy-start | bytes 148
  61.8 222.5 %copy-start.51 = (f32[768]{0:T(1024)}, f32[768]{0:T(1024)S(1)}, u32[]{:S(2)}) copy-start(f32[768]{0:T(1024)S(1)} %get-tuple-element.425) | copy-start | bytes 9220
  61.8 222.5 %copy-start.53 = (f32[768]{0:T(1024)}, f32[768]{0:T(1024)S(1)}, u32[]{:S(2)}) copy-start(f32[768]{0:T(1024)S(1)} %get-tuple-element.426) | copy-start | bytes 9220
  61.9 222.5 %copy-start.55 = (f32[768]{0:T(1024)}, f32[768]{0:T(1024)S(1)}, u32[]{:S(2)}) copy-start(f32[768]{0:T(1024)S(1)} %get-tuple-element.427) | copy-start | bytes 9220
  61.9 222.5 %copy-start.57 = (f32[768]{0:T(1024)}, f32[768]{0:T(1024)S(1)}, u32[]{:S(2)}) copy-start(f32[768]{0:T(1024)S(1)} %get-tuple-element.428) | copy-start | bytes 9220
  92.6 51.2 %copy-start.33 = (bf16[1536,12]{0,1:T(8,128)(2,1)}, bf16[1536,12]{0,1:T(8,128)(2,1)S(1)}, u32[]{:S(2)}) copy-start(bf16[1536,12]{0,1:T(8,128)(2,1)S(1)} %reshape.822) | copy-start | bytes 110596
  144.1 206.0 %copy-start.38 = (f32[8,256,12]{1,2,0:T(8,128)}, f32[8,256,12]{1,2,0:T(8,128)S(1)}, u32[]{:S(2)}) copy-start(f32[8,256,12]{1,2,0:T(8,128)S(1)} %copy.310) | copy-start | bytes 294916
  144.1 205.9 %copy-start.41 = (f32[8,256,12]{1,2,0:T(8,128)}, f32[8,256,12]{1,2,0:T(8,128)S(1)}, u32[]{:S(2)}) copy-start(f32[8,256,12]{1,2,0:T(8,128)S(1)} %copy.307) | copy-start | bytes 294916
  144.7 159.6 %copy-start.30 = (f32[8,256,12]{1,2,0:T(8,128)}, f32[8,256,12]{1,2,0:T(8,128)S(1)}, u32[]{:S(2)}) copy-start(f32[8,256,12]{1,2,0:T(8,128)S(1)} %copy.315) | copy-start | bytes 294916
  344.4 43.2 %copy-start.27 = (f32[8,256,256]{2,1,0:T(8,128)}, f32[8,256,256]{2,1,0:T(8,128)S(1)}, u32[]{:S(2)}) copy-start(f32[8,256,256]{2,1,0:T(8,128)S(1)} %fusion.155) | copy-start | bytes 6291460
  470.0 47.0 %copy-start.1 = (f32[96,8,8,256]{3,2,1,0:T(8,128)}, f32[96,8,8,256]{3,2,1,0:T(8,128)S(1)}, u32[]{:S(2)}) copy-start(f32[96,8,8,256]{3,2,1,0:T(8,128)S(1)} %copy.396) | copy-start | bytes 18874372
  626.1 39.0 %copy-start.32 = (f32[2048,12]{0,1:T(8,128)S(1)}, f32[2048,12]{0,1:T(8,128)}, u32[]{:S(2)}) copy-start(f32[2048,12]{0,1:T(8,128)} %get-tuple-element.510) | copy-start | bytes 294916
  670.9 227.1 %reduce-scatter.14.cloned.1.call-start = ((), (), s32[]{:S(2)}) async-start(), calls=%async_computation.13 | async-start | bytes 10616832 | tf_op jit(solution)/shard_map/reduce_scatter | solution.py:211
  696.7 302.8 %reduce-scatter.12.cloned.1.call-start = ((), (), s32[]{:S(2)}) async-start(), calls=%async_computation.12 | async-start | bytes 15728640 | tf_op jit(solution)/shard_map/reduce_scatter | solution.py:195
  782.5 320.1 %reduce-scatter.10.cloned.1.call-start = ((), (), s32[]{:S(2)}) async-start(), calls=%async_computation.10 | async-start | bytes 15728640 | tf_op jit(solution)/shard_map/reduce_scatter | solution.py:155
  793.9 412.2 %reduce-scatter.16.cloned.1.call-start = ((), (), s32[]{:S(2)}) async-start(), calls=%async_computation.14 | async-start | bytes 1622016 | tf_op jit(solution)/shard_map/reduce_scatter | solution.py:217
  805.7 499.4 %reduce-scatter.18.cloned.1.call-start = ((), (), s32[]{:S(2)}) async-start(), calls=%async_computation.15 | async-start | bytes 5308416 | tf_op jit(solution)/shard_map/reduce_scatter | solution.py:213
  820.1 179.5 %copy-start.5 = (f32[1,512,1536]{2,1,0:T(8,128)S(1)}, f32[1,512,1536]{2,1,0:T(8,128)}, u32[]{:S(2)}) copy-start(f32[1,512,1536]{2,1,0:T(8,128)} %param.19) | copy-start | bytes 9437188
  820.1 179.5 %copy-start.45 = (f32[1536]{0:T(1024)S(1)}, f32[1536]{0:T(1024)}, u32[]{:S(2)}) copy-start(f32[1536]{0:T(1024)} %copy-done.44) | copy-start | bytes 18436
  820.1 179.5 %copy-start.60 = (f32[512]{0:T(512)S(1)}, f32[512]{0:T(512)}, u32[]{:S(2)}) copy-start(f32[512]{0:T(512)} %copy-done.59) | copy-start | bytes 6148
  820.1 224.0 %copy-start.64 = (f32[512]{0:T(512)S(1)}, f32[512]{0:T(512)}, u32[]{:S(2)}) copy-start(f32[512]{0:T(512)} %copy-done.63) | copy-start | bytes 6148
  (72 other events, 904.3 us)
Sparse Core Ops, SparseCore 0:
  57.0 46.2 all-gather.7
  106.8 54.9 all-gather.11
  164.5 78.3 all-gather.9
  244.9 50.1 all-gather.13
  297.1 44.8 all-gather.15
  671.1 61.3 reduce-scatter.19
  736.0 161.9 reduce-scatter.13
  900.6 98.9 reduce-scatter.11
  1002.2 100.4 reduce-scatter.9
  1108.3 97.7 reduce-scatter.15
  1210.4 94.6 reduce-scatter.17
where the time goes:
time: 1320 us; the launch traced here: 1310 us
  waiting for transfers between devices  480 us (36%)
  matrix products  312 us (24%)
  blocking collectives  202 us (15%)
  other arithmetic  153 us (12%)
  local copies, waits for them, and re-layouts  147 us (11%)
  between operations  15.8 us (1%)
    dot_general x3, matrix products, state_space(): jnp.einsum('bijh,bjhp->bihp', kernel, x_blocks, precision=maximum_precision)  106 us
    reduce_scatter x1, waiting for transfers between devices, on_device(): lax.psum_scatter(output_weight_gradient, 'dp', scatter_dimension=1, tiled...  99 us
    reduce_scatter x1, waiting for transfers between devices, on_device(): lax.psum_scatter(normalized_gradient, 'tensor', scatter_dimension=1, tile...  98.3 us
    reduce_scatter x1, waiting for transfers between devices, on_device(): lax.psum_scatter(key_query_weight_gradient, ('dp', 'tensor'), scatter_dim...  96.2 us
    unnamed x2, blocking collectives  82.2 us
    all_gather x1, waiting for transfers between devices, on_device(): lax.all_gather(proj_zx, 'dp', axis=0, tiled=True)  70.9 us
    reduce_scatter x1, waiting for transfers between devices, on_device(): lax.psum_scatter(partial_output_sum, 'tensor', scatter_dimension=1, tiled...  58.5 us
    unnamed x210, local copies, waits for them, and re-layouts  45.4 us
  transfers between devices with their start and end apart: 11, of which 7 were waited for; matrix products, arithmetic and copies ran while one was open for 27% of the time, Pallas kernels for 0%

commit v1 on v0

v1 whole, which is shorter than its diff:
```python
import functools, math
import jax, jax.numpy as jnp
from jax import lax
from jax.experimental import pallas as pl
from jax.experimental.pallas import tpu as pltpu
from jax.sharding import PartitionSpec as P

EPSILON = 1e-05
CHUNK = 128
LANES = 128
TAPS = 4
LOG2E = 1.4426950408889634
BF = jnp.bfloat16
F32 = jnp.float32


MESH = pl.DeviceIdType.MESH
PARTS = 4
ROW_PARTS = 6


def _place():
    d, t = lax.axis_index("dp"), lax.axis_index("tensor")
    return d // 2, d % 2, t // 2, t % 2


def _peer(outer, inner, far, near):
    return (outer * 2 + inner, far * 2 + near)


def _greet(outer_n):
    z, y, x, c = _place()
    barrier = pltpu.get_barrier_semaphore()
    peers = []
    for k in range(outer_n):
        for j in (0, 1):
            if k or j:
                peers.append(_peer((z + k) % outer_n, (y + j) % 2, x, c))
    for k in (0, 1):
        for j in (0, 1):
            if k or j:
                peers.append(_peer(z, y, (x + k) % 2, (c + j) % 2))
    for peer in peers:
        pl.semaphore_signal(barrier, inc=1, device_id=peer, device_id_type=MESH)
    pl.semaphore_wait(barrier, len(peers))


def _parts(rows):
    return max(p for p in range(1, ROW_PARTS + 1) if rows % (16 * p) == 0)


def _remote(src, dst, send, recv, peer):
    return pltpu.make_async_remote_copy(
        src_ref=src, dst_ref=dst, send_sem=send, recv_sem=recv, device_id=peer, device_id_type=MESH)


def _rows(start, size):
    return pl.ds(pl.multiple_of(start, 16), size)


class _Reduction:
    def __init__(self, outer_n, partial, grads, block_sum, owned, own_tokens, near_buf, far_src, far_buf,
                 own_grads, in_buf, out_src, out_buf, near_sem, far_sem, in_sem, out_sem, local_sem):
        self.__dict__.update(locals())
        self.z, self.y, self.x, self.c = _place()
        self.me = _peer(self.z, self.y, self.x, self.c)
        self.own_rows = block_sum.shape[0]
        self.block = owned.shape[0]
        self.wparts = _parts(self.block)
        self.late = -(-self.wparts // 6)
        self.size = self.own_rows // PARTS
        self.bsize = self.block // self.wparts
        order = list(range(1, outer_n))
        order.sort(key=lambda k: -min(k, outer_n - k))
        self.order = order + [0]

    def token_rows(self, far, near, part):
        return _rows((far * 2 + near) * self.own_rows + part * self.size, self.size)

    def grad_rows(self, outer, inner, part):
        return _rows((outer * 2 + inner) * self.block + part * self.bsize, self.bsize)

    def near_copy(self, i, part):
        far = (1 - self.x, self.x)[i]
        at = pl.ds(part * self.size, self.size)
        return _remote(self.partial.at[self.token_rows(far, 1 - self.c, part), :], self.near_buf.at[i, at, :],
                       self.near_sem.at[0, i, part], self.near_sem.at[1, i, part],
                       _peer(self.z, self.y, self.x, 1 - self.c))

    def far_copy(self, part):
        at = pl.ds(part * self.size, self.size)
        return _remote(self.far_src.at[at, :], self.far_buf.at[at, :], self.far_sem.at[0, part],
                       self.far_sem.at[1, part], _peer(self.z, self.y, 1 - self.x, self.c))

    def in_copy(self, k, part):
        at = pl.ds(part * self.bsize, self.bsize)
        rows = self.grad_rows((self.z + k) % self.outer_n, 1 - self.y, part)
        return _remote(self.grads.at[rows, :], self.in_buf.at[k, at, :], self.in_sem.at[0, k, part],
                       self.in_sem.at[1, k, part], _peer(self.z, 1 - self.y, self.x, self.c))

    def out_copy(self, k, part):
        at = pl.ds(part * self.bsize, self.bsize)
        return _remote(self.out_src.at[k - 1, at, :], self.out_buf.at[k - 1, at, :], self.out_sem.at[0, k - 1, part],
                       self.out_sem.at[1, k - 1, part], _peer((self.z + k) % self.outer_n, self.y, self.x, self.c))

    def local_copies(self):
        copies = []
        for i, far in enumerate((1 - self.x, self.x)):
            rows = _rows((far * 2 + self.c) * self.own_rows, self.own_rows)
            copies.append(pltpu.make_async_copy(self.partial.at[rows, :], self.own_tokens.at[i], self.local_sem.at[i]))
        for k in range(self.outer_n):
            rows = _rows((((self.z + k) % self.outer_n) * 2 + self.y) * self.block, self.block)
            copies.append(pltpu.make_async_copy(self.grads.at[rows, :], self.own_grads.at[k], self.local_sem.at[2 + k]))
        return copies

    def begin(self):
        _greet(self.outer_n)
        for part in range(PARTS):
            self.near_copy(0, part).start()
        for part in range(self.wparts):
            for k in self.order:
                self.in_copy(k, part).start()
        for part in range(PARTS):
            self.near_copy(1, part).start()
        for copy in self.local_copies():
            copy.start()

    def ready(self):
        for copy in self.local_copies():
            copy.wait()

    def token_step(self, part):
        at = pl.ds(part * self.size, self.size)
        self.near_copy(0, part).wait_recv()
        self.far_src[at, :] = (self.own_tokens[0, at, :].astype(F32) + self.near_buf[0, at, :].astype(F32)).astype(BF)
        self.far_copy(part).start()

    def grad_step(self, part):
        at = pl.ds(part * self.bsize, self.bsize)
        for k in self.order:
            self.in_copy(k, part).wait_recv()
            both = self.own_grads[k, at, :].astype(F32) + self.in_buf[k, at, :].astype(F32)
            if k:
                self.out_src[k - 1, at, :] = both.astype(BF)
                self.out_copy(k, part).start()
            else:
                self.owned[at, :] = both

    def plan(self, steps):
        pieces = [(1, self.ready)]
        for part in range(PARTS):
            pieces.append((min(1 + part, steps - 1), functools.partial(self.token_step, part)))
        for part in range(self.wparts - self.late):
            pieces.append((min(2 + part * (steps - 2) // self.wparts, steps - 1),
                           functools.partial(self.grad_step, part)))
        return pieces

    def end(self):
        for part in range(self.wparts - self.late, self.wparts):
            self.grad_step(part)
        for part in range(PARTS):
            at = pl.ds(part * self.size, self.size)
            self.near_copy(1, part).wait_recv()
            self.far_copy(part).wait_recv()
            self.block_sum[at, :] = (self.own_tokens[1, at, :].astype(F32) + self.near_buf[1, at, :].astype(F32)
                                     + self.far_buf[at, :].astype(F32))
        for part in range(self.wparts):
            at = pl.ds(part * self.bsize, self.bsize)
            total = self.owned[at, :]
            for k in self.order[:-1]:
                self.out_copy(k, part).wait_recv()
                total = total + self.out_buf[k - 1, at, :].astype(F32)
            self.owned[at, :] = total
        for part in range(PARTS):
            self.near_copy(0, part).wait_send()
            self.near_copy(1, part).wait_send()
            self.far_copy(part).wait_send()
        for part in range(self.wparts):
            for k in self.order:
                self.in_copy(k, part).wait_send()
                if k:
                    self.out_copy(k, part).wait_send()


def reduction_scratch(outer_n, tokens, grads):
    dma = pltpu.SemaphoreType.DMA
    parts = _parts(grads[0])
    return [pltpu.VMEM((2,) + tokens, BF), pltpu.VMEM((2,) + tokens, BF), pltpu.VMEM(tokens, BF),
            pltpu.VMEM(tokens, BF), pltpu.VMEM((outer_n,) + grads, BF), pltpu.VMEM((outer_n,) + grads, BF),
            pltpu.VMEM((outer_n - 1,) + grads, BF), pltpu.VMEM((outer_n - 1,) + grads, BF),
            dma((2, 2, PARTS)), dma((2, PARTS)), dma((2, outer_n, parts)), dma((2, outer_n - 1, parts)),
            dma((2 + outer_n,))]


def _sigmoid(v):
    return 1.0 / (1.0 + jnp.exp(-v))


def _softplus(t):
    return jnp.maximum(t, 0.0) + jnp.log1p(jnp.exp(-jnp.abs(t)))


def _dot_last(a, b):
    return lax.dot_general(a, b, (((1,), (1,)), ((), ())), preferred_element_type=F32)


def _dot_exact(a, b):
    return jnp.dot(a, b, precision=lax.Precision.HIGHEST, preferred_element_type=F32)


def _halves(v):
    high = v.astype(BF)
    return high, (v - high.astype(F32)).astype(BF)


def _dot_three(a, b):
    a_high, a_low = _halves(a)
    b_high, b_low = _halves(b)
    return _dot_last(jnp.concatenate([a_high, a_low, a_high], axis=1),
                     jnp.concatenate([b_high, b_high, b_low], axis=1))


def _rows_sum(v):
    return v.reshape(v.shape[0] // 8, 8, v.shape[1]).sum(axis=0)


def _split(lo, v):
    zero = jnp.zeros_like(v)
    return [jnp.where(lo, v, zero), jnp.where(lo, zero, v)]


def _times(dt_raw, head, rows, cols):
    t = dt_raw + head[0:1, :]
    delta = _softplus(t)
    rate = -jnp.exp(head[1:2, :])
    tri = (rows >= cols).astype(F32)
    cum = _dot_exact(tri, delta * (rate * LOG2E))
    return t, delta, rate, cum


def _pair_cols(lo, v, q):
    return jnp.where(lo, v[:, 2 * q : 2 * q + 1], v[:, 2 * q + 1 : 2 * q + 2])


def _conv(buf, start, cols, w, length):
    shifted = [buf[start + k : start + k + length, cols] for k in range(TAPS)]
    v = w[TAPS : TAPS + 1, :] + w[0:1, :] * shifted[0]
    for k in range(1, TAPS):
        v = v + w[k : k + 1, :] * shifted[k]
    return v, shifted


def forward_kernel(width, p_ref, dg_ref, convx_ref, convbc_ref, head_ref, lane_ref,
                   y_ref, h_ref, s_ref, state, xbuf, bcbuf, sums, sum_sem):
    tokens = p_ref.shape[0]
    pairs = width // LANES
    step = pl.program_id(0)
    z, y_at, x, c = _place()
    me = x * 2 + c
    half = sums.shape[1] // 2
    tensor_peers = [_peer(z, y_at, (x + k) % 2, (c + j) % 2) for k in (0, 1) for j in (0, 1) if k or j]

    @pl.when(step == 0)
    def _():
        barrier = pltpu.get_barrier_semaphore()
        for peer in tensor_peers:
            pl.semaphore_signal(barrier, inc=1, device_id=peer, device_id_type=MESH)
        pl.semaphore_wait(barrier, len(tensor_peers))
        state[...] = jnp.zeros_like(state)
        xbuf[0:8, :] = jnp.zeros((8, width), F32)
        bcbuf[0:8, :] = jnp.zeros((8, 2 * LANES), F32)

    @pl.when(step > 0)
    def _():
        xbuf[0:8, :] = xbuf[tokens : tokens + 8, :]
        bcbuf[0:8, :] = bcbuf[tokens : tokens + 8, :]

    xbuf[8 : 8 + tokens, :] = p_ref[:, width : 2 * width]
    bcbuf[8 : 8 + tokens, :] = p_ref[:, 2 * width : 2 * width + 2 * LANES]
    rows = lax.broadcasted_iota(jnp.int32, (CHUNK, CHUNK), 0)
    cols = lax.broadcasted_iota(jnp.int32, (CHUNK, CHUNK), 1)
    lo = cols < LANES // 2
    head = head_ref[...]
    ones = jnp.ones((8, LANES), F32)
    for sub in range(tokens // CHUNK):
        base = sub * CHUNK
        span = slice(base, base + CHUNK)
        vbc, _ = _conv(bcbuf, base + 5, slice(0, 2 * LANES), convbc_ref[...], CHUNK)
        bc = vbc * _sigmoid(vbc)
        b_in, c_out = bc[:, :LANES], bc[:, LANES:]
        c_high, c_low = _halves(c_out)
        c_wide = jnp.concatenate([c_high, c_low, c_high], axis=1)
        _, delta, _, cum = _times(p_ref[span, 2 * width + 2 * LANES :], head, rows, cols)
        cum_t = cum.T
        scores = jnp.where(rows >= cols, _dot_three(c_out, b_in), 0.0)
        last = cum[CHUNK - 1 : CHUNK, :]
        tail = jnp.exp2(last - cum)
        grow = jnp.exp2(cum)
        decay = jnp.exp2(last)
        b_t = b_in.T.astype(BF)
        squares = jnp.zeros((CHUNK, LANES), F32)
        inner = jnp.zeros((CHUNK, LANES), F32)
        h_ref[sub] = state[...]
        for q in range(pairs):
            lanes = slice(q * LANES, (q + 1) * LANES)
            v, _ = _conv(xbuf, base + 5, lanes, convx_ref[:, lanes], CHUNK)
            x_act = v * _sigmoid(v)
            u = x_act * _pair_cols(lo, delta, q)
            left = []
            for h in (2 * q, 2 * q + 1):
                e = jnp.exp2(jnp.minimum(cum[:, h : h + 1] - cum_t[h : h + 1, :], 0.0))
                left.append((e * scores).astype(BF))
            held = state[:, lanes]
            held_high, held_low = _halves(held)
            y = jnp.dot(jnp.concatenate(left, axis=1), jnp.concatenate(_split(lo, u.astype(BF)), axis=0),
                        preferred_element_type=F32)
            outer = jnp.dot(c_wide, jnp.concatenate([held_high, held_high, held_low], axis=0),
                            preferred_element_type=F32)
            y = y + outer * _pair_cols(lo, grow, q) + lane_ref[0:1, lanes] * x_act
            y_ref[span, lanes] = y
            uw = (u * _pair_cols(lo, tail, q)).astype(BF)
            factor = _pair_cols(lo[0:1, :], decay, q)
            state[:, lanes] = held * factor + jnp.dot(b_t, uw, preferred_element_type=F32)
            z = p_ref[span, lanes]
            product = y * (z * _sigmoid(z))
            squares = squares + product * product
            inner = inner + dg_ref[span, lanes].astype(F32) * lane_ref[1:2, lanes] * product
        row_sq = lax.dot_general(ones, squares, (((1,), (1,)), ((), ())),
                                 precision=lax.Precision.HIGHEST, preferred_element_type=F32)
        row_in = lax.dot_general(ones, inner, (((1,), (1,)), ((), ())),
                                 precision=lax.Precision.HIGHEST, preferred_element_type=F32)
        at = step * (tokens // CHUNK) + sub
        sums[me, pl.ds(at, 1), :] = row_sq[0:1, :]
        sums[me, pl.ds(half + at, 1), :] = row_in[0:1, :]

    @pl.when(step == pl.num_programs(0) - 1)
    def _():
        copies = [_remote(sums.at[me], sums.at[me], sum_sem.at[0, i], sum_sem.at[1, i], peer)
                  for i, peer in enumerate(tensor_peers)]
        for copy in copies:
            copy.start()
        for copy in copies:
            copy.wait_recv()
        s_ref[...] = (sums[0] + sums[1]) + (sums[2] + sums[3])
        for copy in copies:
            copy.wait_send()


def backward_kernel(width, outer_n, p_ref, prev_ref, y_ref, dy_ref, h_ref,
                    convx_ref, convbc_ref, head_ref, lane_ref, partial, grads,
                    dp_ref, gx_ref, gbc_ref, gh_ref, block_sum, owned,
                    grad_state, carry_hg, xbuf, bcbuf, dvx, dvbc, *comm):
    tokens = p_ref.shape[0]
    pairs = width // LANES
    step = pl.program_id(0)
    is_first_block = step == pl.num_programs(0) - 1
    length = partial.shape[0]
    reduction = _Reduction(outer_n, partial, grads, block_sum, owned, *comm)

    @pl.when(step == 0)
    def _():
        reduction.begin()

    for at, piece in reduction.plan(length // tokens):
        @pl.when(step == at)
        def _(piece=piece):
            piece()

    @pl.when(step == 0)
    def _():
        grad_state[...] = jnp.zeros_like(grad_state)
        carry_hg[...] = jnp.zeros_like(carry_hg)
        dvx[0:8, :] = jnp.zeros((8, width), F32)
        dvbc[0:8, :] = jnp.zeros((8, 2 * LANES), F32)
        gx_ref[...] = jnp.zeros_like(gx_ref)
        gbc_ref[...] = jnp.zeros_like(gbc_ref)
        gh_ref[...] = jnp.zeros_like(gh_ref)

    keep = jnp.where(is_first_block, 0.0, 1.0)
    xbuf[0:8, :] = prev_ref[:, width : 2 * width] * keep
    bcbuf[0:8, :] = prev_ref[:, 2 * width : 2 * width + 2 * LANES] * keep
    xbuf[8 : 8 + tokens, :] = p_ref[:, width : 2 * width]
    bcbuf[8 : 8 + tokens, :] = p_ref[:, 2 * width : 2 * width + 2 * LANES]
    rows = lax.broadcasted_iota(jnp.int32, (CHUNK, CHUNK), 0)
    cols = lax.broadcasted_iota(jnp.int32, (CHUNK, CHUNK), 1)
    lo = cols < LANES // 2
    head = head_ref[...]
    for sub in reversed(range(tokens // CHUNK)):
        base = sub * CHUNK
        span = slice(base, base + CHUNK)
        vbc, shifted_bc = _conv(bcbuf, base + 5, slice(0, 2 * LANES), convbc_ref[...], CHUNK)
        sbc = _sigmoid(vbc)
        bc = vbc * sbc
        b_in, c_out = bc[:, :LANES], bc[:, LANES:]
        b_half, c_half = b_in.astype(BF), c_out.astype(BF)
        t, delta, rate, cum = _times(p_ref[span, 2 * width + 2 * LANES :], head, rows, cols)
        cum_t = cum.T
        causal_t = cols >= rows
        scores_t = jnp.where(causal_t, _dot_three(b_in, c_out), 0.0)
        last = cum[CHUNK - 1 : CHUNK, :]
        tail = jnp.exp2(last - cum)
        grow = jnp.exp2(cum)
        decay = jnp.exp2(last)
        c_t = c_out.T.astype(BF)
        d_scores = jnp.zeros((CHUNK, CHUNK), F32)
        d_b = jnp.zeros((CHUNK, LANES), F32)
        d_c = jnp.zeros((CHUNK, LANES), F32)
        per_head = jnp.zeros((CHUNK, LANES), F32)
        hg_heads = jnp.zeros((8, LANES), F32)
        dvx[CHUNK : CHUNK + 8, :] = dvx[0:8, :]
        dvbc[CHUNK : CHUNK + 8, :] = dvbc[0:8, :]
        for q in range(pairs):
            lanes = slice(q * LANES, (q + 1) * LANES)
            wide = _pair_cols(lo, delta, q)
            skip = lane_ref[0:1, lanes]
            v, shifted = _conv(xbuf, base + 5, lanes, convx_ref[:, lanes], CHUNK)
            sv = _sigmoid(v)
            x_act = v * sv
            u = x_act * wide
            u_half = u.astype(BF)
            y = y_ref[span, lanes]
            dy_half = dy_ref[span, lanes]
            dy = dy_half.astype(F32)
            dy_block = jnp.concatenate(_split(lo, dy_half), axis=0)
            d_m = _dot_last(u_half, dy_block)
            left, left_b = [], []
            for a in (0, 1):
                h = 2 * q + a
                e = jnp.exp2(jnp.minimum(cum_t[h : h + 1, :] - cum[:, h : h + 1], 0.0))
                left.append((e * scores_t).astype(BF))
                d_scores = d_scores + e * d_m[:, a * CHUNK : (a + 1) * CHUNK]
                left_b.append((b_in * tail[:, h : h + 1]).astype(BF))
            g_held = grad_state[:, lanes]
            g_half, g_low = _halves(g_held)
            h_held = h_ref[sub, :, lanes]
            h_half, h_low = _halves(h_held)
            right = jnp.concatenate([dy_block] + _split(lo, g_half), axis=0)
            du = jnp.dot(jnp.concatenate(left + left_b, axis=1), right, preferred_element_type=F32)
            dx = du * wide + skip * dy
            dv = dx * (sv * (1.0 + v * (1.0 - sv)))
            dvx[0:CHUNK, lanes] = dv
            w = convx_ref[:, lanes]
            d_in = w[TAPS - 1 : TAPS, :] * dv
            for k in range(TAPS - 1):
                ahead = TAPS - 1 - k
                d_in = d_in + w[k : k + 1, :] * dvx[ahead : ahead + CHUNK, lanes]
            dp_ref[span, lanes] = d_in.astype(BF)
            for k in range(TAPS):
                gx_ref[k, :, lanes] += _rows_sum(dv * shifted[k])
            gx_ref[4, :, lanes] += _rows_sum(dv)
            gx_ref[5, :, lanes] += _rows_sum(dy * x_act)
            edy = (dy * _pair_cols(lo, grow, q)).astype(BF)
            uw = (u * _pair_cols(lo, tail, q)).astype(BF)
            d_c = d_c + _dot_last(jnp.concatenate([edy, edy], axis=1), jnp.concatenate([h_half, h_low], axis=1))
            d_b = d_b + _dot_last(jnp.concatenate([uw, uw], axis=1), jnp.concatenate([g_half, g_low], axis=1))
            g_new = g_held * _pair_cols(lo[0:1, :], decay, q) + jnp.dot(
                c_t, edy, preferred_element_type=F32)
            grad_state[:, lanes] = g_new
            r1 = x_act * du
            r2 = dy * (y - skip * x_act)
            sel1 = (cols == 2 * q + (rows >= LANES // 2).astype(jnp.int32)).astype(BF)
            sel2 = (cols == LANES // 2 + 2 * q + (rows >= LANES // 2).astype(jnp.int32)).astype(BF)
            r1h = r1.astype(BF)
            r1l = (r1 - r1h.astype(F32)).astype(BF)
            r2h = r2.astype(BF)
            r2l = (r2 - r2h.astype(F32)).astype(BF)
            per_head = per_head + jnp.dot(
                jnp.concatenate([r1h, r1l, r2h, r2l], axis=1),
                jnp.concatenate([sel1, sel1, sel2, sel2], axis=0), preferred_element_type=F32)
            hg_heads = hg_heads + _dot_exact(carry_hg[:, lanes], sel1.astype(F32))
            carry_hg[:, lanes] = _rows_sum(g_new * h_held)
        d_scores = jnp.where(causal_t, d_scores, 0.0)
        ds_half = d_scores.astype(BF)
        d_b = d_b + jnp.dot(ds_half, c_half, preferred_element_type=F32)
        d_c = d_c + jnp.dot(d_scores.T.astype(BF), b_half, preferred_element_type=F32)
        dvb = jnp.concatenate([d_b, d_c], axis=1) * (sbc * (1.0 + vbc * (1.0 - sbc)))
        dvbc[0:CHUNK, :] = dvb
        wbc = convbc_ref[...]
        d_bc = wbc[TAPS - 1 : TAPS, :] * dvb
        for k in range(TAPS - 1):
            ahead = TAPS - 1 - k
            d_bc = d_bc + wbc[k : k + 1, :] * dvbc[ahead : ahead + CHUNK, :]
        dp_ref[span, width : width + 2 * LANES] = d_bc.astype(BF)
        for k in range(TAPS):
            gbc_ref[k] += _rows_sum(dvb * shifted_bc[k])
        gbc_ref[4] += _rows_sum(dvb)
        direct = per_head
        through = pltpu.roll(per_head, LANES // 2, 1)
        d_cum = through - delta * direct
        suffix = _dot_exact((cols >= rows).astype(F32), d_cum)
        d_log = suffix + jnp.sum(hg_heads, axis=0, keepdims=True)
        valid = cols < 2 * pairs
        d_delta = direct + rate * d_log
        d_dt = jnp.where(valid, d_delta * _sigmoid(t), 0.0)
        dp_ref[span, width + 2 * LANES :] = d_dt.astype(BF)
        gh_ref[0] += _rows_sum(d_dt)
        gh_ref[1] += _rows_sum(jnp.where(valid, delta * d_log, 0.0)) * rate

    @pl.when(is_first_block)
    def _():
        reduction.end()


def ssd_forward(proj, dg, convx, convbc, head, lane, tokens=256):
    length, total = proj.shape
    width = convx.shape[1]
    subs = tokens // CHUNK
    whole = lambda a: pl.BlockSpec(a.shape, lambda i: (0,) * a.ndim)
    return pl.pallas_call(
        functools.partial(forward_kernel, width),
        grid=(length // tokens,),
        in_specs=[pl.BlockSpec((tokens, total), lambda i: (i, 0)),
                  pl.BlockSpec((tokens, width), lambda i: (i, 0)),
                  whole(convx), whole(convbc), whole(head), whole(lane)],
        out_specs=[pl.BlockSpec((tokens, width), lambda i: (i, 0)),
                   pl.BlockSpec((subs, LANES, width), lambda i: (i, 0, 0)),
                   pl.BlockSpec((2 * length // CHUNK, CHUNK), lambda i: (0, 0))],
        out_shape=[jax.ShapeDtypeStruct((length, width), F32),
                   jax.ShapeDtypeStruct((length // CHUNK, LANES, width), F32),
                   jax.ShapeDtypeStruct((2 * length // CHUNK, CHUNK), F32)],
        scratch_shapes=[pltpu.VMEM((LANES, width), F32),
                        pltpu.VMEM((tokens + 8, width), F32),
                        pltpu.VMEM((tokens + 8, 2 * LANES), F32),
                        pltpu.VMEM((4, 2 * length // CHUNK, CHUNK), F32),
                        pltpu.SemaphoreType.DMA((2, 3))],
        compiler_params=pltpu.CompilerParams(collective_id=2, has_side_effects=True),
        cost_estimate=pl.CostEstimate(flops=4 * 10**9, bytes_accessed=30 * 2**20, transcendentals=10**7),
        name="scan_forward",
    )(proj, dg, convx, convbc, head, lane)


def ssd_backward(proj, y, dy, states, convx, convbc, head, lane, partial, grads, tokens=256):
    length, total = proj.shape
    width = convx.shape[1]
    subs = tokens // CHUNK
    n = length // tokens
    dp, tp = lax.axis_size("dp"), lax.axis_size("tensor")
    whole = lambda a: pl.BlockSpec(a.shape, lambda i: (0,) * a.ndim)
    rev = lambda i: (n - 1 - i, 0)
    own = lambda shape: pl.BlockSpec(shape, lambda i: (0, 0))
    hbm = pl.BlockSpec(memory_space=pl.ANY)
    block_shape = (length // tp, partial.shape[1])
    owned_shape = (grads.shape[0] // dp, grads.shape[1])
    return pl.pallas_call(
        functools.partial(backward_kernel, width, dp // 2),
        grid=(n,),
        in_specs=[pl.BlockSpec((tokens, total), rev),
                  pl.BlockSpec((8, total), lambda i: (jnp.maximum((n - 1 - i) * (tokens // 8) - 1, 0), 0)),
                  pl.BlockSpec((tokens, width), rev),
                  pl.BlockSpec((tokens, width), rev),
                  pl.BlockSpec((subs, LANES, width), lambda i: (n - 1 - i, 0, 0)),
                  whole(convx), whole(convbc), whole(head), whole(lane), hbm, hbm],
        out_specs=[pl.BlockSpec((tokens, total - width), rev),
                   pl.BlockSpec((6, 8, width), lambda i: (0, 0, 0)),
                   pl.BlockSpec((5, 8, 2 * LANES), lambda i: (0, 0, 0)),
                   pl.BlockSpec((2, 8, LANES), lambda i: (0, 0, 0)),
                   own(block_shape), own(owned_shape)],
        out_shape=[jax.ShapeDtypeStruct((length, total - width), BF),
                   jax.ShapeDtypeStruct((6, 8, width), F32),
                   jax.ShapeDtypeStruct((5, 8, 2 * LANES), F32),
                   jax.ShapeDtypeStruct((2, 8, LANES), F32),
                   jax.ShapeDtypeStruct(block_shape, F32),
                   jax.ShapeDtypeStruct(owned_shape, F32)],
        scratch_shapes=[pltpu.VMEM((LANES, width), F32),
                        pltpu.VMEM((8, width), F32),
                        pltpu.VMEM((tokens + 8, width), F32),
                        pltpu.VMEM((tokens + 8, 2 * LANES), F32),
                        pltpu.VMEM((CHUNK + 8, width), F32),
                        pltpu.VMEM((CHUNK + 8, 2 * LANES), F32)] + reduction_scratch(dp // 2, block_shape, owned_shape),
        compiler_params=pltpu.CompilerParams(collective_id=3, has_side_effects=True, vmem_limit_bytes=62 * 2**20),
        cost_estimate=pl.CostEstimate(flops=12 * 10**9, bytes_accessed=50 * 2**20, transcendentals=10**7),
        name="scan_backward",
    )(proj, proj, y, dy, states, convx, convbc, head, lane, partial, grads)


def middle_kernel(width, inner_channels, z_ref, y_ref, dg_ref, s_ref, lane_ref, normed, cot, out_t,
                  dy_ref, dz_ref, out_ref, grads_ref, gg_ref, gated, acc_z, acc_o):
    tokens = z_ref.shape[0]
    step = pl.program_id(0)
    half = s_ref.shape[0] // 2

    @pl.when(step == 0)
    def _():
        gg_ref[...] = jnp.zeros_like(gg_ref)
        acc_z[...] = jnp.zeros_like(acc_z)
        acc_o[...] = jnp.zeros_like(acc_o)

    for sub in range(tokens // CHUNK):
        span = slice(sub * CHUNK, (sub + 1) * CHUNK)
        at = step * (tokens // CHUNK) + sub
        wide = lambda row: jnp.broadcast_to(row, (8, CHUNK)).T[:, 0:1]
        squares, dots = wide(s_ref[pl.ds(at, 1), :]), wide(s_ref[pl.ds(half + at, 1), :])
        inv = lax.rsqrt(squares / inner_channels + EPSILON)
        mean = inv * dots / inner_channels
        for q in range(width // LANES):
            lanes = slice(q * LANES, (q + 1) * LANES)
            gain = lane_ref[1:2, lanes]
            y, z, dg = y_ref[span, lanes], z_ref[span, lanes], dg_ref[span, lanes]
            sz = _sigmoid(z)
            act = z * sz
            quot = y * act * inv
            gg_ref[:, lanes] += _rows_sum(dg * quot)
            gated[span, lanes] = (quot * gain).astype(BF)
            d_prod = inv * (dg * gain - quot * mean)
            dy_ref[span, lanes] = (d_prod * act).astype(BF)
            dz_ref[span, lanes] = (d_prod * y * sz * (1.0 + z * (1.0 - sz))).astype(BF)
    out_ref[...] = _dot_last(gated[...], out_t[...]).astype(BF)
    first = lambda a, b: lax.dot_general(a, b, (((0,), (0,)), ((), ())), preferred_element_type=F32)
    acc_z[...] += first(normed[...], dz_ref[...])
    acc_o[...] += first(cot[...], gated[...])

    @pl.when(step == pl.num_programs(0) - 1)
    def _():
        grads_ref[:, :width] = acc_z[...].astype(BF)
        grads_ref[:, width:] = acc_o[...].astype(BF)


def middle(proj, y, dg, sums, lane, normed, cot, out_t, inner_channels, tokens=512):
    length, model = normed.shape
    width = y.shape[1]
    at = lambda cols: pl.BlockSpec((tokens, cols), lambda i: (i, 0))
    once = lambda shape: pl.BlockSpec(shape, lambda i: (0, 0), pipeline_mode=pl.Buffered(1))
    return pl.pallas_call(
        functools.partial(middle_kernel, width, inner_channels),
        grid=(length // tokens,),
        in_specs=[at(width), at(width), at(width), once(sums.shape), once(lane.shape), at(model), at(model),
                  once(out_t.shape)],
        out_specs=[at(width), at(width), at(model), once((model, 2 * width)), once((8, width))],
        out_shape=[jax.ShapeDtypeStruct((length, width), BF),
                   jax.ShapeDtypeStruct((length, width), BF),
                   jax.ShapeDtypeStruct((length, model), BF),
                   jax.ShapeDtypeStruct((model, 2 * width), BF),
                   jax.ShapeDtypeStruct((8, width), F32)],
        scratch_shapes=[pltpu.VMEM((tokens, width), BF),
                        pltpu.VMEM((model, width), F32),
                        pltpu.VMEM((model, width), F32)],
        cost_estimate=pl.CostEstimate(flops=15 * 10**9, bytes_accessed=50 * 2**20, transcendentals=10**6),
        name="middle",
    )(proj, y, dg, sums, lane, normed, cot, out_t)


def pad_rows(a, rows):
    return jnp.pad(a, ((0, rows - a.shape[0]), (0, 0)))


def pack_params(conv_x_weight, conv_x_bias, conv_bc_weight, conv_bc_bias, dt_bias, a_log, skip_gain, gate_gain):
    width = conv_x_weight.shape[1]
    convx = pad_rows(jnp.concatenate([conv_x_weight, conv_x_bias[None]], 0), 8)
    convbc = pad_rows(jnp.concatenate([conv_bc_weight, conv_bc_bias[None]], 0), 8)
    heads = dt_bias.shape[0]
    head = jnp.pad(jnp.stack([dt_bias, a_log]), ((0, 6), (0, LANES - heads)))
    lane = pad_rows(jnp.stack([jnp.repeat(skip_gain, width // heads), gate_gain]), 8)
    return convx, convbc, head, lane
def gather_kernel(outer_n, small, resid, cot, wzx, wdt, wbc, wout,
                  small_all, normed_all, cot_all, weight, weight_out,
                  small_t, small_d, normed_own, cot_own, bc_slots, bc_rows,
                  small_sem_t, small_sem_d, bc_sem, norm_sem, cot_sem, zx_sem, bd_sem, wo_sem, local_sem):
    z, y, x, c = _place()
    t = x * 2 + c
    d = z * 2 + y
    block = wzx.shape[0]
    zx_cols = wzx.shape[1]
    bc_cols = wbc.shape[1]
    wparts = _parts(block)
    own_rows = resid.shape[0]
    model = resid.shape[1]
    cot_own[...] = cot[...].astype(BF)
    _greet(outer_n)
    started = []

    def go(copy):
        copy.start()
        started.append(copy)
        return copy

    dp_peers = [(k, j) for k in range(outer_n) for j in (0, 1) if k or j]
    tensor_peers = [(k, j) for k in (0, 1) for j in (0, 1) if k or j]
    small_first, bc_first = [], []
    for i, (k, j) in enumerate(dp_peers):
        peer = _peer((z + k) % outer_n, (y + j) % 2, x, c)
        small_first.append(go(_remote(small, small_d.at[i], small_sem_d.at[0, i], small_sem_d.at[1, i], peer)))
    for i, (k, j) in enumerate(tensor_peers):
        peer = _peer(z, y, (x + k) % 2, (c + j) % 2)
        bc_first.append(go(_remote(wbc, bc_slots.at[t], bc_sem.at[0, i], bc_sem.at[1, i], peer)))
    bc_slots[t] = wbc[...]

    order = [k for k in range(1, outer_n)]
    order.sort(key=lambda k: -min(k, outer_n - k))

    def block_rows(outer, inner, part):
        size = block // wparts
        return _rows((outer * 2 + inner) * block + part * size, size)

    def send_out(src, dst, cols, sem, part):
        size = block // wparts
        rows = block_rows(z, y, part)
        piece = src.at[part * size : (part + 1) * size, :]
        for k in order:
            go(_remote(piece, dst.at[rows, cols], sem.at[0, k, part], sem.at[1, k, part],
                       _peer((z + k) % outer_n, y, x, c)))
        go(_remote(piece, dst.at[rows, cols], sem.at[2, 0, part], sem.at[3, 0, part],
                   _peer(z, 1 - y, x, c)))

    def pass_on(dst, cols, sem, part):
        for k in order:
            rows = block_rows((z - k) % outer_n, y, part)
            view = dst.at[rows, cols]
            _remote(view, view, sem.at[0, k, part], sem.at[1, k, part], _peer(z, y, x, c)).wait_recv()
            go(_remote(view, view, sem.at[2, k, part], sem.at[3, k, part], _peer(z, 1 - y, x, c)))

    def finish(dst, cols, sem, part):
        for k in range(outer_n):
            view = dst.at[block_rows((z - k) % outer_n, 1 - y, part), cols]
            _remote(view, view, sem.at[2, k, part], sem.at[3, k, part], _peer(z, y, x, c)).wait_recv()

    zx_at = slice(0, zx_cols)
    bc_at = slice(zx_cols, zx_cols + bc_cols)
    dt_at = slice(zx_cols + bc_cols, weight.shape[1])
    all_cols = slice(0, wout.shape[1])
    for part in range(wparts):
        send_out(wzx, weight, zx_at, zx_sem, part)

    for copy in small_first:
        copy.wait_recv()
    total = small[...]
    for i in range(len(dp_peers)):
        total = total + small_d[i]
    small_t[3] = total
    second = []
    for i, (k, j) in enumerate(tensor_peers):
        peer = _peer(z, y, (x + k) % 2, (c + j) % 2)
        second.append(go(_remote(small_t.at[3], small_t.at[i], small_sem_t.at[0, i], small_sem_t.at[1, i], peer)))

    values = resid[...]
    inv = lax.rsqrt(jnp.mean(values * values, axis=-1, keepdims=True) + EPSILON)
    for copy in second:
        copy.wait_recv()
    total = small_t[3]
    for i in range(len(second)):
        total = total + small_t[i]
    small_all[...] = total
    for j in range(model // LANES):
        lanes = slice(j * LANES, (j + 1) * LANES)
        normed_own[:, lanes] = (resid[:, lanes] * inv * total[j : j + 1, :]).astype(BF)

    def token_rows(far, near, part):
        size = own_rows // PARTS
        return _rows((far * 2 + near) * own_rows + part * size, size)

    def send_tokens(src, dst, sem, part):
        size = own_rows // PARTS
        piece = src.at[part * size : (part + 1) * size, :]
        view = dst.at[token_rows(x, c, part), :]
        go(_remote(piece, view, sem.at[0, 0, part], sem.at[1, 0, part], _peer(z, y, 1 - x, c)))
        go(_remote(piece, view, sem.at[0, 1, part], sem.at[1, 1, part], _peer(z, y, x, 1 - c)))

    def pass_tokens(dst, sem, part):
        view = dst.at[token_rows(1 - x, c, part), :]
        _remote(view, view, sem.at[0, 0, part], sem.at[1, 0, part], _peer(z, y, x, c)).wait_recv()
        go(_remote(view, view, sem.at[0, 2, part], sem.at[1, 2, part], _peer(z, y, x, 1 - c)))

    def finish_tokens(dst, sem, part):
        for i, far in ((1, x), (2, 1 - x)):
            view = dst.at[token_rows(far, 1 - c, part), :]
            _remote(view, view, sem.at[0, i, part], sem.at[1, i, part], _peer(z, y, x, c)).wait_recv()

    for part in range(PARTS):
        send_tokens(normed_own, normed_all, norm_sem, part)
    for part in range(PARTS):
        send_tokens(cot_own, cot_all, cot_sem, part)
    for copy in bc_first:
        copy.wait_recv()
    for i in range(4):
        bc_rows[i * wbc.shape[0] : (i + 1) * wbc.shape[0], :] = bc_slots[i]
    for part in range(wparts):
        send_out(bc_rows, weight, bc_at, bd_sem.at[0], part)
        send_out(wdt, weight, dt_at, bd_sem.at[1], part)
        send_out(wout, weight_out, all_cols, wo_sem, part)
    mine = _rows(d * block, block)
    tokens = _rows(t * own_rows, own_rows)
    local = [
        pltpu.make_async_copy(wzx, weight.at[mine, zx_at], local_sem.at[0]),
        pltpu.make_async_copy(bc_rows, weight.at[mine, bc_at], local_sem.at[1]),
        pltpu.make_async_copy(wdt, weight.at[mine, dt_at], local_sem.at[2]),
        pltpu.make_async_copy(wout, weight_out.at[mine, :], local_sem.at[3]),
        pltpu.make_async_copy(normed_own, normed_all.at[tokens, :], local_sem.at[4]),
        pltpu.make_async_copy(cot_own, cot_all.at[tokens, :], local_sem.at[5]),
    ]
    for copy in local:
        copy.start()
    for part in range(max(PARTS, wparts)):
        if part < wparts:
            pass_on(weight, zx_at, zx_sem, part)
        if part < PARTS:
            pass_tokens(normed_all, norm_sem, part)
    for part in range(max(PARTS, wparts)):
        if part < wparts:
            pass_on(weight, bc_at, bd_sem.at[0], part)
            pass_on(weight, dt_at, bd_sem.at[1], part)
            pass_on(weight_out, all_cols, wo_sem, part)
        if part < PARTS:
            pass_tokens(cot_all, cot_sem, part)
    for part in range(wparts):
        finish(weight, zx_at, zx_sem, part)
        finish(weight, bc_at, bd_sem.at[0], part)
        finish(weight, dt_at, bd_sem.at[1], part)
        finish(weight_out, all_cols, wo_sem, part)
    for part in range(PARTS):
        finish_tokens(normed_all, norm_sem, part)
        finish_tokens(cot_all, cot_sem, part)
    for copy in started:
        copy.wait_send()
    for copy in local:
        copy.wait()


def gather_all(small, resid, cot, wzx, wdt, wbc, wout):
    dp, tp = lax.axis_size("dp"), lax.axis_size("tensor")
    outer_n = dp // 2
    block, zx_cols = wzx.shape
    total = zx_cols + wbc.shape[1] + wdt.shape[1]
    vm = pl.BlockSpec(memory_space=pltpu.VMEM)
    hbm = pl.BlockSpec(memory_space=pl.ANY)
    dma = pltpu.SemaphoreType.DMA
    return pl.pallas_call(
        functools.partial(gather_kernel, outer_n),
        in_specs=[vm] * 7,
        out_specs=[vm, hbm, hbm, hbm, hbm],
        out_shape=[jax.ShapeDtypeStruct(small.shape, F32),
                   jax.ShapeDtypeStruct((resid.shape[0] * tp, resid.shape[1]), BF),
                   jax.ShapeDtypeStruct((resid.shape[0] * tp, resid.shape[1]), BF),
                   jax.ShapeDtypeStruct((block * dp, total), BF),
                   jax.ShapeDtypeStruct((block * dp, wout.shape[1]), BF)],
        scratch_shapes=[pltpu.VMEM((4,) + small.shape, F32),
                        pltpu.VMEM((dp - 1,) + small.shape, F32),
                        pltpu.VMEM(resid.shape, BF),
                        pltpu.VMEM(resid.shape, BF),
                        pltpu.VMEM((4,) + wbc.shape, BF),
                        pltpu.VMEM((block, wbc.shape[1]), BF),
                        dma((2, 3)), dma((2, dp - 1)), dma((2, 3)), dma((2, 3, PARTS)), dma((2, 3, PARTS)),
                        dma((4, outer_n, _parts(block))), dma((2, 4, outer_n, _parts(block))), dma((4, outer_n, _parts(block))),
                        dma((6,))],
        compiler_params=pltpu.CompilerParams(collective_id=0, has_side_effects=True),
        cost_estimate=pl.CostEstimate(flops=10**7, bytes_accessed=40 * 2**20, transcendentals=0),
        name="gather_all",
    )(small, resid, cot, wzx, wdt, wbc, wout)


def reduce_kernel(outer_n, small_rows_both, partial, grads, small, resid, gain,
                  d_local, owned, small_out,
                  near_buf, far_src, far_buf, in_buf, out_src, out_buf, small_d, small_t, gain_acc,
                  near_sem, far_sem, in_sem, out_sem, small_sem_d, small_sem_t):
    z, y, x, c = _place()
    own_rows = resid.shape[0]
    model = resid.shape[1]
    block = owned.shape[0]
    pairs_n = partial.shape[0] // (4 * own_rows)
    _greet(outer_n)
    started = []

    def go(copy):
        copy.start()
        started.append(copy)
        return copy

    me = _peer(z, y, x, c)
    size = own_rows // PARTS
    wparts = _parts(block)
    bsize = block // wparts

    def token_rows(far, near, part):
        return _rows((far * 2 + near) * own_rows + part * size, size)

    for part in range(PARTS):
        for i, far in ((0, 1 - x), (1, x)):
            at = pl.ds(part * size, size)
            go(_remote(partial.at[token_rows(far, 1 - c, part), :], near_buf.at[i, at, :],
                       near_sem.at[0, i, part], near_sem.at[1, i, part], _peer(z, y, x, 1 - c)))
    order = [k for k in range(1, outer_n)]
    order.sort(key=lambda k: -min(k, outer_n - k))
    order = order + [0]

    def grad_rows(outer, inner, part):
        return _rows((outer * 2 + inner) * block + part * bsize, bsize)

    for part in range(wparts):
        for k in order:
            at = pl.ds(part * bsize, bsize)
            go(_remote(grads.at[grad_rows((z + k) % outer_n, 1 - y, part), :], in_buf.at[k, at, :],
                       in_sem.at[0, k, part], in_sem.at[1, k, part], _peer(z, 1 - y, x, c)))

    def token_step(part):
        at = pl.ds(part * size, size)
        view = near_buf.at[0, at, :]
        _remote(view, view, near_sem.at[0, 0, part], near_sem.at[1, 0, part], me).wait_recv()
        far_src[at, :] = (partial[token_rows(1 - x, c, part), :].astype(F32) + view[...].astype(F32)).astype(BF)
        go(_remote(far_src.at[at, :], far_buf.at[at, :], far_sem.at[0, part], far_sem.at[1, part],
                   _peer(z, y, 1 - x, c)))

    def grad_step(part):
        at = pl.ds(part * bsize, bsize)
        for k in order:
            view = in_buf.at[k, at, :]
            _remote(view, view, in_sem.at[0, k, part], in_sem.at[1, k, part], me).wait_recv()
            both = grads[grad_rows((z + k) % outer_n, y, part), :].astype(F32) + view[...].astype(F32)
            if k:
                out_src[k - 1, at, :] = both.astype(BF)
                go(_remote(out_src.at[k - 1, at, :], out_buf.at[k - 1, at, :], out_sem.at[0, k - 1, part],
                           out_sem.at[1, k - 1, part], _peer((z + k) % outer_n, y, x, c)))
            else:
                owned[at, :] = both

    for part in range(max(PARTS, wparts)):
        if part < PARTS:
            token_step(part)
        if part < wparts:
            grad_step(part)

    gain_acc[...] = jnp.zeros_like(gain_acc)
    for part in range(PARTS):
        at = pl.ds(part * size, size)
        view, last = near_buf.at[1, at, :], far_buf.at[at, :]
        _remote(view, view, near_sem.at[0, 1, part], near_sem.at[1, 1, part], me).wait_recv()
        _remote(last, last, far_sem.at[0, part], far_sem.at[1, part], me).wait_recv()
        got = partial[token_rows(x, c, part), :].astype(F32) + view[...].astype(F32) + last[...].astype(F32)
        d_local[at, :] = got
        values = resid[at, :]
        inv = lax.rsqrt(jnp.mean(values * values, axis=-1, keepdims=True) + EPSILON)
        gain_acc[...] += _rows_sum(got * values * inv)

    small_d[0] = small[...]
    for j in range(model // LANES):
        small_d[0, j : j + 1, :] = jnp.sum(gain_acc[:, j * LANES : (j + 1) * LANES], axis=0, keepdims=True)
    first = []
    i = 0
    for k in range(outer_n):
        for j in (0, 1):
            if k or j:
                peer = _peer((z + k) % outer_n, (y + j) % 2, x, c)
                first.append(go(_remote(small_d.at[0], small_d.at[k * 2 + j], small_sem_d.at[0, i],
                                        small_sem_d.at[1, i], peer)))
                i += 1
    for part in range(wparts):
        at = pl.ds(part * bsize, bsize)
        total = owned[at, :]
        for k in order[:-1]:
            view = out_buf.at[k - 1, at, :]
            _remote(view, view, out_sem.at[0, k - 1, part], out_sem.at[1, k - 1, part], me).wait_recv()
            total = total + view[...].astype(F32)
        owned[at, :] = total
    for copy in first:
        copy.wait_recv()
    total = None
    for zz in range(outer_n):
        for yy in (0, 1):
            slot = ((z - zz) % outer_n) * 2 + (y - yy) % 2
            term = small_d[slot]
            total = term if total is None else total + term
    small_out[...] = total
    small_t[0] = total[:small_rows_both, :]
    second = []
    i = 0
    for k in (0, 1):
        for j in (0, 1):
            if k or j:
                peer = _peer(z, y, (x + k) % 2, (c + j) % 2)
                second.append(go(_remote(small_t.at[0], small_t.at[k * 2 + j], small_sem_t.at[0, i],
                                         small_sem_t.at[1, i], peer)))
                i += 1
    for copy in second:
        copy.wait_recv()
    small_out[0:small_rows_both, :] = (small_t[0] + small_t[1]) + (small_t[2] + small_t[3])
    for copy in started:
        copy.wait_send()


def reduce_all(partial, grads, small, resid, gain_rows, both_rows):
    dp, tp = lax.axis_size("dp"), lax.axis_size("tensor")
    outer_n = dp // 2
    own_rows, model = resid.shape
    block, cols = grads.shape[0] // dp, grads.shape[1]
    vm = pl.BlockSpec(memory_space=pltpu.VMEM)
    dma = pltpu.SemaphoreType.DMA
    return pl.pallas_call(
        functools.partial(reduce_kernel, outer_n, both_rows),
        in_specs=[vm] * 5,
        out_specs=[vm] * 3,
        out_shape=[jax.ShapeDtypeStruct((own_rows, model), F32),
                   jax.ShapeDtypeStruct((block, cols), F32),
                   jax.ShapeDtypeStruct(small.shape, F32)],
        scratch_shapes=[pltpu.VMEM((2, own_rows, model), BF),
                        pltpu.VMEM((own_rows, model), BF),
                        pltpu.VMEM((own_rows, model), BF),
                        pltpu.VMEM((outer_n, block, cols), BF),
                        pltpu.VMEM((outer_n - 1, block, cols), BF),
                        pltpu.VMEM((outer_n - 1, block, cols), BF),
                        pltpu.VMEM((dp,) + small.shape, F32),
                        pltpu.VMEM((4, both_rows, LANES), F32),
                        pltpu.VMEM((8, model), F32),
                        dma((2, 2, PARTS)), dma((2, PARTS)), dma((2, outer_n, _parts(block))),
                        dma((2, outer_n - 1, _parts(block))), dma((2, dp - 1)), dma((2, 3))],
        compiler_params=pltpu.CompilerParams(collective_id=1, has_side_effects=True,
                                             vmem_limit_bytes=62 * 2**20),
        cost_estimate=pl.CostEstimate(flops=10**7, bytes_accessed=40 * 2**20, transcendentals=0),
        name="reduce_all",
    )(partial, grads, small, resid, gain_rows)


def _spread(values, index, count):
    size = values.shape[-1]
    full = jnp.zeros(values.shape[:-1] + (size * count,), F32)
    return lax.dynamic_update_slice_in_dim(full, values, index * size, axis=values.ndim - 1)


def _own(values, index, count):
    size = values.shape[-1] // count
    return lax.dynamic_slice_in_dim(values, index * size, size, axis=values.ndim - 1)


def on_device(
    resid_in, norm_gain, proj_zx, proj_dt, proj_bc, conv_x_weight, conv_x_bias, conv_bc_weight,
    conv_bc_bias, dt_bias, a_log, skip_gain, gate_gain, proj_out, cotangent,
):
    dp, tp = lax.axis_size("dp"), lax.axis_size("tensor")
    index = lax.axis_index("dp") * tp + lax.axis_index("tensor")
    count = dp * tp
    model = resid_in.shape[-1]
    width = conv_x_weight.shape[1]
    heads = dt_bias.shape[0]
    inner_channels = width * tp
    states2 = 2 * LANES
    rows = proj_zx.shape[0]
    resid, cot = resid_in[0], cotangent[0]
    small = jnp.concatenate([
        _spread(norm_gain, index, count).reshape(-1, LANES),
        _spread(conv_bc_weight, index, count).reshape(-1, LANES),
        _spread(conv_bc_bias, index, count).reshape(-1, LANES)], axis=0)
    gain_rows = model // LANES
    both_rows = -(-small.shape[0] // 8) * 8
    small = pad_rows(small, both_rows)
    dt_cols = jnp.pad(proj_dt, ((0, 0), (0, LANES - heads)))
    small_all, normed, cot_full, weight, out_t = gather_all(
        small, resid, cot, proj_zx.reshape(rows, 2 * width), dt_cols, proj_bc, proj_out.T)
    full_cbw = small_all[gain_rows : gain_rows + 4 * states2 // LANES].reshape(4, states2)
    full_cbb = small_all[gain_rows + 4 * states2 // LANES : gain_rows + 5 * states2 // LANES].reshape(states2)
    full_gain = small_all[:gain_rows].reshape(model)
    proj = jnp.dot(normed, weight, preferred_element_type=F32)
    d_gated = jnp.dot(cot_full, out_t, preferred_element_type=F32)
    packs = pack_params(conv_x_weight, conv_x_bias, full_cbw, full_cbb, dt_bias, a_log, skip_gain, gate_gain)
    y, states, partial = ssd_forward(proj, d_gated, *packs)
    dy, dz, out_partial, grads_zo, ggain = middle(proj, y, d_gated, partial, packs[3], normed, cot_full, out_t, inner_channels)
    d_rest, gx, gbc, gh, block_sum, owned_zo = ssd_backward(proj, y, dy, states, *packs, out_partial, grads_zo)
    block_out = resid + block_sum
    gx = jnp.concatenate([gx.sum(1), ggain.sum(0)[None]], 0)
    gbc, gh = gbc.sum(1), gh.sum(1)
    d_proj = jnp.concatenate([dz, d_rest], axis=1)
    d_normed = lax.dot_general(d_proj, weight, (((1,), (1,)), ((), ())), preferred_element_type=F32).astype(BF)
    grads = lax.dot_general(normed, d_rest, (((0,), (0,)), ((), ())), preferred_element_type=F32).astype(BF)
    to_sum = jnp.concatenate([
        pad_rows(jnp.concatenate([jnp.zeros((gain_rows, LANES), F32), gbc.reshape(-1, LANES)], 0), both_rows),
        gx.reshape(-1, LANES), gh], axis=0)
    to_sum = pad_rows(to_sum, -(-to_sum.shape[0] // 8) * 8)
    d_local, owned, totals = reduce_all(d_normed, grads, to_sum, resid, small_all, both_rows)
    inv_in = lax.rsqrt(jnp.mean(resid * resid, axis=-1, keepdims=True) + EPSILON)
    scaled = resid * inv_in
    d_scaled = d_local * full_gain
    grad_resid = inv_in * (d_scaled - scaled * jnp.mean(d_scaled * scaled, axis=-1, keepdims=True)) + cot
    grad_zx = jnp.stack([owned_zo[:, :width], owned[:, :width]], axis=1)
    bc_part = owned[:, width : width + states2]
    grad_bc = lax.psum_scatter(bc_part.astype(BF), "tensor", scatter_dimension=0, tiled=True).astype(F32)
    grad_dt = owned[:, width + states2 : width + states2 + heads]
    owned_out = owned_zo[:, width:].T
    owned_gain = _own(totals[:gain_rows].reshape(model), index, count)
    at = gain_rows + 4 * states2 // LANES
    owned_cbw = _own(totals[gain_rows:at].reshape(4, states2), index, count)
    owned_cbb = _own(totals[at : at + states2 // LANES].reshape(states2), index, count)
    gx_all = totals[both_rows : both_rows + 7 * width // LANES].reshape(7, width)
    gh_all = totals[both_rows + 7 * width // LANES :]
    skip = gx_all[5].reshape(heads, -1).sum(1)
    return (
        block_out[None], grad_resid[None], owned_gain, grad_zx, grad_dt, grad_bc, gx_all[:4], gx_all[4],
        owned_cbw, owned_cbb, gh_all[0, :heads], gh_all[1, :heads], skip, gx_all[6], owned_out,
    )


def solution(mesh):
    specs = (
        P("dp", "tensor", None), P(("dp", "tensor")), P("dp", None, "tensor"), P("dp", "tensor"),
        P(("dp", "tensor"), None), P(None, "tensor"), P("tensor"), P(None, ("dp", "tensor")),
        P(("dp", "tensor")), P("tensor"), P("tensor"), P("tensor"), P("tensor"), P("tensor", "dp"),
        P("dp", "tensor", None),
    )
    outs = (specs[0], specs[0]) + specs[1:14]
    return jax.shard_map(on_device, mesh=mesh, in_specs=specs, out_specs=outs, check_vma=False)
```

time: 1320 us -> 439 us (0.33)
  waiting for transfers between devices: 480 us -> 0.02 us
  Pallas kernels: 0 us -> 321 us
  matrix products: 312 us -> 57.3 us
  blocking collectives: 202 us -> 0 us
  other arithmetic: 153 us -> 17.1 us
  local copies, waits for them, and re-layouts: 147 us -> 20.3 us
    reduce_scatter x5 -> x1, waiting for transfers between devices: 392 us -> 0.01 us  [on_device(): lax.psum_scatter(bc_part.astype(BF), 'tensor', scatter_dimension=0, tiled...]
    pallas_call x0 -> x5, Pallas kernels: none -> 321 us  [the longest x1 122 us: gather_all(): pl.pallas_call(functools.partial(gather_kernel, outer_n), in_specs=[vm] *...]
    dot_general x22 -> x4, matrix products: 301 us -> 57.3 us  [the longest x1 19.4 us: on_device(): proj = jnp.dot(normed, weight, preferred_element_type=F32)]
    all_gather x5 -> x0, waiting for transfers between devices: 87.9 us -> none  [the longest x1 70.9 us: on_device(): lax.all_gather(proj_zx, 'dp', axis=0, tiled=True)]
    unnamed x2 -> x0, blocking collectives: 82.2 us -> none
    all_gather x2 -> x0, blocking collectives: 71 us -> none  [the longest x1 40.5 us: on_device(): lax.all_gather(conv_bc_weight, ('dp', 'tensor'), axis=1, tiled=True)]
    psum x3 -> x0, blocking collectives: 48.6 us -> none  [the longest x1 36.2 us: on_device(): lax.psum((core_grads[3], core_grads[4], core_grads[7], core_grads[8], cor...]
    reduce_sum x17 -> x7, other arithmetic: 50.1 us -> 5.85 us  [the longest x1 2.17 us: on_device(): jnp.mean(resid * resid, axis=-1, keepdims=True) + EPSILON]
  transfers between devices with their start and end apart: 11 -> 1, of which waited for: 7 -> 0; matrix products, arithmetic and copies ran while one was open for 27% -> 5% of each run, Pallas kernels for 0% -> 0%
where the time goes in v1:
time: 439 us; the launch traced here: 430 us
  Pallas kernels  321 us (73%)
  matrix products  57.3 us (13%)
  local copies, waits for them, and re-layouts  20.3 us (5%)
  other arithmetic  17.1 us (4%)
  between operations  14.8 us (3%)
    pallas_call x1, Pallas kernels, gather_all(): pl.pallas_call(functools.partial(gather_kernel, outer_n), in_specs=[vm] *...  122 us
    pallas_call x1, Pallas kernels, ssd_backward(): pl.pallas_call(functools.partial(backward_kernel, width, dp // 2), grid=(...  73.1 us
    pallas_call x1, Pallas kernels, reduce_all(): pl.pallas_call(functools.partial(reduce_kernel, outer_n, both_rows), in_s...  61.6 us
    pallas_call x1, Pallas kernels, ssd_forward(): pl.pallas_call(functools.partial(forward_kernel, width), grid=(length //...  34.7 us
    pallas_call x1, Pallas kernels, middle(): pl.pallas_call(functools.partial(middle_kernel, width, inner_channels), g...  29.6 us
    dot_general x1, matrix products, on_device(): proj = jnp.dot(normed, weight, preferred_element_type=F32)  19.4 us
    dot_general x1, matrix products, on_device(): lax.dot_general(d_proj, weight, (((1,), (1,)), ((), ())), preferred_eleme...  17 us
    dot_general x1, matrix products, on_device(): lax.dot_general(normed, d_rest, (((0,), (0,)), ((), ())), preferred_eleme...  14.1 us
  transfers between devices with their start and end apart: 1, of which 0 were waited for; matrix products, arithmetic and copies ran while one was open for 5% of the time, Pallas kernels for 0%

profile of v1, /device:TPU:0, one launch (start us, length us, event | category | flops | bytes accessed | tf_op | source)
XLA Modules:
  0.0 430.2 jit_solution(17399993224604931913)
XLA Ops:
  7.2 0.8 dynamic_update_slice.10
  8.1 1.9 copy.33
  10.0 0.8 copy.30
  10.8 0.9 dynamic_update_slice.11
  11.7 0.6 pad.33.wdt
  12.3 0.8 dynamic_update_slice.9
  13.8 121.8 %gather_all.1 = (f32[24,128]{1,0:T(8,128)}, bf16[2048,1536]{1,0:T(8,128)(2,1)}, bf16[2048,1536]{1,0:T(8,128)(2,1)}, bf16[1536,1920]{1,0:T(8,128)(2,1)}, bf16[1536,768]{1,0:T(8,128)(2,1)}) custom-call(f32[24,128]{1,0:T(8,128)} %select_maximum_fusion.3.small, f32[512,1536]{1,0:T(8,128)} %bitcast.46, f32[512,1536]{1,0:T(8,128)} %bitcast.48, ...), custom_call_target="tpu_custom_call" | custom-call | flops 10000000 | bytes 41943040 | tf_op jit(solution)/shard_map/gather_all/pallas_call | solution.py:825
  135.5 0.7 slice.66
  136.2 0.7 slice.67
  137.7 19.4 %fusion.9.p_ref.z_ref.prev_ref = f32[2048,1920]{1,0:T(8,128)} fusion(bf16[2048,1536]{1,0:T(8,128)(2,1)} %get-tuple-element.37.normed, bf16[1536,1920]{1,0:T(8,128)(2,1)} %get-tuple-element.38), kind=kOutput, calls=%fused_computation.42 | convolution fusion | flops 12079595520 | bytes 27918336 | tf_op jit(solution)/shard_map/dot_general | solution.py:1047
  157.2 6.8 %fusion.10.dg_ref = f32[2048,768]{1,0:T(8,128)} fusion(bf16[2048,1536]{1,0:T(8,128)(2,1)S(1)} %copy-done.11, bf16[1536,768]{1,0:T(8,128)(2,1)S(1)} %copy-done.12), kind=kOutput, calls=%fused_computation.43 | convolution fusion | flops 4831838208 | bytes 14942208 | tf_op jit(solution)/shard_map/dot_general | solution.py:1048
  164.6 0.6 select_maximum_fusion.1
  165.2 34.7 %scan_forward.1 = (f32[2048,768]{1,0:T(8,128)}, f32[16,128,768]{2,1,0:T(8,128)}, f32[32,128]{1,0:T(8,128)}) custom-call(f32[2048,1920]{1,0:T(8,128)} %fusion.9.p_ref.z_ref.prev_ref, f32[2048,768]{1,0:T(8,128)} %fusion.10.dg_ref, f32[8,768]{1,0:T(8,128)} %get-tuple-element.84.convx_ref, f32[8,256]{1,0:T(8,128)} %select_maximum_fusion.5.convbc_ref, ...), custom_call_target="tpu_custom_call" | custom-call | flops 4000000000 | bytes 31457280 | tf_op jit(solution)/shard_map/scan_forward/pallas_call | solution.py:509
  200.0 29.6 %middle.1 = (bf16[2048,768]{1,0:T(8,128)(2,1)}, bf16[2048,768]{1,0:T(8,128)(2,1)}, bf16[2048,1536]{1,0:T(8,128)(2,1)}, bf16[1536,1536]{1,0:T(8,128)(2,1)}, f32[8,768]{1,0:T(8,128)}) custom-call(f32[2048,1920]{1,0:T(8,128)} %fusion.9.p_ref.z_ref.prev_ref, f32[2048,768]{1,0:T(8,128)} %get-tuple-element.42.y_ref, f32[2048,768]{1,0:T(8,128)} %fusion.10.dg_ref, ...), custom_call_target="tpu_custom_call" | custom-call | flops 15000000512 | bytes 52428800 | tf_op jit(solution)/shard_map/middle/pallas_call | solution.py:623
  229.5 73.1 %scan_backward.1 = (bf16[2048,1152]{1,0:T(8,128)(2,1)}, f32[6,8,768]{2,1,0:T(8,128)}, f32[5,8,256]{2,1,0:T(8,128)}, f32[2,8,128]{2,1,0:T(8,128)}, f32[512,1536]{1,0:T(8,128)}, /*index=5*/f32[192,1536]{1,0:T(8,128)}) custom-call(f32[2048,1920]{1,0:T(8,128)} %fusion.9.p_ref.z_ref.prev_ref, f32[2048,1920]{1,0:T(8,128)} %fusion.9.p_ref.z_ref.prev_ref, ...), custom_call_target="tpu_custom_call" | custom-call | flops 12000000000 | bytes 52428800 | tf_op jit(solution)/shard_map/scan_backward/pallas_call | solution.py:544
  302.6 1.0 reduce_sum.65
  303.7 0.8 reduce_sum.64
  304.5 0.7 reduce_sum.67
  305.9 14.1 %convolution_convert_fusion.grads = bf16[1536,1152]{1,0:T(8,128)(2,1)} fusion(bf16[2048,1536]{1,0:T(8,128)(2,1)} %get-tuple-element.37.normed, bf16[2048,1152]{1,0:T(8,128)(2,1)} %get-tuple-element.50), kind=kOutput, calls=%fused_computation.5 | convolution fusion | flops 7249526784 | bytes 14548992 | tf_op jit(solution)/shard_map/dot_general | solution.py:1058
  320.0 17.0 %fusion.4.partial = bf16[2048,1536]{1,0:T(8,128)(2,1)} fusion(bf16[1536,1920]{1,0:T(8,128)(2,1)} %get-tuple-element.38, bf16[2048,1152]{1,0:T(8,128)(2,1)S(1)} %bitcast.58, bf16[2048,768]{1,0:T(8,128)(2,1)S(1)} %copy-done.13), kind=kOutput, calls=%fused_computation.4 | convolution fusion | flops 12098469888 | bytes 20054016 | tf_op jit(solution)/shard_map/dot_general | solution.py:1057
  337.0 61.6 %reduce_all.1 = (f32[512,1536]{1,0:T(8,128)}, f32[192,1152]{1,0:T(8,128)}, f32[72,128]{1,0:T(8,128)}) custom-call(bf16[2048,1536]{1,0:T(8,128)(2,1)} %fusion.4.partial, bf16[1536,1152]{1,0:T(8,128)(2,1)} %convolution_convert_fusion.grads, f32[72,128]{1,0:T(8,128)} %pad.39.small, f32[512,1536]{1,0:T(8,128)} %bitcast.47, f32[24,128]{1,0:T(8,128)} %get-tuple-element.41.gain), custom_call_target="tpu_custom_call" | custom-call | flops 10000000 | bytes 41943040 | tf_op jit(solution)/shard_map/reduce_all/pallas_call | solution.py:984
  398.6 1.6 slice.96
  400.2 1.1 slice_bitcast_fusion.1
  401.3 2.2 multiply_reduce_fusion.1
  403.5 0.9 slice.72
  405.1 2.3 slice_bitcast_fusion
  407.4 1.9 copy.31
  409.9 0.7 copy.32
  411.9 0.6 reduce_sum.69
  412.5 0.6 constant_dynamic-slice_fusion
  413.7 7.3 %add_bitcast_fusion = (f32[1,512,1536]{2,1,0:T(8,128)}, f32[1,512,1536]{2,1,0:T(8,128)}) fusion(f32[512,1536]{1,0:T(8,128)} %get-tuple-element.55, f32[512]{0:T(512)S(1)} %broadcast_multiply_fusion, f32[1536]{0:T(1024)S(1)} %slice_bitcast_fusion.4, f32[512]{0:T(512)S(1)} %add_rsqrt_fusion, f32[1,512,1536]{2,1,0:T(8,128)} %param.29, ...), kind=kLoop, calls=%fused_computation.6 | loop fusion | flops 5505024 | bytes 18884608 | tf_op jit(solution)/shard_map/broadcast_in_dim | solution.py:1081
  421.6 1.4 convert_element_type.27
  (71 shorter events, 6.4 us)
Async XLA Ops:
  7.2 414.4 %reduce-scatter.2.cloned.1.call-start = ((), (), s32[]{:S(2)}) async-start(), calls=%async_computation.1 | async-start | bytes 122880 | tf_op jit(solution)/shard_map/reduce_scatter | solution.py:1070
  13.8 123.2 %copy-start.8 = (f32[12]{0:T(128)S(1)}, f32[12]{0:T(128)}, u32[]{:S(2)}) copy-start(f32[12]{0:T(128)} %param.26) | copy-start | bytes 148
  13.8 123.3 %copy-start.6 = (f32[768]{0:T(1024)S(1)}, f32[768]{0:T(1024)}, u32[]{:S(2)}) copy-start(f32[768]{0:T(1024)} %param.21) | copy-start | bytes 9220
  13.8 123.3 %copy-start.7 = (f32[768]{0:T(1024)S(1)}, f32[768]{0:T(1024)}, u32[]{:S(2)}) copy-start(f32[768]{0:T(1024)} %param.27) | copy-start | bytes 9220
  137.7 19.4 %copy-start.11 = (bf16[2048,1536]{1,0:T(8,128)(2,1)S(1)}, bf16[2048,1536]{1,0:T(8,128)(2,1)}, u32[]{:S(2)}) copy-start(bf16[2048,1536]{1,0:T(8,128)(2,1)} %get-tuple-element.39.cot) | copy-start | bytes 18874372
  137.7 19.4 %copy-start.12 = (bf16[1536,768]{1,0:T(8,128)(2,1)S(1)}, bf16[1536,768]{1,0:T(8,128)(2,1)}, u32[]{:S(2)}) copy-start(bf16[1536,768]{1,0:T(8,128)(2,1)} %get-tuple-element.40.out_t) | copy-start | bytes 7077892
  157.1 6.9 %copy-start.9 = (f32[12]{0:T(128)S(1)}, f32[12]{0:T(128)}, u32[]{:S(2)}) copy-start(f32[12]{0:T(128)} %param.25) | copy-start | bytes 148
  157.1 6.9 %copy-start.10 = (f32[12]{0:T(128)S(1)}, f32[12]{0:T(128)}, u32[]{:S(2)}) copy-start(f32[12]{0:T(128)} %param.24) | copy-start | bytes 148
  157.1 7.5 %copy-start.5 = (f32[4,768]{1,0:T(4,128)S(1)}, f32[4,768]{1,0:T(4,128)}, u32[]{:S(2)}) copy-start(f32[4,768]{1,0:T(4,128)} %param.20) | copy-start | bytes 36868
  229.5 74.1 %copy-start.4 = (f32[8,768]{1,0:T(8,128)S(1)}, f32[8,768]{1,0:T(8,128)}, u32[]{:S(2)}) copy-start(f32[8,768]{1,0:T(8,128)} %get-tuple-element.53) | copy-start | bytes 73732
  303.6 16.4 %slice-start = ((s8[4718592]{0:T(1024)(128)(4,1)}), s8[524288]{0:T(1024)(128)(4,1)S(1)}, s32[]{:S(2)}) async-start(s8[4718592]{0:T(1024)(128)(4,1)} %bitcast.57), calls=%async_computation.2 | async-start | bytes 1048576
  305.9 14.1 %slice-start.1 = ((s8[4718592]{0:T(1024)(128)(4,1)}), s8[4194304]{0:T(1024)(128)(4,1)S(1)}, s32[]{:S(2)}) async-start(s8[4718592]{0:T(1024)(128)(4,1)} %bitcast.57), calls=%async_computation.3 | async-start | bytes 8388608
  305.9 14.1 %copy-start.13 = (bf16[2048,768]{1,0:T(8,128)(2,1)S(1)}, bf16[2048,768]{1,0:T(8,128)(2,1)}, u32[]{:S(2)}) copy-start(bf16[2048,768]{1,0:T(8,128)(2,1)} %get-tuple-element.49) | copy-start | bytes 9437188
  336.9 64.4 %copy-start.2 = (f32[24,128]{1,0:T(8,128)S(1)}, f32[24,128]{1,0:T(8,128)}, u32[]{:S(2)}) copy-start(f32[24,128]{1,0:T(8,128)} %get-tuple-element.41.gain) | copy-start | bytes 36868
  398.6 5.8 %copy-start.3 = (f32[72,128]{1,0:T(8,128)S(1)}, f32[72,128]{1,0:T(8,128)}, u32[]{:S(2)}) copy-start(f32[72,128]{1,0:T(8,128)} %get-tuple-element.56) | copy-start | bytes 110596
  405.0 4.3 %copy-start = (f32[1,512,1536]{2,1,0:T(8,128)S(1)}, f32[1,512,1536]{2,1,0:T(8,128)}, u32[]{:S(2)}) copy-start(f32[1,512,1536]{2,1,0:T(8,128)} %param.15) | copy-start | bytes 9437188
  405.1 4.3 %copy-start.1 = (f32[512,1536]{1,0:T(8,128)S(1)}, f32[512,1536]{1,0:T(8,128)}, u32[]{:S(2)}) copy-start(f32[512,1536]{1,0:T(8,128)} %get-tuple-element.55) | copy-start | bytes 9437188
Sparse Core Ops, SparseCore 0:
  400.3 19.8 reduce-scatter.1

commit v2 on v1

--- a/solution.py
+++ b/solution.py
@@ -67,7 +67,6 @@
         self.own_rows = block_sum.shape[0]
         self.block = owned.shape[0]
         self.wparts = _parts(self.block)
-        self.late = -(-self.wparts // 6)
         self.size = self.own_rows // PARTS
         self.bsize = self.block // self.wparts
         order = list(range(1, outer_n))
@@ -117,8 +116,8 @@
         _greet(self.outer_n)
         for part in range(PARTS):
             self.near_copy(0, part).start()
-        for part in range(self.wparts):
-            for k in self.order:
+        for k in self.order:
+            for part in range(self.wparts):
                 self.in_copy(k, part).start()
         for part in range(PARTS):
             self.near_copy(1, part).start()
@@ -135,29 +134,33 @@
         self.far_src[at, :] = (self.own_tokens[0, at, :].astype(F32) + self.near_buf[0, at, :].astype(F32)).astype(BF)
         self.far_copy(part).start()
 
-    def grad_step(self, part):
+    def grad_step(self, k, part):
         at = pl.ds(part * self.bsize, self.bsize)
-        for k in self.order:
-            self.in_copy(k, part).wait_recv()
-            both = self.own_grads[k, at, :].astype(F32) + self.in_buf[k, at, :].astype(F32)
-            if k:
-                self.out_src[k - 1, at, :] = both.astype(BF)
-                self.out_copy(k, part).start()
-            else:
-                self.owned[at, :] = both
+        self.in_copy(k, part).wait_recv()
+        both = self.own_grads[k, at, :].astype(F32) + self.in_buf[k, at, :].astype(F32)
+        if k:
+            self.out_src[k - 1, at, :] = both.astype(BF)
+            self.out_copy(k, part).start()
+        else:
+            self.owned[at, :] = both
+
+    def grad_steps(self):
+        return [(k, part) for k in self.order for part in range(self.wparts)]
 
     def plan(self, steps):
         pieces = [(1, self.ready)]
         for part in range(PARTS):
             pieces.append((min(1 + part, steps - 1), functools.partial(self.token_step, part)))
-        for part in range(self.wparts - self.late):
-            pieces.append((min(2 + part * (steps - 2) // self.wparts, steps - 1),
-                           functools.partial(self.grad_step, part)))
+        todo = self.grad_steps()
+        self.late = len(todo) // 8
+        for i, (k, part) in enumerate(todo[: len(todo) - self.late]):
+            pieces.append((min(1 + (i + 2) * (steps - 1) // len(todo), steps - 1),
+                           functools.partial(self.grad_step, k, part)))
         return pieces
 
     def end(self):
-        for part in range(self.wparts - self.late, self.wparts):
-            self.grad_step(part)
+        for k, part in self.grad_steps()[-self.late :]:
+            self.grad_step(k, part)
         for part in range(PARTS):
             at = pl.ds(part * self.size, self.size)
             self.near_copy(1, part).wait_recv()
@@ -651,359 +654,535 @@
     head = jnp.pad(jnp.stack([dt_bias, a_log]), ((0, 6), (0, LANES - heads)))
     lane = pad_rows(jnp.stack([jnp.repeat(skip_gain, width // heads), gate_gain]), 8)
     return convx, convbc, head, lane
-def gather_kernel(outer_n, small, resid, cot, wzx, wdt, wbc, wout,
-                  small_all, normed_all, cot_all, weight, weight_out,
-                  small_t, small_d, normed_own, cot_own, bc_slots, bc_rows,
-                  small_sem_t, small_sem_d, bc_sem, norm_sem, cot_sem, zx_sem, bd_sem, wo_sem, local_sem):
+def gather_kernel(outer_n, heads, small, wzx, wdt, wbc, wout, resid_in, cot_in,
+                  small_all, normed_out, cot_out, weight_out, wout_out, proj, d_gated,
+                  normed, cot, weight, w_out, resid, cot_f, stage, stage_g,
+                  small_t, small_d, bc_slots, dt_slots,
+                  small_sem_t, small_sem_d, bc_sem_t, bc_sem_d, dt_sem, norm_sem, cot_sem, zx_sem, wo_sem,
+                  local_sem, stage_sem, stage_g_sem):
     z, y, x, c = _place()
+    me = _peer(z, y, x, c)
     t = x * 2 + c
     d = z * 2 + y
-    block = wzx.shape[0]
-    zx_cols = wzx.shape[1]
+    block, zx_cols = wzx.shape
     bc_cols = wbc.shape[1]
+    bc_rows = wbc.shape[0]
     wparts = _parts(block)
-    own_rows = resid.shape[0]
-    model = resid.shape[1]
-    cot_own[...] = cot[...].astype(BF)
+    bsize = block // wparts
+    own_rows, model = resid.shape
+    size = own_rows // PARTS
+    length = normed.shape[0]
+    tile = stage.shape[1]
+    loads = [pltpu.make_async_copy(resid_in, resid, local_sem.at[0]),
+             pltpu.make_async_copy(cot_in, cot_f, local_sem.at[1])]
+    for copy in loads:
+        copy.start()
     _greet(outer_n)
-    started = []
-
-    def go(copy):
-        copy.start()
-        started.append(copy)
-        return copy
-
     dp_peers = [(k, j) for k in range(outer_n) for j in (0, 1) if k or j]
     tensor_peers = [(k, j) for k in (0, 1) for j in (0, 1) if k or j]
-    small_first, bc_first = [], []
-    for i, (k, j) in enumerate(dp_peers):
-        peer = _peer((z + k) % outer_n, (y + j) % 2, x, c)
-        small_first.append(go(_remote(small, small_d.at[i], small_sem_d.at[0, i], small_sem_d.at[1, i], peer)))
-    for i, (k, j) in enumerate(tensor_peers):
-        peer = _peer(z, y, (x + k) % 2, (c + j) % 2)
-        bc_first.append(go(_remote(wbc, bc_slots.at[t], bc_sem.at[0, i], bc_sem.at[1, i], peer)))
-    bc_slots[t] = wbc[...]
-
-    order = [k for k in range(1, outer_n)]
+    order = list(range(1, outer_n))
     order.sort(key=lambda k: -min(k, outer_n - k))
-
-    def block_rows(outer, inner, part):
-        size = block // wparts
-        return _rows((outer * 2 + inner) * block + part * size, size)
-
-    def send_out(src, dst, cols, sem, part):
-        size = block // wparts
-        rows = block_rows(z, y, part)
-        piece = src.at[part * size : (part + 1) * size, :]
+    at_dp = lambda k, j: _peer((z + k) % outer_n, (y + j) % 2, x, c)
+    at_tensor = lambda k, j: _peer(z, y, (x + k) % 2, (c + j) % 2)
+
+    small_first = [_remote(small, small_d.at[i], small_sem_d.at[0, i], small_sem_d.at[1, i], at_dp(k, j))
+                   for i, (k, j) in enumerate(dp_peers)]
+    bc_first = [_remote(wbc, bc_slots.at[t, d], bc_sem_d.at[0, i], bc_sem_d.at[1, i], at_dp(k, j))
+                for i, (k, j) in enumerate(dp_peers)]
+    dt_first = [_remote(wdt, dt_slots.at[d], dt_sem.at[0, i], dt_sem.at[1, i], at_dp(k, j))
+                for i, (k, j) in enumerate(dp_peers)]
+    for copy in small_first + bc_first + dt_first:
+        copy.start()
+
+    def rows_of(outer, inner, part):
+        return _rows((outer * 2 + inner) * block + part * bsize, bsize)
+
+    def across(src, dst, cols, sem, k, part):
+        return _remote(src.at[pl.ds(part * bsize, bsize), :], dst.at[rows_of(z, y, part), cols],
+                       sem.at[0, k, part], sem.at[1, k, part], _peer(lax.rem(z + k, outer_n), y, x, c))
+
+    def beside(src, dst, cols, sem, part):
+        return _remote(src.at[pl.ds(part * bsize, bsize), :], dst.at[rows_of(z, y, part), cols],
+                       sem.at[2, 0, part], sem.at[3, 0, part], _peer(z, 1 - y, x, c))
+
+    def onward(dst, cols, sem, k, part):
+        view = dst.at[rows_of(lax.rem(z - k + outer_n, outer_n), y, part), cols]
+        return _remote(view, view, sem.at[2, k, part], sem.at[3, k, part], _peer(z, 1 - y, x, c))
+
+    def send_out(src, dst, cols, sem):
+        for part in range(wparts):
+            for k in order:
+                across(src, dst, cols, sem, k, part).start()
+            beside(src, dst, cols, sem, part).start()
+
+    def pass_on(src, dst, cols, sem, part):
         for k in order:
-            go(_remote(piece, dst.at[rows, cols], sem.at[0, k, part], sem.at[1, k, part],
-                       _peer((z + k) % outer_n, y, x, c)))
-        go(_remote(piece, dst.at[rows, cols], sem.at[2, 0, part], sem.at[3, 0, part],
-                   _peer(z, 1 - y, x, c)))
-
-    def pass_on(dst, cols, sem, part):
-        for k in order:
-            rows = block_rows((z - k) % outer_n, y, part)
-            view = dst.at[rows, cols]
-            _remote(view, view, sem.at[0, k, part], sem.at[1, k, part], _peer(z, y, x, c)).wait_recv()
-            go(_remote(view, view, sem.at[2, k, part], sem.at[3, k, part], _peer(z, 1 - y, x, c)))
-
-    def finish(dst, cols, sem, part):
-        for k in range(outer_n):
-            view = dst.at[block_rows((z - k) % outer_n, 1 - y, part), cols]
-            _remote(view, view, sem.at[2, k, part], sem.at[3, k, part], _peer(z, y, x, c)).wait_recv()
-
-    zx_at = slice(0, zx_cols)
-    bc_at = slice(zx_cols, zx_cols + bc_cols)
-    dt_at = slice(zx_cols + bc_cols, weight.shape[1])
-    all_cols = slice(0, wout.shape[1])
-    for part in range(wparts):
-        send_out(wzx, weight, zx_at, zx_sem, part)
-
-    for copy in small_first:
+            across(src, dst, cols, sem, k, part).wait_recv()
+            onward(dst, cols, sem, k, part).start()
+
+    def finish(src, dst, cols, sem):
+        for part in range(wparts):
+            for k in range(outer_n):
+                onward(dst, cols, sem, k, part).wait_recv()
+
+    def finish_sends(src, dst, cols, sem):
+        for part in range(wparts):
+            beside(src, dst, cols, sem, part).wait_send()
+            for k in order:
+                across(src, dst, cols, sem, k, part).wait_send()
+                onward(dst, cols, sem, k, part).wait_send()
+
+    zx = (wzx, weight, pl.ds(0, zx_cols), zx_sem)
+    wo = (wout, w_out, pl.ds(0, wout.shape[1]), wo_sem)
+    send_out(*zx)
+    mine = _rows(d * block, block)
+    place = [pltpu.make_async_copy(wzx, weight.at[mine, pl.ds(0, zx_cols)], local_sem.at[2]),
+             pltpu.make_async_copy(wout, w_out.at[mine, :], local_sem.at[3])]
+    for copy in place:
+        copy.start()
+    bc_slots[t, d] = wbc[...]
+    dt_slots[d] = wdt[...]
+    loads[0].wait()
+    values = resid[...]
+    inv = lax.rsqrt(jnp.mean(values * values, axis=-1, keepdims=True) + EPSILON)
+
+    for copy in small_first + bc_first:
         copy.wait_recv()
     total = small[...]
     for i in range(len(dp_peers)):
         total = total + small_d[i]
     small_t[3] = total
-    second = []
-    for i, (k, j) in enumerate(tensor_peers):
-        peer = _peer(z, y, (x + k) % 2, (c + j) % 2)
-        second.append(go(_remote(small_t.at[3], small_t.at[i], small_sem_t.at[0, i], small_sem_t.at[1, i], peer)))
-
-    values = resid[...]
-    inv = lax.rsqrt(jnp.mean(values * values, axis=-1, keepdims=True) + EPSILON)
-    for copy in second:
+    small_second = [_remote(small_t.at[3], small_t.at[i], small_sem_t.at[0, i], small_sem_t.at[1, i], at_tensor(k, j))
+                    for i, (k, j) in enumerate(tensor_peers)]
+    bc_second = [_remote(bc_slots.at[t], bc_slots.at[t], bc_sem_t.at[0, i], bc_sem_t.at[1, i], at_tensor(k, j))
+                 for i, (k, j) in enumerate(tensor_peers)]
+    for copy in small_second:
+        copy.start()
+    send_out(*wo)
+    for copy in small_second:
         copy.wait_recv()
     total = small_t[3]
-    for i in range(len(second)):
+    for i in range(3):
         total = total + small_t[i]
     small_all[...] = total
+    own_at = _rows(t * own_rows, own_rows)
     for j in range(model // LANES):
         lanes = slice(j * LANES, (j + 1) * LANES)
-        normed_own[:, lanes] = (resid[:, lanes] * inv * total[j : j + 1, :]).astype(BF)
+        normed[own_at, lanes] = (resid[:, lanes] * inv * total[j : j + 1, :]).astype(BF)
 
     def token_rows(far, near, part):
-        size = own_rows // PARTS
         return _rows((far * 2 + near) * own_rows + part * size, size)
 
-    def send_tokens(src, dst, sem, part):
-        size = own_rows // PARTS
-        piece = src.at[part * size : (part + 1) * size, :]
-        view = dst.at[token_rows(x, c, part), :]
-        go(_remote(piece, view, sem.at[0, 0, part], sem.at[1, 0, part], _peer(z, y, 1 - x, c)))
-        go(_remote(piece, view, sem.at[0, 1, part], sem.at[1, 1, part], _peer(z, y, x, 1 - c)))
-
-    def pass_tokens(dst, sem, part):
-        view = dst.at[token_rows(1 - x, c, part), :]
-        _remote(view, view, sem.at[0, 0, part], sem.at[1, 0, part], _peer(z, y, x, c)).wait_recv()
-        go(_remote(view, view, sem.at[0, 2, part], sem.at[1, 2, part], _peer(z, y, x, 1 - c)))
-
-    def finish_tokens(dst, sem, part):
-        for i, far in ((1, x), (2, 1 - x)):
-            view = dst.at[token_rows(far, 1 - c, part), :]
-            _remote(view, view, sem.at[0, i, part], sem.at[1, i, part], _peer(z, y, x, c)).wait_recv()
-
-    for part in range(PARTS):
-        send_tokens(normed_own, normed_all, norm_sem, part)
-    for part in range(PARTS):
-        send_tokens(cot_own, cot_all, cot_sem, part)
-    for copy in bc_first:
+    def token_copy(buf, sem, which, part):
+        far = 1 - x if which == 2 else x
+        view = buf.at[token_rows(far, c, part), :]
+        peer = _peer(z, y, 1 - x, c) if which == 0 else _peer(z, y, x, 1 - c)
+        return _remote(view, view, sem.at[0, which, part], sem.at[1, which, part], peer)
+
+    def send_tokens(buf, sem):
+        for part in range(PARTS):
+            token_copy(buf, sem, 0, part).start()
+            token_copy(buf, sem, 1, part).start()
+
+    def pass_tokens(buf, sem, part):
+        token_copy(buf, sem, 0, part).wait_recv()
+        token_copy(buf, sem, 2, part).start()
+
+    def finish_tokens(buf, sem):
+        for part in range(PARTS):
+            token_copy(buf, sem, 1, part).wait_recv()
+            token_copy(buf, sem, 2, part).wait_recv()
+
+    send_tokens(normed, norm_sem)
+    for copy in bc_second:
+        copy.start()
+    loads[1].wait()
+    cot[own_at, :] = cot_f[...].astype(BF)
+    send_tokens(cot, cot_sem)
+    for copy in dt_first:
         copy.wait_recv()
-    for i in range(4):
-        bc_rows[i * wbc.shape[0] : (i + 1) * wbc.shape[0], :] = bc_slots[i]
-    for part in range(wparts):
-        send_out(bc_rows, weight, bc_at, bd_sem.at[0], part)
-        send_out(wdt, weight, dt_at, bd_sem.at[1], part)
-        send_out(wout, weight_out, all_cols, wo_sem, part)
-    mine = _rows(d * block, block)
-    tokens = _rows(t * own_rows, own_rows)
-    local = [
-        pltpu.make_async_copy(wzx, weight.at[mine, zx_at], local_sem.at[0]),
-        pltpu.make_async_copy(bc_rows, weight.at[mine, bc_at], local_sem.at[1]),
-        pltpu.make_async_copy(wdt, weight.at[mine, dt_at], local_sem.at[2]),
-        pltpu.make_async_copy(wout, weight_out.at[mine, :], local_sem.at[3]),
-        pltpu.make_async_copy(normed_own, normed_all.at[tokens, :], local_sem.at[4]),
-        pltpu.make_async_copy(cot_own, cot_all.at[tokens, :], local_sem.at[5]),
-    ]
-    for copy in local:
-        copy.start()
+    for copy in place:
+        copy.wait()
+    for i in range(outer_n * 2):
+        columns = dt_slots[i].astype(F32)
+        columns = jnp.concatenate([columns, jnp.zeros((LANES - columns.shape[0], columns.shape[1]), F32)], axis=0)
+        weight[i * block : (i + 1) * block, zx_cols + bc_cols :] = columns.T[:block, :].astype(BF)
     for part in range(max(PARTS, wparts)):
         if part < wparts:
-            pass_on(weight, zx_at, zx_sem, part)
+            pass_on(*zx, part)
         if part < PARTS:
-            pass_tokens(normed_all, norm_sem, part)
-    for part in range(max(PARTS, wparts)):
-        if part < wparts:
-            pass_on(weight, bc_at, bd_sem.at[0], part)
-            pass_on(weight, dt_at, bd_sem.at[1], part)
-            pass_on(weight_out, all_cols, wo_sem, part)
-        if part < PARTS:
-            pass_tokens(cot_all, cot_sem, part)
-    for part in range(wparts):
-        finish(weight, zx_at, zx_sem, part)
-        finish(weight, bc_at, bd_sem.at[0], part)
-        finish(weight, dt_at, bd_sem.at[1], part)
-        finish(weight_out, all_cols, wo_sem, part)
+            pass_tokens(normed, norm_sem, part)
+    for copy in bc_second:
+        copy.wait_recv()
+    for i in range(outer_n * 2):
+        for j in range(4):
+            first = i * block + j * bc_rows
+            weight[first : first + bc_rows, zx_cols : zx_cols + bc_cols] = bc_slots[j, i]
+    finish_tokens(normed, norm_sem)
+    finish(*zx)
+    save = [pltpu.make_async_copy(normed, normed_out, local_sem.at[4]),
+            pltpu.make_async_copy(weight, weight_out, local_sem.at[5])]
+    for copy in save:
+        copy.start()
+
+    steps = length // tile
+
+    def store(ref, buf, sem, i):
+        slot = lax.rem(i, 2)
+        return pltpu.make_async_copy(buf.at[slot], ref.at[pl.ds(pl.multiple_of(i * tile, tile), tile), :], sem.at[slot])
+
+    @pl.loop(0, steps)
+    def _(i):
+        @pl.when(i >= 2)
+        def _():
+            store(proj, stage, stage_sem, i - 2).wait()
+
+        rows = pl.ds(pl.multiple_of(i * tile, tile), tile)
+        stage[lax.rem(i, 2)] = jnp.dot(normed[rows, :], weight[...], preferred_element_type=F32)
+        store(proj, stage, stage_sem, i).start()
+
+        @pl.when(i < wparts)
+        def _():
+            pass_on(*wo, i)
+
+        @pl.when(i < PARTS)
+        def _():
+            pass_tokens(cot, cot_sem, i)
+
+    for i in range(steps, wparts):
+        pass_on(*wo, i)
+    for i in range(steps, PARTS):
+        pass_tokens(cot, cot_sem, i)
+    finish_tokens(cot, cot_sem)
+    finish(*wo)
+    save_late = [pltpu.make_async_copy(cot, cot_out, local_sem.at[6]),
+                 pltpu.make_async_copy(w_out, wout_out, local_sem.at[7])]
+    for copy in save_late:
+        copy.start()
+
+    @pl.loop(0, steps)
+    def _(i):
+        @pl.when(i >= 2)
+        def _():
+            store(d_gated, stage_g, stage_g_sem, i - 2).wait()
+
+        rows = pl.ds(pl.multiple_of(i * tile, tile), tile)
+        stage_g[lax.rem(i, 2)] = jnp.dot(cot[rows, :], w_out[...], preferred_element_type=F32)
+        store(d_gated, stage_g, stage_g_sem, i).start()
+
+    for i in range(max(steps - 2, 0), steps):
+        store(proj, stage, stage_sem, i).wait()
+        store(d_gated, stage_g, stage_g_sem, i).wait()
+    finish_sends(*zx)
+    finish_sends(*wo)
     for part in range(PARTS):
-        finish_tokens(normed_all, norm_sem, part)
-        finish_tokens(cot_all, cot_sem, part)
-    for copy in started:
+        for which in range(3):
+            token_copy(normed, norm_sem, which, part).wait_send()
+            token_copy(cot, cot_sem, which, part).wait_send()
+    for copy in small_first + bc_first + dt_first + small_second + bc_second:
         copy.wait_send()
-    for copy in local:
+    for copy in save + save_late:
         copy.wait()
 
 
-def gather_all(small, resid, cot, wzx, wdt, wbc, wout):
+def gather_all(small, resid, cot, wzx, wdt, wbc, wout, tile=256):
     dp, tp = lax.axis_size("dp"), lax.axis_size("tensor")
     outer_n = dp // 2
     block, zx_cols = wzx.shape
-    total = zx_cols + wbc.shape[1] + wdt.shape[1]
+    total = zx_cols + wbc.shape[1] + LANES
+    width = wout.shape[1]
+    heads = wdt.shape[1]
+    length, model = resid.shape[0] * tp, resid.shape[1]
+    wdt = jnp.pad(wdt.T, ((0, -heads % 16), (0, -block % LANES)))
+    wparts = _parts(block)
     vm = pl.BlockSpec(memory_space=pltpu.VMEM)
     hbm = pl.BlockSpec(memory_space=pl.ANY)
     dma = pltpu.SemaphoreType.DMA
+    shape = jax.ShapeDtypeStruct
     return pl.pallas_call(
-        functools.partial(gather_kernel, outer_n),
-        in_specs=[vm] * 7,
-        out_specs=[vm, hbm, hbm, hbm, hbm],
-        out_shape=[jax.ShapeDtypeStruct(small.shape, F32),
-                   jax.ShapeDtypeStruct((resid.shape[0] * tp, resid.shape[1]), BF),
-                   jax.ShapeDtypeStruct((resid.shape[0] * tp, resid.shape[1]), BF),
-                   jax.ShapeDtypeStruct((block * dp, total), BF),
-                   jax.ShapeDtypeStruct((block * dp, wout.shape[1]), BF)],
-        scratch_shapes=[pltpu.VMEM((4,) + small.shape, F32),
-                        pltpu.VMEM((dp - 1,) + small.shape, F32),
-                        pltpu.VMEM(resid.shape, BF),
-                        pltpu.VMEM(resid.shape, BF),
-                        pltpu.VMEM((4,) + wbc.shape, BF),
-                        pltpu.VMEM((block, wbc.shape[1]), BF),
-                        dma((2, 3)), dma((2, dp - 1)), dma((2, 3)), dma((2, 3, PARTS)), dma((2, 3, PARTS)),
-                        dma((4, outer_n, _parts(block))), dma((2, 4, outer_n, _parts(block))), dma((4, outer_n, _parts(block))),
-                        dma((6,))],
-        compiler_params=pltpu.CompilerParams(collective_id=0, has_side_effects=True),
-        cost_estimate=pl.CostEstimate(flops=10**7, bytes_accessed=40 * 2**20, transcendentals=0),
+        functools.partial(gather_kernel, outer_n, heads),
+        in_specs=[vm] * 5 + [hbm] * 2,
+        out_specs=[vm] + [hbm] * 6,
+        out_shape=[shape(small.shape, F32), shape((length, model), BF), shape((length, model), BF),
+                   shape((model, total), BF), shape((model, width), BF),
+                   shape((length, total), F32), shape((length, width), F32)],
+        scratch_shapes=[pltpu.VMEM((length, model), BF), pltpu.VMEM((length, model), BF),
+                        pltpu.VMEM((model, total), BF), pltpu.VMEM((model, width), BF),
+                        pltpu.VMEM(resid.shape, F32), pltpu.VMEM(resid.shape, F32),
+                        pltpu.VMEM((2, tile, total), F32), pltpu.VMEM((2, tile, width), F32),
+                        pltpu.VMEM((4,) + small.shape, F32), pltpu.VMEM((dp - 1,) + small.shape, F32),
+                        pltpu.VMEM((4, dp) + wbc.shape, BF), pltpu.VMEM((dp,) + wdt.shape, BF),
+                        dma((2, 3)), dma((2, dp - 1)), dma((2, 3)), dma((2, dp - 1)), dma((2, dp - 1)),
+                        dma((2, 3, PARTS)), dma((2, 3, PARTS)), dma((4, outer_n, wparts)), dma((4, outer_n, wparts)),
+                        dma((8,)), dma((2,)), dma((2,))],
+        compiler_params=pltpu.CompilerParams(collective_id=0, has_side_effects=True, vmem_limit_bytes=62 * 2**20),
+        cost_estimate=pl.CostEstimate(flops=17 * 10**9, bytes_accessed=60 * 2**20, transcendentals=0),
         name="gather_all",
-    )(small, resid, cot, wzx, wdt, wbc, wout)
-
-
-def reduce_kernel(outer_n, small_rows_both, partial, grads, small, resid, gain,
-                  d_local, owned, small_out,
-                  near_buf, far_src, far_buf, in_buf, out_src, out_buf, small_d, small_t, gain_acc,
-                  near_sem, far_sem, in_sem, out_sem, small_sem_d, small_sem_t):
+    )(small, wzx, wdt, wbc, wout, resid, cot)
+
+
+def final_kernel(outer_n, both_rows, gain_rows, dz_in, rest_in, weight_in, normed_in, resid_in, small,
+                 d_local, owned, small_out, bc_out,
+                 dz, rest, weight, normed, resid, g_all, tok, near_buf, far_src, far_buf, in_buf, out_src, out_buf,
+                 small_d, small_t, gain_d, gain_t, gain_acc, bc_src, bc_buf,
+                 load_sem, near_sem, far_sem, in_sem, out_sem, small_sem_d, small_sem_t, gain_sem_d, gain_sem_t, bc_sem):
     z, y, x, c = _place()
-    own_rows = resid.shape[0]
-    model = resid.shape[1]
-    block = owned.shape[0]
-    pairs_n = partial.shape[0] // (4 * own_rows)
-    _greet(outer_n)
-    started = []
-
-    def go(copy):
-        copy.start()
-        started.append(copy)
-        return copy
-
     me = _peer(z, y, x, c)
-    size = own_rows // PARTS
+    t = x * 2 + c
+    own_rows, model = d_local.shape
+    block, cols = owned.shape
+    width = dz.shape[1]
     wparts = _parts(block)
     bsize = block // wparts
-
-    def token_rows(far, near, part):
-        return _rows((far * 2 + near) * own_rows + part * size, size)
-
-    for part in range(PARTS):
-        for i, far in ((0, 1 - x), (1, x)):
-            at = pl.ds(part * size, size)
-            go(_remote(partial.at[token_rows(far, 1 - c, part), :], near_buf.at[i, at, :],
-                       near_sem.at[0, i, part], near_sem.at[1, i, part], _peer(z, y, x, 1 - c)))
-    order = [k for k in range(1, outer_n)]
-    order.sort(key=lambda k: -min(k, outer_n - k))
-    order = order + [0]
-
-    def grad_rows(outer, inner, part):
-        return _rows((outer * 2 + inner) * block + part * bsize, bsize)
-
-    for part in range(wparts):
-        for k in order:
-            at = pl.ds(part * bsize, bsize)
-            go(_remote(grads.at[grad_rows((z + k) % outer_n, 1 - y, part), :], in_buf.at[k, at, :],
-                       in_sem.at[0, k, part], in_sem.at[1, k, part], _peer(z, 1 - y, x, c)))
+    size = own_rows // PARTS
+    half = own_rows // 2
+    per_group = next(g for g in range(1, outer_n + 1) if (2 * g * block) % LANES == 0)
+    groups = outer_n // per_group
+    loads = [pltpu.make_async_copy(src, dst, load_sem.at[i]) for i, (src, dst) in enumerate(
+        [(dz_in, dz), (rest_in, rest), (weight_in, weight), (normed_in, normed), (resid_in, resid)])]
+    for copy in loads:
+        copy.start()
+    _greet(outer_n)
+    dp_peers = [(k, j) for k in range(outer_n) for j in (0, 1) if k or j]
+    tensor_peers = [(k, j) for k in (0, 1) for j in (0, 1) if k or j]
+
+    def dp_copies(src, dst, sem):
+        return [_remote(src, dst.at[k * 2 + j], sem.at[0, i], sem.at[1, i],
+                        _peer((z + k) % outer_n, (y + j) % 2, x, c)) for i, (k, j) in enumerate(dp_peers)]
+
+    def tensor_copies(src, dst, sem):
+        return [_remote(src, dst.at[k * 2 + j], sem.at[0, i], sem.at[1, i],
+                        _peer(z, y, (x + k) % 2, (c + j) % 2)) for i, (k, j) in enumerate(tensor_peers)]
+
+    def dp_total(buf):
+        total = None
+        for zz in range(outer_n):
+            for yy in (0, 1):
+                term = buf[lax.rem(z - zz + outer_n, outer_n) * 2 + lax.rem(y - yy + 2, 2)]
+                total = term if total is None else total + term
+        return total
+
+    def near_copy(i, part):
+        at = pl.ds(part * size, size)
+        return _remote(tok.at[2 * i, at, :], near_buf.at[i, at, :], near_sem.at[0, i, part], near_sem.at[1, i, part],
+                       _peer(z, y, x, 1 - c))
+
+    def far_copy(part):
+        at = pl.ds(part * size, size)
+        return _remote(far_src.at[at, :], far_buf.at[at, :], far_sem.at[0, part], far_sem.at[1, part],
+                       _peer(z, y, 1 - x, c))
+
+    def in_copy(k, zz, part):
+        at = pl.ds(part * bsize, bsize)
+        return _remote(g_all.at[zz, 1 - y, at, :], in_buf.at[k, at, :], in_sem.at[0, k, part], in_sem.at[1, k, part],
+                       _peer(z, 1 - y, x, c))
+
+    def out_copy(k, part):
+        at = pl.ds(part * bsize, bsize)
+        return _remote(out_src.at[k - 1, at, :], out_buf.at[k - 1, at, :], out_sem.at[0, k - 1, part],
+                       out_sem.at[1, k - 1, part], _peer((z + k) % outer_n, y, x, c))
+
+    def token_product(i, part):
+        far, near = ((1 - x, 1 - c), (1 - x, c), (x, 1 - c), (x, c))[i]
+        rows = pl.ds(pl.multiple_of((far * 2 + near) * own_rows + part * half, LANES), half)
+        value = _dot_last(dz[rows, :], weight[:, :width]) + _dot_last(rest[rows, :], weight[:, width:])
+        at = pl.ds(pl.multiple_of(part * half, LANES), half)
+        if i < 3:
+            tok[i, at, :] = value.astype(BF)
+        else:
+            d_local[at, :] = value
+
+    def group(i):
+        grp = lax.rem(z // per_group + 1 + i, groups)
+        at = pl.ds(pl.multiple_of(grp * (2 * per_group * block), LANES), 2 * per_group * block)
+        value = lax.dot_general(normed[:, at], rest[...], (((0,), (0,)), ((), ())), preferred_element_type=F32)
+        for j in range(per_group):
+            zz = grp * per_group + j
+            for yy in (0, 1):
+                first = (2 * j + yy) * block
+                g_all[zz, yy] = value[first : first + block, :].astype(BF)
+            k = lax.rem(zz - z + outer_n, outer_n)
+            for part in range(wparts):
+                in_copy(k, zz, part).start()
 
     def token_step(part):
         at = pl.ds(part * size, size)
-        view = near_buf.at[0, at, :]
-        _remote(view, view, near_sem.at[0, 0, part], near_sem.at[1, 0, part], me).wait_recv()
-        far_src[at, :] = (partial[token_rows(1 - x, c, part), :].astype(F32) + view[...].astype(F32)).astype(BF)
-        go(_remote(far_src.at[at, :], far_buf.at[at, :], far_sem.at[0, part], far_sem.at[1, part],
-                   _peer(z, y, 1 - x, c)))
-
-    def grad_step(part):
+        near_copy(0, part).wait_recv()
+        far_src[at, :] = (tok[1, at, :].astype(F32) + near_buf[0, at, :].astype(F32)).astype(BF)
+        far_copy(part).start()
+
+    def grad_step(k, part):
         at = pl.ds(part * bsize, bsize)
-        for k in order:
-            view = in_buf.at[k, at, :]
-            _remote(view, view, in_sem.at[0, k, part], in_sem.at[1, k, part], me).wait_recv()
-            both = grads[grad_rows((z + k) % outer_n, y, part), :].astype(F32) + view[...].astype(F32)
-            if k:
-                out_src[k - 1, at, :] = both.astype(BF)
-                go(_remote(out_src.at[k - 1, at, :], out_buf.at[k - 1, at, :], out_sem.at[0, k - 1, part],
-                           out_sem.at[1, k - 1, part], _peer((z + k) % outer_n, y, x, c)))
-            else:
-                owned[at, :] = both
-
-    for part in range(max(PARTS, wparts)):
-        if part < PARTS:
-            token_step(part)
-        if part < wparts:
-            grad_step(part)
-
+        zz = lax.rem(z + k, outer_n)
+        in_copy(k, zz, part).wait_recv()
+        both = g_all[zz, y, at, :].astype(F32) + in_buf[k, at, :].astype(F32)
+        if k:
+            out_src[k - 1, at, :] = both.astype(BF)
+            out_copy(k, part).start()
+        else:
+            owned[at, :] = both
+
+    small_d[0] = small[...]
+    first = dp_copies(small, small_d, small_sem_d)
+    for copy in first:
+        copy.start()
+    for copy in loads[:3]:
+        copy.wait()
+    parts_half = PARTS // 2
+
+    @pl.loop(0, 2)
+    def _(part):
+        token_product(0, part)
+
+    for part in range(PARTS):
+        near_copy(0, part).start()
+    loads[3].wait()
+    group(0)
+
+    @pl.loop(0, 2)
+    def _(part):
+        token_product(1, part)
+
+    for part in range(PARTS):
+        token_step(part)
+
+    @pl.loop(1, groups)
+    def _(i):
+        group(i)
+
+    order = list(range(1, outer_n)) + [0]
+    todo = [(k, part) for k in order for part in range(wparts)]
+    quarter = -(-len(todo) // 4)
+    for k, part in todo[:quarter]:
+        grad_step(k, part)
+
+    @pl.loop(0, 2)
+    def _(part):
+        token_product(2, part)
+
+    for part in range(PARTS):
+        near_copy(1, part).start()
+    for copy in first:
+        copy.wait_recv()
+    total = dp_total(small_d)
+    small_out[...] = total
+    small_t[0] = total[:both_rows, :]
+    second = tensor_copies(small_t.at[0], small_t, small_sem_t)
+    for copy in second:
+        copy.start()
+    for k, part in todo[quarter : 2 * quarter]:
+        grad_step(k, part)
+
+    @pl.loop(0, 2)
+    def _(part):
+        token_product(3, part)
+
+    for k, part in todo[2 * quarter : 3 * quarter]:
+        grad_step(k, part)
+    loads[4].wait()
     gain_acc[...] = jnp.zeros_like(gain_acc)
     for part in range(PARTS):
         at = pl.ds(part * size, size)
-        view, last = near_buf.at[1, at, :], far_buf.at[at, :]
-        _remote(view, view, near_sem.at[0, 1, part], near_sem.at[1, 1, part], me).wait_recv()
-        _remote(last, last, far_sem.at[0, part], far_sem.at[1, part], me).wait_recv()
-        got = partial[token_rows(x, c, part), :].astype(F32) + view[...].astype(F32) + last[...].astype(F32)
+        near_copy(1, part).wait_recv()
+        far_copy(part).wait_recv()
+        got = d_local[at, :] + near_buf[1, at, :].astype(F32) + far_buf[at, :].astype(F32)
         d_local[at, :] = got
         values = resid[at, :]
         inv = lax.rsqrt(jnp.mean(values * values, axis=-1, keepdims=True) + EPSILON)
         gain_acc[...] += _rows_sum(got * values * inv)
-
-    small_d[0] = small[...]
-    for j in range(model // LANES):
-        small_d[0, j : j + 1, :] = jnp.sum(gain_acc[:, j * LANES : (j + 1) * LANES], axis=0, keepdims=True)
-    first = []
-    i = 0
-    for k in range(outer_n):
-        for j in (0, 1):
-            if k or j:
-                peer = _peer((z + k) % outer_n, (y + j) % 2, x, c)
-                first.append(go(_remote(small_d.at[0], small_d.at[k * 2 + j], small_sem_d.at[0, i],
-                                        small_sem_d.at[1, i], peer)))
-                i += 1
+    for j in range(gain_rows):
+        gain_d[0, j : j + 1, :] = jnp.sum(gain_acc[:, j * LANES : (j + 1) * LANES], axis=0, keepdims=True)
+    gain_first = dp_copies(gain_d.at[0], gain_d, gain_sem_d)
+    for copy in gain_first:
+        copy.start()
+    for k, part in todo[3 * quarter :]:
+        grad_step(k, part)
     for part in range(wparts):
         at = pl.ds(part * bsize, bsize)
         total = owned[at, :]
         for k in order[:-1]:
-            view = out_buf.at[k - 1, at, :]
-            _remote(view, view, out_sem.at[0, k - 1, part], out_sem.at[1, k - 1, part], me).wait_recv()
-            total = total + view[...].astype(F32)
+            out_copy(k, part).wait_recv()
+            total = total + out_buf[k - 1, at, :].astype(F32)
         owned[at, :] = total
-    for copy in first:
+    bc_rows = block // 4
+    for i in range(4):
+        bc_src[i] = owned[i * bc_rows : (i + 1) * bc_rows, width : width + 2 * LANES]
+    bc_copies = []
+    for i, (k, j) in enumerate(tensor_peers):
+        other = lax.rem(x + k, 2) * 2 + lax.rem(c + j, 2)
+        bc_copies.append(_remote(bc_src.at[other], bc_buf.at[i], bc_sem.at[0, i], bc_sem.at[1, i],
+                                 _peer(z, y, (x + k) % 2, (c + j) % 2)))
+    for copy in bc_copies:
+        copy.start()
+    for copy in gain_first:
         copy.wait_recv()
-    total = None
-    for zz in range(outer_n):
-        for yy in (0, 1):
-            slot = ((z - zz) % outer_n) * 2 + (y - yy) % 2
-            term = small_d[slot]
-            total = term if total is None else total + term
-    small_out[...] = total
-    small_t[0] = total[:small_rows_both, :]
-    second = []
-    i = 0
-    for k in (0, 1):
-        for j in (0, 1):
-            if k or j:
-                peer = _peer(z, y, (x + k) % 2, (c + j) % 2)
-                second.append(go(_remote(small_t.at[0], small_t.at[k * 2 + j], small_sem_t.at[0, i],
-                                         small_sem_t.at[1, i], peer)))
-                i += 1
+    total = dp_total(gain_d)
+    gain_t[0] = total
+    gain_second = tensor_copies(gain_t.at[0], gain_t, gain_sem_t)
+    for copy in gain_second:
+        copy.start()
     for copy in second:
         copy.wait_recv()
-    small_out[0:small_rows_both, :] = (small_t[0] + small_t[1]) + (small_t[2] + small_t[3])
-    for copy in started:
+    small_out[0:both_rows, :] = (small_t[0] + small_t[1]) + (small_t[2] + small_t[3])
+    for copy in bc_copies:
+        copy.wait_recv()
+    bc_out[...] = (bc_src[t] + bc_buf[0]) + (bc_buf[1] + bc_buf[2])
+    for copy in gain_second:
+        copy.wait_recv()
+    gains = (gain_t[0] + gain_t[1]) + (gain_t[2] + gain_t[3])
+    small_out[0:gain_rows, :] = gains[:gain_rows, :]
+    for part in range(PARTS):
+        near_copy(0, part).wait_send()
+        near_copy(1, part).wait_send()
+        far_copy(part).wait_send()
+    for k in range(outer_n):
+        zz = lax.rem(z + k, outer_n)
+        for part in range(wparts):
+            in_copy(k, zz, part).wait_send()
+            if k:
+                out_copy(k, part).wait_send()
+    for copy in first + second + gain_first + gain_second + bc_copies:
         copy.wait_send()
 
 
-def reduce_all(partial, grads, small, resid, gain_rows, both_rows):
+def final_sums(dz, rest, weight, normed, resid, small, both_rows):
     dp, tp = lax.axis_size("dp"), lax.axis_size("tensor")
     outer_n = dp // 2
     own_rows, model = resid.shape
-    block, cols = grads.shape[0] // dp, grads.shape[1]
+    block, cols = model // dp, rest.shape[1]
+    gain_rows = model // LANES
+    gain_pad = -(-gain_rows // 8) * 8
+    wparts = _parts(block)
     vm = pl.BlockSpec(memory_space=pltpu.VMEM)
+    hbm = pl.BlockSpec(memory_space=pl.ANY)
     dma = pltpu.SemaphoreType.DMA
+    tokens = (own_rows, model)
+    bc = (4, block // 4, 2 * LANES)
     return pl.pallas_call(
-        functools.partial(reduce_kernel, outer_n, both_rows),
-        in_specs=[vm] * 5,
-        out_specs=[vm] * 3,
-        out_shape=[jax.ShapeDtypeStruct((own_rows, model), F32),
+        functools.partial(final_kernel, outer_n, both_rows, gain_rows),
+        in_specs=[hbm] * 5 + [vm],
+        out_specs=[vm] * 4,
+        out_shape=[jax.ShapeDtypeStruct(tokens, F32),
                    jax.ShapeDtypeStruct((block, cols), F32),
-                   jax.ShapeDtypeStruct(small.shape, F32)],
-        scratch_shapes=[pltpu.VMEM((2, own_rows, model), BF),
-                        pltpu.VMEM((own_rows, model), BF),
-                        pltpu.VMEM((own_rows, model), BF),
+                   jax.ShapeDtypeStruct(small.shape, F32),
+                   jax.ShapeDtypeStruct(bc[1:], F32)],
+        scratch_shapes=[pltpu.VMEM(dz.shape, BF), pltpu.VMEM(rest.shape, BF), pltpu.VMEM(weight.shape, BF),
+                        pltpu.VMEM(normed.shape, BF), pltpu.VMEM(tokens, F32),
+                        pltpu.VMEM((outer_n, 2, block, cols), BF),
+                        pltpu.VMEM((3,) + tokens, BF), pltpu.VMEM((2,) + tokens, BF),
+                        pltpu.VMEM(tokens, BF), pltpu.VMEM(tokens, BF),
                         pltpu.VMEM((outer_n, block, cols), BF),
-                        pltpu.VMEM((outer_n - 1, block, cols), BF),
-                        pltpu.VMEM((outer_n - 1, block, cols), BF),
-                        pltpu.VMEM((dp,) + small.shape, F32),
-                        pltpu.VMEM((4, both_rows, LANES), F32),
-                        pltpu.VMEM((8, model), F32),
-                        dma((2, 2, PARTS)), dma((2, PARTS)), dma((2, outer_n, _parts(block))),
-                        dma((2, outer_n - 1, _parts(block))), dma((2, dp - 1)), dma((2, 3))],
-        compiler_params=pltpu.CompilerParams(collective_id=1, has_side_effects=True,
-                                             vmem_limit_bytes=62 * 2**20),
-        cost_estimate=pl.CostEstimate(flops=10**7, bytes_accessed=40 * 2**20, transcendentals=0),
-        name="reduce_all",
-    )(partial, grads, small, resid, gain_rows)
+                        pltpu.VMEM((outer_n - 1, block, cols), BF), pltpu.VMEM((outer_n - 1, block, cols), BF),
+                        pltpu.VMEM((dp,) + small.shape, F32), pltpu.VMEM((4, both_rows, LANES), F32),
+                        pltpu.VMEM((dp, gain_pad, LANES), F32), pltpu.VMEM((4, gain_pad, LANES), F32),
+                        pltpu.VMEM((8, model), F32), pltpu.VMEM(bc, F32), pltpu.VMEM((3,) + bc[1:], F32),
+                        dma((5,)), dma((2, 2, PARTS)), dma((2, PARTS)), dma((2, outer_n, wparts)),
+                        dma((2, outer_n - 1, wparts)), dma((2, dp - 1)), dma((2, 3)), dma((2, dp - 1)), dma((2, 3)),
+                        dma((2, 3))],
+        compiler_params=pltpu.CompilerParams(collective_id=1, has_side_effects=True, vmem_limit_bytes=63 * 2**20),
+        cost_estimate=pl.CostEstimate(flops=20 * 10**9, bytes_accessed=40 * 2**20, transcendentals=0),
+        name="final_sums",
+    )(dz, rest, weight, normed, resid, small)
 
 
 def _spread(values, index, count):
@@ -1038,14 +1217,11 @@
     gain_rows = model // LANES
     both_rows = -(-small.shape[0] // 8) * 8
     small = pad_rows(small, both_rows)
-    dt_cols = jnp.pad(proj_dt, ((0, 0), (0, LANES - heads)))
-    small_all, normed, cot_full, weight, out_t = gather_all(
-        small, resid, cot, proj_zx.reshape(rows, 2 * width), dt_cols, proj_bc, proj_out.T)
+    small_all, normed, cot_full, weight, out_t, proj, d_gated = gather_all(
+        small, resid, cot, proj_zx.reshape(rows, 2 * width), proj_dt, proj_bc, proj_out.T)
     full_cbw = small_all[gain_rows : gain_rows + 4 * states2 // LANES].reshape(4, states2)
     full_cbb = small_all[gain_rows + 4 * states2 // LANES : gain_rows + 5 * states2 // LANES].reshape(states2)
     full_gain = small_all[:gain_rows].reshape(model)
-    proj = jnp.dot(normed, weight, preferred_element_type=F32)
-    d_gated = jnp.dot(cot_full, out_t, preferred_element_type=F32)
     packs = pack_params(conv_x_weight, conv_x_bias, full_cbw, full_cbb, dt_bias, a_log, skip_gain, gate_gain)
     y, states, partial = ssd_forward(proj, d_gated, *packs)
     dy, dz, out_partial, grads_zo, ggain = middle(proj, y, d_gated, partial, packs[3], normed, cot_full, out_t, inner_channels)
@@ -1053,21 +1229,16 @@
     block_out = resid + block_sum
     gx = jnp.concatenate([gx.sum(1), ggain.sum(0)[None]], 0)
     gbc, gh = gbc.sum(1), gh.sum(1)
-    d_proj = jnp.concatenate([dz, d_rest], axis=1)
-    d_normed = lax.dot_general(d_proj, weight, (((1,), (1,)), ((), ())), preferred_element_type=F32).astype(BF)
-    grads = lax.dot_general(normed, d_rest, (((0,), (0,)), ((), ())), preferred_element_type=F32).astype(BF)
     to_sum = jnp.concatenate([
         pad_rows(jnp.concatenate([jnp.zeros((gain_rows, LANES), F32), gbc.reshape(-1, LANES)], 0), both_rows),
         gx.reshape(-1, LANES), gh], axis=0)
     to_sum = pad_rows(to_sum, -(-to_sum.shape[0] // 8) * 8)
-    d_local, owned, totals = reduce_all(d_normed, grads, to_sum, resid, small_all, both_rows)
+    d_local, owned, totals, grad_bc = final_sums(dz, d_rest, weight, normed, resid, to_sum, both_rows)
     inv_in = lax.rsqrt(jnp.mean(resid * resid, axis=-1, keepdims=True) + EPSILON)
     scaled = resid * inv_in
     d_scaled = d_local * full_gain
     grad_resid = inv_in * (d_scaled - scaled * jnp.mean(d_scaled * scaled, axis=-1, keepdims=True)) + cot
     grad_zx = jnp.stack([owned_zo[:, :width], owned[:, :width]], axis=1)
-    bc_part = owned[:, width : width + states2]
-    grad_bc = lax.psum_scatter(bc_part.astype(BF), "tensor", scatter_dimension=0, tiled=True).astype(F32)
     grad_dt = owned[:, width + states2 : width + states2 + heads]
     owned_out = owned_zo[:, width:].T
     owned_gain = _own(totals[:gain_rows].reshape(model), index, count)

time: 439 us -> 366 us (0.83)
  matrix products: 57.3 us -> 0 us
  between operations: 14.8 us -> 1.22 us
    dot_general x4 -> x0, matrix products: 57.3 us -> none  [the longest x1 19.4 us: on_device(): proj = jnp.dot(normed, weight, preferred_element_type=F32)]
    pallas_call x2, Pallas kernels: 183 us -> 191 us  [the longest x1 123 us: gather_all(): pl.pallas_call(functools.partial(gather_kernel, outer_n, heads), in_specs...]
    pallas_call x1, Pallas kernels: 73.1 us -> 67.5 us  [ssd_backward(): pl.pallas_call(functools.partial(backward_kernel, width, dp // 2), grid=(...]
  transfers between devices with their start and end apart: 1 -> 0, of which waited for: 0 -> 0; matrix products, arithmetic and copies ran while one was open for 5% -> 0% of each run, Pallas kernels for 0% -> 0%
where the time goes in v2:
time: 366 us; the launch traced here: 359 us
  Pallas kernels  323 us (88%)
  other arithmetic  18.1 us (5%)
  local copies, waits for them, and re-layouts  16.1 us (4%)
    pallas_call x1, Pallas kernels, gather_all(): pl.pallas_call(functools.partial(gather_kernel, outer_n, heads), in_specs...  123 us
    pallas_call x1, Pallas kernels, final_sums(): pl.pallas_call(functools.partial(final_kernel, outer_n, both_rows, gain_r...  68.4 us
    pallas_call x1, Pallas kernels, ssd_backward(): pl.pallas_call(functools.partial(backward_kernel, width, dp // 2), grid=(...  67.5 us
    pallas_call x1, Pallas kernels, ssd_forward(): pl.pallas_call(functools.partial(forward_kernel, width), grid=(length //...  34.7 us
    pallas_call x1, Pallas kernels, middle(): pl.pallas_call(functools.partial(middle_kernel, width, inner_channels), g...  29.9 us

profile of v2, /device:TPU:0, one launch (start us, length us, event | category | flops | bytes accessed | tf_op | source)
XLA Modules:
  0.0 358.8 jit_solution(18385841829495977878)
XLA Ops:
  0.8 0.9 dynamic_update_slice.11
  1.7 2.2 multiply_reduce_fusion.1
  3.9 0.6 select_maximum_fusion.6.head_ref
  4.7 0.6 pad.33.wdt
  5.7 0.6 select_maximum_fusion.3.small
  6.3 0.6 select_maximum_fusion.1
  6.9 0.9 copy.32
  7.8 122.9 %gather_all.1 = (f32[24,128]{1,0:T(8,128)}, bf16[2048,1536]{1,0:T(8,128)(2,1)}, bf16[2048,1536]{1,0:T(8,128)(2,1)}, bf16[1536,1920]{1,0:T(8,128)(2,1)}, bf16[153...) custom-call(f32[24,128]{1,0:T(8,128)} %select_maximum_fusion.3.small, bf16[192,1536]{1,0:T(8,128)(2,1)} %bitcast.44, ...), custom_call_target="tpu_custom_call" | custom-call | flops 16999999488 | bytes 62914560 | tf_op jit(solution)/shard_map/gather_all/pallas_call | solution.py:902
  130.7 0.7 slice.63
  131.4 0.7 slice.62
  132.1 0.7 slice_bitcast_fusion.4
  132.8 0.6 select_maximum_fusion.5.convbc_ref
  133.4 34.7 %scan_forward.1 = (f32[2048,768]{1,0:T(8,128)}, f32[16,128,768]{2,1,0:T(8,128)}, f32[32,128]{1,0:T(8,128)}) custom-call(f32[2048,1920]{1,0:T(8,128)} %get-tuple-element.40.p_ref.z_ref.prev_ref, f32[2048,768]{1,0:T(8,128)} %get-tuple-element.41.dg_ref, f32[8,768]{1,0:T(8,128)} %get-tuple-element.90.convx_ref, f32[8,256]{1,0:T(8,128)} %select_maximum_fusion.5.convbc_ref, ...), custom_call_target="tpu_custom_call" | custom-call | flops 4000000000 | bytes 31457280 | tf_op jit(solution)/shard_map/scan_forward/pallas_call | solution.py:512
  168.1 29.9 %middle.1 = (bf16[2048,768]{1,0:T(8,128)(2,1)}, bf16[2048,768]{1,0:T(8,128)(2,1)}, bf16[2048,1536]{1,0:T(8,128)(2,1)}, bf16[1536,1536]{1,0:T(8,128)(2,1)}, f32[8,768]{1,0:T(8,128)}) custom-call(f32[2048,1920]{1,0:T(8,128)} %get-tuple-element.40.p_ref.z_ref.prev_ref, f32[2048,768]{1,0:T(8,128)} %get-tuple-element.43.y_ref, ...), custom_call_target="tpu_custom_call" | custom-call | flops 15000000512 | bytes 52428800 | tf_op jit(solution)/shard_map/middle/pallas_call | solution.py:626
  198.1 67.5 %scan_backward.1 = (bf16[2048,1152]{1,0:T(8,128)(2,1)}, f32[6,8,768]{2,1,0:T(8,128)}, f32[5,8,256]{2,1,0:T(8,128)}, f32[2,8,128]{2,1,0:T(8,128)}, f32[512,1536]{1,0:T(8,128)}, /*index=5*/f32[192,1536]{1,0:T(8,128)}) custom-call(f32[2048,1920]{1,0:T(8,128)} %get-tuple-element.40.p_ref.z_ref.prev_ref, f32[2048,1920]{1,0:T(8,128)} %get-tuple-element.40.p_ref.z_ref.prev_ref, ...), custom_call_target="tpu_custom_call" | custom-call | flops 12000000000 | bytes 52428800 | tf_op jit(solution)/shard_map/scan_backward/pallas_call | solution.py:547
  265.6 0.7 reduce_sum.67
  266.3 0.8 reduce_sum.64
  267.1 1.0 reduce_sum.65
  268.1 0.6 pad.39.small
  268.7 68.4 %final_sums.1 = (f32[512,1536]{1,0:T(8,128)}, f32[192,1152]{1,0:T(8,128)}, f32[72,128]{1,0:T(8,128)}, f32[48,256]{1,0:T(8,128)}) custom-call(bf16[2048,768]{1,0:T(8,128)(2,1)} %get-tuple-element.53.dz_in, bf16[2048,1152]{1,0:T(8,128)(2,1)} %get-tuple-element.54.rest_in, bf16[1536,1920]{1,0:T(8,128)(2,1)} %get-tuple-element.55.weight_in, ...), custom_call_target="tpu_custom_call" | custom-call | flops 20000000000 | bytes 41943040 | tf_op jit(solution)/shard_map/final_sums/pallas_call | solution.py:1161
  337.1 0.7 slice_bitcast_fusion.7
  338.4 1.3 slice_bitcast_fusion.8
  339.7 3.5 multiply_reduce_fusion
  343.4 1.0 copy-done.1
  344.4 6.7 %add_bitcast_fusion = (f32[1,512,1536]{2,1,0:T(8,128)}, f32[1,512,1536]{2,1,0:T(8,128)}) fusion(f32[512,1536]{1,0:T(8,128)S(1)} %copy-done.1, f32[512]{0:T(512)S(1)} %broadcast_multiply_fusion, f32[1536]{0:T(1024)S(1)} %slice_bitcast_fusion.4, f32[512]{0:T(512)S(1)} %add_rsqrt_fusion, f32[1,512,1536]{2,1,0:T(8,128)} %param.29, f32[1,512,1536]{2,1,0:T(8,128)S(1)} %copy-done, ...), kind=kLoop, calls=%fused_computation | loop fusion | flops 5505024 | bytes 18884608 | tf_op jit(solution)/shard_map/broadcast_in_dim | solution.py:1252
  351.1 0.7 constant_dynamic-slice_fusion
  352.9 0.6 slice.70
  353.6 0.6 reduce_sum.69
  354.3 0.7 copy.31
  355.0 0.9 slice_bitcast_fusion
  356.0 1.9 copy.30
  357.9 0.6 copy.37
  (63 shorter events, 2.8 us)
Async XLA Ops:
  0.6 3.2 copy-start.11
  0.7 4.6 %copy-start.15 = (f32[12]{0:T(128)S(1)}, f32[12]{0:T(128)}, u32[]{:S(2)}) copy-start(f32[12]{0:T(128)} %param.26) | copy-start | bytes 148
  0.7 3.2 copy-start.13
  0.7 3.2 copy-start.14
  0.7 3.8 %copy-start.12 = (f32[4,8]{1,0:T(4,128)S(1)}, f32[4,8]{1,0:T(4,128)}, u32[]{:S(2)}) copy-start(f32[4,8]{1,0:T(4,128)} %param.22) | copy-start | bytes 388
  0.7 3.2 copy-start.10
  0.7 5.6 %copy-start.8 = (f32[4,768]{1,0:T(4,128)S(1)}, f32[4,768]{1,0:T(4,128)}, u32[]{:S(2)}) copy-start(f32[4,768]{1,0:T(4,128)} %param.20) | copy-start | bytes 36868
  0.7 3.9 %copy-start.9 = (bf16[192,12]{0,1:T(8,128)(2,1)S(1)}, bf16[192,12]{0,1:T(8,128)(2,1)}, u32[]{:S(2)}) copy-start(bf16[192,12]{0,1:T(8,128)(2,1)} %param.18) | copy-start | bytes 13828
  0.7 6.2 %copy-start.3 = (bf16[192,2,768]{2,1,0:T(2,128)(2,1)S(1)}, bf16[192,2,768]{2,1,0:T(2,128)(2,1)}, u32[]{:S(2)}) copy-start(bf16[192,2,768]{2,1,0:T(2,128)(2,1)} %param.17) | copy-start | bytes 1769476
  0.7 4.7 %copy-start.16 = (f32[48]{0:T(128)S(1)}, f32[48]{0:T(128)}, u32[]{:S(2)}) copy-start(f32[48]{0:T(128)} %param.16) | copy-start | bytes 580
  198.1 68.2 %copy-start.7 = (f32[8,768]{1,0:T(8,128)S(1)}, f32[8,768]{1,0:T(8,128)}, u32[]{:S(2)}) copy-start(f32[8,768]{1,0:T(8,128)} %get-tuple-element.58) | copy-start | bytes 73732
  339.7 3.7 %copy-start = (f32[1,512,1536]{2,1,0:T(8,128)S(1)}, f32[1,512,1536]{2,1,0:T(8,128)}, u32[]{:S(2)}) copy-start(f32[1,512,1536]{2,1,0:T(8,128)} %param.15) | copy-start | bytes 9437188
  339.7 4.7 %copy-start.1 = (f32[512,1536]{1,0:T(8,128)S(1)}, f32[512,1536]{1,0:T(8,128)}, u32[]{:S(2)}) copy-start(f32[512,1536]{1,0:T(8,128)} %get-tuple-element.60) | copy-start | bytes 9437188
  344.4 6.7 %copy-start.6 = (f32[72,128]{1,0:T(8,128)S(1)}, f32[72,128]{1,0:T(8,128)}, u32[]{:S(2)}) copy-start(f32[72,128]{1,0:T(8,128)} %get-tuple-element.61) | copy-start | bytes 110596
  344.4 9.9 %copy-start.4 = (f32[192,1152]{1,0:T(8,128)S(1)}, f32[192,1152]{1,0:T(8,128)}, u32[]{:S(2)}) copy-start(f32[192,1152]{1,0:T(8,128)} %get-tuple-element.63) | copy-start | bytes 2654212
  344.4 10.6 %copy-start.2 = (f32[192,1536]{1,0:T(8,128)S(1)}, f32[192,1536]{1,0:T(8,128)}, u32[]{:S(2)}) copy-start(f32[192,1536]{1,0:T(8,128)} %get-tuple-element.62) | copy-start | bytes 3538948
  355.0 2.9 copy-start.5

commit v3 on v2

--- a/solution.py
+++ b/solution.py
@@ -59,7 +59,7 @@
 
 
 class _Reduction:
-    def __init__(self, outer_n, partial, grads, block_sum, owned, own_tokens, near_buf, far_src, far_buf,
+    def __init__(self, outer_n, partial, grads, resid, block_sum, owned, resid_buf, own_tokens, near_buf, far_src, far_buf,
                  own_grads, in_buf, out_src, out_buf, near_sem, far_sem, in_sem, out_sem, local_sem):
         self.__dict__.update(locals())
         self.z, self.y, self.x, self.c = _place()
@@ -103,7 +103,7 @@
                        self.out_sem.at[1, k - 1, part], _peer((self.z + k) % self.outer_n, self.y, self.x, self.c))
 
     def local_copies(self):
-        copies = []
+        copies = [pltpu.make_async_copy(self.resid, self.resid_buf, self.local_sem.at[2 + self.outer_n])]
         for i, far in enumerate((1 - self.x, self.x)):
             rows = _rows((far * 2 + self.c) * self.own_rows, self.own_rows)
             copies.append(pltpu.make_async_copy(self.partial.at[rows, :], self.own_tokens.at[i], self.local_sem.at[i]))
@@ -166,7 +166,7 @@
             self.near_copy(1, part).wait_recv()
             self.far_copy(part).wait_recv()
             self.block_sum[at, :] = (self.own_tokens[1, at, :].astype(F32) + self.near_buf[1, at, :].astype(F32)
-                                     + self.far_buf[at, :].astype(F32))
+                                     + self.far_buf[at, :].astype(F32)) + self.resid_buf[at, :]
         for part in range(self.wparts):
             at = pl.ds(part * self.bsize, self.bsize)
             total = self.owned[at, :]
@@ -188,15 +188,15 @@
 def reduction_scratch(outer_n, tokens, grads):
     dma = pltpu.SemaphoreType.DMA
     parts = _parts(grads[0])
-    return [pltpu.VMEM((2,) + tokens, BF), pltpu.VMEM((2,) + tokens, BF), pltpu.VMEM(tokens, BF),
+    return [pltpu.VMEM(tokens, F32), pltpu.VMEM((2,) + tokens, BF), pltpu.VMEM((2,) + tokens, BF), pltpu.VMEM(tokens, BF),
             pltpu.VMEM(tokens, BF), pltpu.VMEM((outer_n,) + grads, BF), pltpu.VMEM((outer_n,) + grads, BF),
             pltpu.VMEM((outer_n - 1,) + grads, BF), pltpu.VMEM((outer_n - 1,) + grads, BF),
             dma((2, 2, PARTS)), dma((2, PARTS)), dma((2, outer_n, parts)), dma((2, outer_n - 1, parts)),
-            dma((2 + outer_n,))]
+            dma((3 + outer_n,))]
 
 
 def _sigmoid(v):
-    return 1.0 / (1.0 + jnp.exp(-v))
+    return 0.5 * jnp.tanh(0.5 * v) + 0.5
 
 
 def _softplus(t):
@@ -241,20 +241,38 @@
     return t, delta, rate, cum
 
 
-def _pair_cols(lo, v, q):
-    return jnp.where(lo, v[:, 2 * q : 2 * q + 1], v[:, 2 * q + 1 : 2 * q + 2])
-
-
 def _conv(buf, start, cols, w, length):
-    shifted = [buf[start + k : start + k + length, cols] for k in range(TAPS)]
+    ahead = buf[start : start + 8 + length, cols]
+    shifted = [pltpu.roll(ahead, TAPS - 1 - k, 0)[8:] for k in range(TAPS - 1)] + [ahead[8:]]
     v = w[TAPS : TAPS + 1, :] + w[0:1, :] * shifted[0]
     for k in range(1, TAPS):
         v = v + w[k : k + 1, :] * shifted[k]
     return v, shifted
 
 
+def _conv_back(dv, after, w):
+    behind = jnp.concatenate([dv, after], axis=0)
+    length = dv.shape[0]
+    total = w[TAPS - 1 : TAPS, :] * dv
+    for k in range(TAPS - 1):
+        total = total + w[k : k + 1, :] * pltpu.roll(behind, length + 8 - (TAPS - 1 - k), 0)[:length]
+    return total
+
+
+def _fill_spread(spread, head_width):
+    shape = spread.shape
+    head = lax.broadcasted_iota(jnp.int32, shape, 0) % LANES
+    lane = lax.broadcasted_iota(jnp.int32, shape, 1)
+    spread[...] = (lane // head_width == head).astype(F32).astype(BF)
+
+
+def _widen(wide, delta, tail, grow, spread):
+    high, low = _halves(jnp.concatenate([delta, tail, grow], axis=0))
+    wide[...] = jnp.dot(jnp.concatenate([high, low], axis=1), spread[...], preferred_element_type=F32)
+
+
 def forward_kernel(width, p_ref, dg_ref, convx_ref, convbc_ref, head_ref, lane_ref,
-                   y_ref, h_ref, s_ref, state, xbuf, bcbuf, sums, sum_sem):
+                   y_ref, h_ref, s_ref, state, xbuf, bcbuf, spread, wide, sums, sum_sem):
     tokens = p_ref.shape[0]
     pairs = width // LANES
     step = pl.program_id(0)
@@ -270,6 +288,7 @@
             pl.semaphore_signal(barrier, inc=1, device_id=peer, device_id_type=MESH)
         pl.semaphore_wait(barrier, len(tensor_peers))
         state[...] = jnp.zeros_like(state)
+        _fill_spread(spread, LANES // 2)
         xbuf[0:8, :] = jnp.zeros((8, width), F32)
         bcbuf[0:8, :] = jnp.zeros((8, 2 * LANES), F32)
 
@@ -288,7 +307,7 @@
     for sub in range(tokens // CHUNK):
         base = sub * CHUNK
         span = slice(base, base + CHUNK)
-        vbc, _ = _conv(bcbuf, base + 5, slice(0, 2 * LANES), convbc_ref[...], CHUNK)
+        vbc, _ = _conv(bcbuf, base, slice(0, 2 * LANES), convbc_ref[...], CHUNK)
         bc = vbc * _sigmoid(vbc)
         b_in, c_out = bc[:, :LANES], bc[:, LANES:]
         c_high, c_low = _halves(c_out)
@@ -299,16 +318,16 @@
         last = cum[CHUNK - 1 : CHUNK, :]
         tail = jnp.exp2(last - cum)
         grow = jnp.exp2(cum)
-        decay = jnp.exp2(last)
+        _widen(wide, delta, tail, grow, spread)
         b_t = b_in.T.astype(BF)
         squares = jnp.zeros((CHUNK, LANES), F32)
         inner = jnp.zeros((CHUNK, LANES), F32)
         h_ref[sub] = state[...]
         for q in range(pairs):
             lanes = slice(q * LANES, (q + 1) * LANES)
-            v, _ = _conv(xbuf, base + 5, lanes, convx_ref[:, lanes], CHUNK)
+            v, _ = _conv(xbuf, base, lanes, convx_ref[:, lanes], CHUNK)
             x_act = v * _sigmoid(v)
-            u = x_act * _pair_cols(lo, delta, q)
+            u = x_act * wide[0:CHUNK, lanes]
             left = []
             for h in (2 * q, 2 * q + 1):
                 e = jnp.exp2(jnp.minimum(cum[:, h : h + 1] - cum_t[h : h + 1, :], 0.0))
@@ -319,10 +338,10 @@
                         preferred_element_type=F32)
             outer = jnp.dot(c_wide, jnp.concatenate([held_high, held_high, held_low], axis=0),
                             preferred_element_type=F32)
-            y = y + outer * _pair_cols(lo, grow, q) + lane_ref[0:1, lanes] * x_act
+            y = y + outer * wide[2 * CHUNK :, lanes] + lane_ref[0:1, lanes] * x_act
             y_ref[span, lanes] = y
-            uw = (u * _pair_cols(lo, tail, q)).astype(BF)
-            factor = _pair_cols(lo[0:1, :], decay, q)
+            uw = (u * wide[CHUNK : 2 * CHUNK, lanes]).astype(BF)
+            factor = wide[3 * CHUNK - 1 : 3 * CHUNK, lanes]
             state[:, lanes] = held * factor + jnp.dot(b_t, uw, preferred_element_type=F32)
             z = p_ref[span, lanes]
             product = y * (z * _sigmoid(z))
@@ -350,15 +369,15 @@
 
 
 def backward_kernel(width, outer_n, p_ref, prev_ref, y_ref, dy_ref, h_ref,
-                    convx_ref, convbc_ref, head_ref, lane_ref, partial, grads,
+                    convx_ref, convbc_ref, head_ref, lane_ref, partial, grads, resid,
                     dp_ref, gx_ref, gbc_ref, gh_ref, block_sum, owned,
-                    grad_state, carry_hg, xbuf, bcbuf, dvx, dvbc, *comm):
+                    grad_state, carry_hg, xbuf, bcbuf, after_x, after_bc, spread, wide, *comm):
     tokens = p_ref.shape[0]
     pairs = width // LANES
     step = pl.program_id(0)
     is_first_block = step == pl.num_programs(0) - 1
     length = partial.shape[0]
-    reduction = _Reduction(outer_n, partial, grads, block_sum, owned, *comm)
+    reduction = _Reduction(outer_n, partial, grads, resid, block_sum, owned, *comm)
 
     @pl.when(step == 0)
     def _():
@@ -373,8 +392,9 @@
     def _():
         grad_state[...] = jnp.zeros_like(grad_state)
         carry_hg[...] = jnp.zeros_like(carry_hg)
-        dvx[0:8, :] = jnp.zeros((8, width), F32)
-        dvbc[0:8, :] = jnp.zeros((8, 2 * LANES), F32)
+        after_x[...] = jnp.zeros_like(after_x)
+        after_bc[...] = jnp.zeros_like(after_bc)
+        _fill_spread(spread, LANES // 2)
         gx_ref[...] = jnp.zeros_like(gx_ref)
         gbc_ref[...] = jnp.zeros_like(gbc_ref)
         gh_ref[...] = jnp.zeros_like(gh_ref)
@@ -391,7 +411,7 @@
     for sub in reversed(range(tokens // CHUNK)):
         base = sub * CHUNK
         span = slice(base, base + CHUNK)
-        vbc, shifted_bc = _conv(bcbuf, base + 5, slice(0, 2 * LANES), convbc_ref[...], CHUNK)
+        vbc, shifted_bc = _conv(bcbuf, base, slice(0, 2 * LANES), convbc_ref[...], CHUNK)
         sbc = _sigmoid(vbc)
         bc = vbc * sbc
         b_in, c_out = bc[:, :LANES], bc[:, LANES:]
@@ -403,23 +423,21 @@
         last = cum[CHUNK - 1 : CHUNK, :]
         tail = jnp.exp2(last - cum)
         grow = jnp.exp2(cum)
-        decay = jnp.exp2(last)
+        _widen(wide, delta, tail, grow, spread)
         c_t = c_out.T.astype(BF)
         d_scores = jnp.zeros((CHUNK, CHUNK), F32)
         d_b = jnp.zeros((CHUNK, LANES), F32)
         d_c = jnp.zeros((CHUNK, LANES), F32)
         per_head = jnp.zeros((CHUNK, LANES), F32)
         hg_heads = jnp.zeros((8, LANES), F32)
-        dvx[CHUNK : CHUNK + 8, :] = dvx[0:8, :]
-        dvbc[CHUNK : CHUNK + 8, :] = dvbc[0:8, :]
         for q in range(pairs):
             lanes = slice(q * LANES, (q + 1) * LANES)
-            wide = _pair_cols(lo, delta, q)
+            step_wide = wide[0:CHUNK, lanes]
             skip = lane_ref[0:1, lanes]
-            v, shifted = _conv(xbuf, base + 5, lanes, convx_ref[:, lanes], CHUNK)
+            v, shifted = _conv(xbuf, base, lanes, convx_ref[:, lanes], CHUNK)
             sv = _sigmoid(v)
             x_act = v * sv
-            u = x_act * wide
+            u = x_act * step_wide
             u_half = u.astype(BF)
             y = y_ref[span, lanes]
             dy_half = dy_ref[span, lanes]
@@ -439,24 +457,20 @@
             h_half, h_low = _halves(h_held)
             right = jnp.concatenate([dy_block] + _split(lo, g_half), axis=0)
             du = jnp.dot(jnp.concatenate(left + left_b, axis=1), right, preferred_element_type=F32)
-            dx = du * wide + skip * dy
+            dx = du * step_wide + skip * dy
             dv = dx * (sv * (1.0 + v * (1.0 - sv)))
-            dvx[0:CHUNK, lanes] = dv
-            w = convx_ref[:, lanes]
-            d_in = w[TAPS - 1 : TAPS, :] * dv
-            for k in range(TAPS - 1):
-                ahead = TAPS - 1 - k
-                d_in = d_in + w[k : k + 1, :] * dvx[ahead : ahead + CHUNK, lanes]
+            d_in = _conv_back(dv, after_x[:, lanes], convx_ref[:, lanes])
+            after_x[:, lanes] = dv[0:8, :]
             dp_ref[span, lanes] = d_in.astype(BF)
             for k in range(TAPS):
                 gx_ref[k, :, lanes] += _rows_sum(dv * shifted[k])
             gx_ref[4, :, lanes] += _rows_sum(dv)
             gx_ref[5, :, lanes] += _rows_sum(dy * x_act)
-            edy = (dy * _pair_cols(lo, grow, q)).astype(BF)
-            uw = (u * _pair_cols(lo, tail, q)).astype(BF)
+            edy = (dy * wide[2 * CHUNK :, lanes]).astype(BF)
+            uw = (u * wide[CHUNK : 2 * CHUNK, lanes]).astype(BF)
             d_c = d_c + _dot_last(jnp.concatenate([edy, edy], axis=1), jnp.concatenate([h_half, h_low], axis=1))
             d_b = d_b + _dot_last(jnp.concatenate([uw, uw], axis=1), jnp.concatenate([g_half, g_low], axis=1))
-            g_new = g_held * _pair_cols(lo[0:1, :], decay, q) + jnp.dot(
+            g_new = g_held * wide[3 * CHUNK - 1 : 3 * CHUNK, lanes] + jnp.dot(
                 c_t, edy, preferred_element_type=F32)
             grad_state[:, lanes] = g_new
             r1 = x_act * du
@@ -477,12 +491,8 @@
         d_b = d_b + jnp.dot(ds_half, c_half, preferred_element_type=F32)
         d_c = d_c + jnp.dot(d_scores.T.astype(BF), b_half, preferred_element_type=F32)
         dvb = jnp.concatenate([d_b, d_c], axis=1) * (sbc * (1.0 + vbc * (1.0 - sbc)))
-        dvbc[0:CHUNK, :] = dvb
-        wbc = convbc_ref[...]
-        d_bc = wbc[TAPS - 1 : TAPS, :] * dvb
-        for k in range(TAPS - 1):
-            ahead = TAPS - 1 - k
-            d_bc = d_bc + wbc[k : k + 1, :] * dvbc[ahead : ahead + CHUNK, :]
+        d_bc = _conv_back(dvb, after_bc[...], convbc_ref[...])
+        after_bc[...] = dvb[0:8, :]
         dp_ref[span, width : width + 2 * LANES] = d_bc.astype(BF)
         for k in range(TAPS):
             gbc_ref[k] += _rows_sum(dvb * shifted_bc[k])
@@ -524,6 +534,8 @@
         scratch_shapes=[pltpu.VMEM((LANES, width), F32),
                         pltpu.VMEM((tokens + 8, width), F32),
                         pltpu.VMEM((tokens + 8, 2 * LANES), F32),
+                        pltpu.VMEM((2 * LANES, width), BF),
+                        pltpu.VMEM((3 * CHUNK, width), F32),
                         pltpu.VMEM((4, 2 * length // CHUNK, CHUNK), F32),
                         pltpu.SemaphoreType.DMA((2, 3))],
         compiler_params=pltpu.CompilerParams(collective_id=2, has_side_effects=True),
@@ -532,7 +544,7 @@
     )(proj, dg, convx, convbc, head, lane)
 
 
-def ssd_backward(proj, y, dy, states, convx, convbc, head, lane, partial, grads, tokens=256):
+def ssd_backward(proj, y, dy, states, convx, convbc, head, lane, partial, grads, resid, tokens=256):
     length, total = proj.shape
     width = convx.shape[1]
     subs = tokens // CHUNK
@@ -552,7 +564,7 @@
                   pl.BlockSpec((tokens, width), rev),
                   pl.BlockSpec((tokens, width), rev),
                   pl.BlockSpec((subs, LANES, width), lambda i: (n - 1 - i, 0, 0)),
-                  whole(convx), whole(convbc), whole(head), whole(lane), hbm, hbm],
+                  whole(convx), whole(convbc), whole(head), whole(lane), hbm, hbm, hbm],
         out_specs=[pl.BlockSpec((tokens, total - width), rev),
                    pl.BlockSpec((6, 8, width), lambda i: (0, 0, 0)),
                    pl.BlockSpec((5, 8, 2 * LANES), lambda i: (0, 0, 0)),
@@ -568,12 +580,14 @@
                         pltpu.VMEM((8, width), F32),
                         pltpu.VMEM((tokens + 8, width), F32),
                         pltpu.VMEM((tokens + 8, 2 * LANES), F32),
-                        pltpu.VMEM((CHUNK + 8, width), F32),
-                        pltpu.VMEM((CHUNK + 8, 2 * LANES), F32)] + reduction_scratch(dp // 2, block_shape, owned_shape),
+                        pltpu.VMEM((8, width), F32),
+                        pltpu.VMEM((8, 2 * LANES), F32),
+                        pltpu.VMEM((2 * LANES, width), BF),
+                        pltpu.VMEM((3 * CHUNK, width), F32)] + reduction_scratch(dp // 2, block_shape, owned_shape),
         compiler_params=pltpu.CompilerParams(collective_id=3, has_side_effects=True, vmem_limit_bytes=62 * 2**20),
         cost_estimate=pl.CostEstimate(flops=12 * 10**9, bytes_accessed=50 * 2**20, transcendentals=10**7),
         name="scan_backward",
-    )(proj, proj, y, dy, states, convx, convbc, head, lane, partial, grads)
+    )(proj, proj, y, dy, states, convx, convbc, head, lane, partial, grads, resid)
 
 
 def middle_kernel(width, inner_channels, z_ref, y_ref, dg_ref, s_ref, lane_ref, normed, cot, out_t,
@@ -655,7 +669,7 @@
     lane = pad_rows(jnp.stack([jnp.repeat(skip_gain, width // heads), gate_gain]), 8)
     return convx, convbc, head, lane
 def gather_kernel(outer_n, heads, small, wzx, wdt, wbc, wout, resid_in, cot_in,
-                  small_all, normed_out, cot_out, weight_out, wout_out, proj, d_gated,
+                  small_all, inv_out, normed_out, cot_out, weight_out, wout_out, proj, d_gated,
                   normed, cot, weight, w_out, resid, cot_f, stage, stage_g,
                   small_t, small_d, bc_slots, dt_slots,
                   small_sem_t, small_sem_d, bc_sem_t, bc_sem_d, dt_sem, norm_sem, cot_sem, zx_sem, wo_sem,
@@ -745,6 +759,7 @@
     loads[0].wait()
     values = resid[...]
     inv = lax.rsqrt(jnp.mean(values * values, axis=-1, keepdims=True) + EPSILON)
+    inv_out[...] = jnp.broadcast_to(inv, inv_out.shape)
 
     for copy in small_first + bc_first:
         copy.wait_recv()
@@ -902,8 +917,8 @@
     return pl.pallas_call(
         functools.partial(gather_kernel, outer_n, heads),
         in_specs=[vm] * 5 + [hbm] * 2,
-        out_specs=[vm] + [hbm] * 6,
-        out_shape=[shape(small.shape, F32), shape((length, model), BF), shape((length, model), BF),
+        out_specs=[vm] * 2 + [hbm] * 6,
+        out_shape=[shape(small.shape, F32), shape((resid.shape[0], LANES), F32), shape((length, model), BF), shape((length, model), BF),
                    shape((model, total), BF), shape((model, width), BF),
                    shape((length, total), F32), shape((length, width), F32)],
         scratch_shapes=[pltpu.VMEM((length, model), BF), pltpu.VMEM((length, model), BF),
@@ -921,9 +936,9 @@
     )(small, wzx, wdt, wbc, wout, resid, cot)
 
 
-def final_kernel(outer_n, both_rows, gain_rows, dz_in, rest_in, weight_in, normed_in, resid_in, small,
+def final_kernel(outer_n, both_rows, gain_rows, dz_in, rest_in, weight_in, normed_in, small, gain,
                  d_local, owned, small_out, bc_out,
-                 dz, rest, weight, normed, resid, g_all, tok, near_buf, far_src, far_buf, in_buf, out_src, out_buf,
+                 dz, rest, weight, normed, g_all, tok, near_buf, far_src, far_buf, in_buf, out_src, out_buf,
                  small_d, small_t, gain_d, gain_t, gain_acc, bc_src, bc_buf,
                  load_sem, near_sem, far_sem, in_sem, out_sem, small_sem_d, small_sem_t, gain_sem_d, gain_sem_t, bc_sem):
     z, y, x, c = _place()
@@ -939,7 +954,7 @@
     per_group = next(g for g in range(1, outer_n + 1) if (2 * g * block) % LANES == 0)
     groups = outer_n // per_group
     loads = [pltpu.make_async_copy(src, dst, load_sem.at[i]) for i, (src, dst) in enumerate(
-        [(dz_in, dz), (rest_in, rest), (weight_in, weight), (normed_in, normed), (resid_in, resid)])]
+        [(rest_in, rest), (normed_in, normed), (dz_in, dz), (weight_in, weight)])]
     for copy in loads:
         copy.start()
     _greet(outer_n)
@@ -983,13 +998,19 @@
                        out_sem.at[1, k - 1, part], _peer((z + k) % outer_n, y, x, c))
 
     def token_product(i, part):
-        far, near = ((1 - x, 1 - c), (1 - x, c), (x, 1 - c), (x, c))[i]
+        a, b = i // 2, i % 2
+        far, near = (1 - x) * (1 - a) + x * a, (1 - c) * (1 - b) + c * b
         rows = pl.ds(pl.multiple_of((far * 2 + near) * own_rows + part * half, LANES), half)
         value = _dot_last(dz[rows, :], weight[:, :width]) + _dot_last(rest[rows, :], weight[:, width:])
+        gain_acc[...] += _rows_sum(value * normed[rows, :].astype(F32))
         at = pl.ds(pl.multiple_of(part * half, LANES), half)
-        if i < 3:
+
+        @pl.when(i < 3)
+        def _():
             tok[i, at, :] = value.astype(BF)
-        else:
+
+        @pl.when(i == 3)
+        def _():
             d_local[at, :] = value
 
     def group(i):
@@ -1026,77 +1047,91 @@
     first = dp_copies(small, small_d, small_sem_d)
     for copy in first:
         copy.start()
-    for copy in loads[:3]:
+    for copy in loads[:2]:
         copy.wait()
+    gain_acc[...] = jnp.zeros_like(gain_acc)
     parts_half = PARTS // 2
-
-    @pl.loop(0, 2)
-    def _(part):
-        token_product(0, part)
-
-    for part in range(PARTS):
-        near_copy(0, part).start()
-    loads[3].wait()
-    group(0)
-
-    @pl.loop(0, 2)
-    def _(part):
-        token_product(1, part)
-
-    for part in range(PARTS):
-        token_step(part)
-
-    @pl.loop(1, groups)
-    def _(i):
-        group(i)
-
     order = list(range(1, outer_n)) + [0]
     todo = [(k, part) for k in order for part in range(wparts)]
-    quarter = -(-len(todo) // 4)
-    for k, part in todo[:quarter]:
-        grad_step(k, part)
-
-    @pl.loop(0, 2)
-    def _(part):
-        token_product(2, part)
-
-    for part in range(PARTS):
-        near_copy(1, part).start()
-    for copy in first:
-        copy.wait_recv()
-    total = dp_total(small_d)
-    small_out[...] = total
-    small_t[0] = total[:both_rows, :]
+    cut = lambda eighths: todo[: eighths * len(todo) // 8]
+    per_slot = -(-groups // 4)
     second = tensor_copies(small_t.at[0], small_t, small_sem_t)
-    for copy in second:
+
+    def near_start(i, which):
+        for part in range(which * parts_half, (which + 1) * parts_half):
+            near_copy(i, part).start()
+
+    def far_start(which):
+        for part in range(which * parts_half, (which + 1) * parts_half):
+            token_step(part)
+
+    def grads_between(low, high):
+        for k, part in cut(high)[len(cut(low)) :]:
+            grad_step(k, part)
+
+    def small_second():
+        for copy in first:
+            copy.wait_recv()
+        total = dp_total(small_d)
+        small_out[...] = total
+        small_t[0] = total[:both_rows, :]
+        for copy in second:
+            copy.start()
+
+    after = {
+        0: lambda: near_start(0, 0),
+        1: lambda: far_start(0),
+        2: lambda: near_start(0, 1),
+        3: lambda: (far_start(1), small_second(), grads_between(0, 1)),
+        4: lambda: (near_start(1, 0), grads_between(1, 2)),
+        5: lambda: grads_between(2, 4),
+        6: lambda: (near_start(1, 1), grads_between(4, 5)),
+        7: lambda: grads_between(5, 6),
+    }
+
+    @pl.loop(0, 8)
+    def _(it):
+        for r in range(per_slot):
+            @pl.when((it % 2 == 0) & (it // 2 * per_slot + r < groups))
+            def _():
+                group(it // 2 * per_slot + r)
+
+        @pl.when(it == 0)
+        def _():
+            for copy in loads[2:]:
+                copy.wait()
+
+        token_product(it // 4 * 2 + it % 2, it // 2 % 2)
+        for step, piece in after.items():
+            @pl.when(it == step)
+            def _(piece=piece):
+                piece()
+
+    for j in range(gain_rows):
+        gain_d[0, j : j + 1, :] = jnp.sum(
+            gain_acc[:, j * LANES : (j + 1) * LANES], axis=0, keepdims=True) / gain[j : j + 1, :]
+    gain_first = dp_copies(gain_d.at[0], gain_d, gain_sem_d)
+    for copy in gain_first:
         copy.start()
-    for k, part in todo[quarter : 2 * quarter]:
-        grad_step(k, part)
-
-    @pl.loop(0, 2)
-    def _(part):
-        token_product(3, part)
-
-    for k, part in todo[2 * quarter : 3 * quarter]:
-        grad_step(k, part)
-    loads[4].wait()
-    gain_acc[...] = jnp.zeros_like(gain_acc)
-    for part in range(PARTS):
+    gain_second = tensor_copies(gain_t.at[0], gain_t, gain_sem_t)
+
+    def token_finish(part):
         at = pl.ds(part * size, size)
         near_copy(1, part).wait_recv()
         far_copy(part).wait_recv()
-        got = d_local[at, :] + near_buf[1, at, :].astype(F32) + far_buf[at, :].astype(F32)
-        d_local[at, :] = got
-        values = resid[at, :]
-        inv = lax.rsqrt(jnp.mean(values * values, axis=-1, keepdims=True) + EPSILON)
-        gain_acc[...] += _rows_sum(got * values * inv)
-    for j in range(gain_rows):
-        gain_d[0, j : j + 1, :] = jnp.sum(gain_acc[:, j * LANES : (j + 1) * LANES], axis=0, keepdims=True)
-    gain_first = dp_copies(gain_d.at[0], gain_d, gain_sem_d)
+        d_local[at, :] = d_local[at, :] + near_buf[1, at, :].astype(F32) + far_buf[at, :].astype(F32)
+
+    grads_between(6, 7)
     for copy in gain_first:
+        copy.wait_recv()
+    gain_t[0] = dp_total(gain_d)
+    for copy in gain_second:
         copy.start()
-    for k, part in todo[3 * quarter :]:
-        grad_step(k, part)
+    for part in range(parts_half):
+        token_finish(part)
+    grads_between(7, 8)
+    for part in range(parts_half, PARTS):
+        token_finish(part)
     for part in range(wparts):
         at = pl.ds(part * bsize, bsize)
         total = owned[at, :]
@@ -1113,13 +1148,6 @@
         bc_copies.append(_remote(bc_src.at[other], bc_buf.at[i], bc_sem.at[0, i], bc_sem.at[1, i],
                                  _peer(z, y, (x + k) % 2, (c + j) % 2)))
     for copy in bc_copies:
-        copy.start()
-    for copy in gain_first:
-        copy.wait_recv()
-    total = dp_total(gain_d)
-    gain_t[0] = total
-    gain_second = tensor_copies(gain_t.at[0], gain_t, gain_sem_t)
-    for copy in gain_second:
         copy.start()
     for copy in second:
         copy.wait_recv()
@@ -1145,10 +1173,10 @@
         copy.wait_send()
 
 
-def final_sums(dz, rest, weight, normed, resid, small, both_rows):
+def final_sums(dz, rest, weight, normed, small, gain, both_rows):
     dp, tp = lax.axis_size("dp"), lax.axis_size("tensor")
     outer_n = dp // 2
-    own_rows, model = resid.shape
+    own_rows, model = normed.shape[0] // tp, normed.shape[1]
     block, cols = model // dp, rest.shape[1]
     gain_rows = model // LANES
     gain_pad = -(-gain_rows // 8) * 8
@@ -1160,14 +1188,14 @@
     bc = (4, block // 4, 2 * LANES)
     return pl.pallas_call(
         functools.partial(final_kernel, outer_n, both_rows, gain_rows),
-        in_specs=[hbm] * 5 + [vm],
+        in_specs=[hbm] * 4 + [vm] * 2,
         out_specs=[vm] * 4,
         out_shape=[jax.ShapeDtypeStruct(tokens, F32),
                    jax.ShapeDtypeStruct((block, cols), F32),
                    jax.ShapeDtypeStruct(small.shape, F32),
                    jax.ShapeDtypeStruct(bc[1:], F32)],
         scratch_shapes=[pltpu.VMEM(dz.shape, BF), pltpu.VMEM(rest.shape, BF), pltpu.VMEM(weight.shape, BF),
-                        pltpu.VMEM(normed.shape, BF), pltpu.VMEM(tokens, F32),
+                        pltpu.VMEM(normed.shape, BF),
                         pltpu.VMEM((outer_n, 2, block, cols), BF),
                         pltpu.VMEM((3,) + tokens, BF), pltpu.VMEM((2,) + tokens, BF),
                         pltpu.VMEM(tokens, BF), pltpu.VMEM(tokens, BF),
@@ -1176,13 +1204,13 @@
                         pltpu.VMEM((dp,) + small.shape, F32), pltpu.VMEM((4, both_rows, LANES), F32),
                         pltpu.VMEM((dp, gain_pad, LANES), F32), pltpu.VMEM((4, gain_pad, LANES), F32),
                         pltpu.VMEM((8, model), F32), pltpu.VMEM(bc, F32), pltpu.VMEM((3,) + bc[1:], F32),
-                        dma((5,)), dma((2, 2, PARTS)), dma((2, PARTS)), dma((2, outer_n, wparts)),
+                        dma((4,)), dma((2, 2, PARTS)), dma((2, PARTS)), dma((2, outer_n, wparts)),
                         dma((2, outer_n - 1, wparts)), dma((2, dp - 1)), dma((2, 3)), dma((2, dp - 1)), dma((2, 3)),
                         dma((2, 3))],
         compiler_params=pltpu.CompilerParams(collective_id=1, has_side_effects=True, vmem_limit_bytes=63 * 2**20),
         cost_estimate=pl.CostEstimate(flops=20 * 10**9, bytes_accessed=40 * 2**20, transcendentals=0),
         name="final_sums",
-    )(dz, rest, weight, normed, resid, small)
+    )(dz, rest, weight, normed, small, gain)
 
 
 def _spread(values, index, count):
@@ -1217,7 +1245,7 @@
     gain_rows = model // LANES
     both_rows = -(-small.shape[0] // 8) * 8
     small = pad_rows(small, both_rows)
-    small_all, normed, cot_full, weight, out_t, proj, d_gated = gather_all(
+    small_all, inv_in, normed, cot_full, weight, out_t, proj, d_gated = gather_all(
         small, resid, cot, proj_zx.reshape(rows, 2 * width), proj_dt, proj_bc, proj_out.T)
     full_cbw = small_all[gain_rows : gain_rows + 4 * states2 // LANES].reshape(4, states2)
     full_cbb = small_all[gain_rows + 4 * states2 // LANES : gain_rows + 5 * states2 // LANES].reshape(states2)
@@ -1225,16 +1253,15 @@
     packs = pack_params(conv_x_weight, conv_x_bias, full_cbw, full_cbb, dt_bias, a_log, skip_gain, gate_gain)
     y, states, partial = ssd_forward(proj, d_gated, *packs)
     dy, dz, out_partial, grads_zo, ggain = middle(proj, y, d_gated, partial, packs[3], normed, cot_full, out_t, inner_channels)
-    d_rest, gx, gbc, gh, block_sum, owned_zo = ssd_backward(proj, y, dy, states, *packs, out_partial, grads_zo)
-    block_out = resid + block_sum
+    d_rest, gx, gbc, gh, block_out, owned_zo = ssd_backward(proj, y, dy, states, *packs, out_partial, grads_zo, resid)
     gx = jnp.concatenate([gx.sum(1), ggain.sum(0)[None]], 0)
     gbc, gh = gbc.sum(1), gh.sum(1)
     to_sum = jnp.concatenate([
         pad_rows(jnp.concatenate([jnp.zeros((gain_rows, LANES), F32), gbc.reshape(-1, LANES)], 0), both_rows),
         gx.reshape(-1, LANES), gh], axis=0)
     to_sum = pad_rows(to_sum, -(-to_sum.shape[0] // 8) * 8)
-    d_local, owned, totals, grad_bc = final_sums(dz, d_rest, weight, normed, resid, to_sum, both_rows)
-    inv_in = lax.rsqrt(jnp.mean(resid * resid, axis=-1, keepdims=True) + EPSILON)
+    d_local, owned, totals, grad_bc = final_sums(dz, d_rest, weight, normed, to_sum, small_all, both_rows)
+    inv_in = inv_in[:, :1]
     scaled = resid * inv_in
     d_scaled = d_local * full_gain
     grad_resid = inv_in * (d_scaled - scaled * jnp.mean(d_scaled * scaled, axis=-1, keepdims=True)) + cot

time: 366 us -> 354 us (0.967); the launches traced: 359 us -> 353 us
  Pallas kernels: 323 us -> 314 us
  local copies, waits for them, and re-layouts: 16.1 us -> 23.8 us
    pallas_call x1, Pallas kernels: 34.7 us -> 28.6 us  [ssd_forward(): pl.pallas_call(functools.partial(forward_kernel, width), grid=(length //...]
    unnamed x38 -> x21, local copies, waits for them, and re-layouts: 5.34 us -> 8.03 us
where the time goes in v3:
time: 354 us; the launch traced here: 353 us
  Pallas kernels  314 us (89%)
  local copies, waits for them, and re-layouts  23.8 us (7%)
  other arithmetic  15.1 us (4%)
    pallas_call x1, Pallas kernels, gather_all(): pl.pallas_call(functools.partial(gather_kernel, outer_n, heads), in_specs...  123 us
    pallas_call x1, Pallas kernels, final_sums(): pl.pallas_call(functools.partial(final_kernel, outer_n, both_rows, gain_r...  66.3 us
    pallas_call x1, Pallas kernels, ssd_backward(): pl.pallas_call(functools.partial(backward_kernel, width, dp // 2), grid=(...  66.2 us
    pallas_call x1, Pallas kernels, middle(): pl.pallas_call(functools.partial(middle_kernel, width, inner_channels), g...  29.4 us
    pallas_call x1, Pallas kernels, ssd_forward(): pl.pallas_call(functools.partial(forward_kernel, width), grid=(length //...  28.6 us
    unnamed x21, local copies, waits for them, and re-layouts  8.03 us

profile of v3, /device:TPU:0, one launch (start us, length us, event | category | flops | bytes accessed | tf_op | source)
XLA Modules:
  0.0 353.3 jit_solution(3518367965548507733)
XLA Ops:
  0.7 0.9 dynamic_update_slice.11
  1.5 0.7 broadcast_in_dim.29
  2.2 0.7 stack.27
  2.9 1.3 select_maximum_fusion.6.head_ref
  4.2 0.8 dynamic_update_slice.10
  5.0 1.3 pad.33.wdt
  6.3 0.7 broadcast_in_dim.30
  7.1 0.8 dynamic_update_slice.9
  8.5 1.3 select_maximum_fusion.1
  9.9 1.9 copy.34
  11.8 123.1 %gather_all.1 = (f32[24,128]{1,0:T(8,128)}, f32[512,128]{1,0:T(8,128)}, bf16[2048,1536]{1,0:T(8,128)(2,1)}, bf16[2048,1536]{1,0:T(8,128)(2,1)}, bf16[1536,1920]{...) custom-call(f32[24,128]{1,0:T(8,128)} %select_maximum_fusion.3.small, ...), custom_call_target="tpu_custom_call" | custom-call | flops 16999999488 | bytes 62914560 | tf_op jit(solution)/shard_map/gather_all/pallas_call | solution.py:917
  134.9 0.7 slice.66
  135.5 1.1 slice_reduce_fusion
  136.6 0.7 slice.65
  138.0 0.7 slice_bitcast_fusion.4
  138.7 28.6 %scan_forward.1 = (f32[2048,768]{1,0:T(8,128)}, f32[16,128,768]{2,1,0:T(8,128)}, f32[32,128]{1,0:T(8,128)}) custom-call(f32[2048,1920]{1,0:T(8,128)} %get-tuple-element.41.p_ref.z_ref.prev_ref, f32[2048,768]{1,0:T(8,128)} %get-tuple-element.42.dg_ref, f32[8,768]{1,0:T(8,128)} %get-tuple-element.105.convx_ref, f32[8,256]{1,0:T(8,128)} %select_maximum_fusion.5.convbc_ref, ...), custom_call_target="tpu_custom_call" | custom-call | flops 4000000000 | bytes 31457280 | tf_op jit(solution)/shard_map/scan_forward/pallas_call | solution.py:522
  167.3 29.4 %middle.1 = (bf16[2048,768]{1,0:T(8,128)(2,1)}, bf16[2048,768]{1,0:T(8,128)(2,1)}, bf16[2048,1536]{1,0:T(8,128)(2,1)}, bf16[1536,1536]{1,0:T(8,128)(2,1)}, f32[8,768]{1,0:T(8,128)}) custom-call(f32[2048,1920]{1,0:T(8,128)} %get-tuple-element.41.p_ref.z_ref.prev_ref, f32[2048,768]{1,0:T(8,128)} %get-tuple-element.44.y_ref, ...), custom_call_target="tpu_custom_call" | custom-call | flops 15000000512 | bytes 52428800 | tf_op jit(solution)/shard_map/middle/pallas_call | solution.py:640
  196.7 66.2 %scan_backward.1 = (bf16[2048,1152]{1,0:T(8,128)(2,1)}, f32[6,8,768]{2,1,0:T(8,128)}, f32[5,8,256]{2,1,0:T(8,128)}, f32[2,8,128]{2,1,0:T(8,128)}, f32[512,1536]{1,0:T(8,128)}, /*index=5*/f32[192,1536]{1,0:T(8,128)}) custom-call(f32[2048,1920]{1,0:T(8,128)} %get-tuple-element.41.p_ref.z_ref.prev_ref, f32[2048,1920]{1,0:T(8,128)} %get-tuple-element.41.p_ref.z_ref.prev_ref, ...), custom_call_target="tpu_custom_call" | custom-call | flops 12000000000 | bytes 52428800 | tf_op jit(solution)/shard_map/scan_backward/pallas_call | solution.py:559
  262.9 0.7 reduce_sum.57
  263.7 0.8 reduce_sum.54
  264.5 1.0 reduce_sum.55
  266.1 66.3 %final_sums.1 = (f32[512,1536]{1,0:T(8,128)}, f32[192,1152]{1,0:T(8,128)}, f32[72,128]{1,0:T(8,128)}, f32[48,256]{1,0:T(8,128)}) custom-call(bf16[2048,768]{1,0:T(8,128)(2,1)} %get-tuple-element.55.dz_in, bf16[2048,1152]{1,0:T(8,128)(2,1)} %get-tuple-element.56.rest_in, bf16[1536,1920]{1,0:T(8,128)(2,1)} %get-tuple-element.57.weight_in, ...), custom_call_target="tpu_custom_call" | custom-call | flops 20000000000 | bytes 41943040 | tf_op jit(solution)/shard_map/final_sums/pallas_call | solution.py:1189
  332.4 0.7 slice_bitcast_fusion.7
  333.7 1.3 slice_bitcast_fusion.8
  334.9 3.5 multiply_reduce_fusion
  338.7 1.0 copy-done.1
  339.6 4.5 %add_bitcast_fusion = f32[1,512,1536]{2,1,0:T(8,128)} fusion(f32[512,1536]{1,0:T(8,128)S(1)} %copy-done.1, f32[512]{0:T(512)S(1)} %broadcast_multiply_fusion, f32[1536]{0:T(1024)S(1)} %slice_bitcast_fusion.4, f32[512]{0:T(512)S(1)} %slice_reduce_fusion, f32[1,512,1536]{2,1,0:T(8,128)} %param.29, f32[1,512,1536]{2,1,0:T(8,128)S(1)} %copy-done), kind=kLoop, calls=%fused_computation | loop fusion | flops 4718592 | bytes 12593152 | tf_op jit(solution)/shard_map/broadcast_in_dim | solution.py:1279
  344.2 0.7 constant_dynamic-slice_fusion
  347.4 0.7 copy.33
  348.1 0.9 slice_bitcast_fusion
  349.1 1.9 copy.32
  351.0 1.7 copy.40
  (45 shorter events, 6.1 us)
Async XLA Ops:
  196.7 67.0 %copy-start.7 = (f32[8,768]{1,0:T(8,128)S(1)}, f32[8,768]{1,0:T(8,128)}, u32[]{:S(2)}) copy-start(f32[8,768]{1,0:T(8,128)} %get-tuple-element.60) | copy-start | bytes 73732
  334.9 3.7 %copy-start = (f32[1,512,1536]{2,1,0:T(8,128)S(1)}, f32[1,512,1536]{2,1,0:T(8,128)}, u32[]{:S(2)}) copy-start(f32[1,512,1536]{2,1,0:T(8,128)} %param.15) | copy-start | bytes 9437188
  334.9 4.7 %copy-start.1 = (f32[512,1536]{1,0:T(8,128)S(1)}, f32[512,1536]{1,0:T(8,128)}, u32[]{:S(2)}) copy-start(f32[512,1536]{1,0:T(8,128)} %get-tuple-element.62) | copy-start | bytes 9437188
  339.6 4.5 %copy-start.6 = (f32[72,128]{1,0:T(8,128)S(1)}, f32[72,128]{1,0:T(8,128)}, u32[]{:S(2)}) copy-start(f32[72,128]{1,0:T(8,128)} %get-tuple-element.63) | copy-start | bytes 110596
  339.6 7.7 %copy-start.4 = (f32[192,1152]{1,0:T(8,128)S(1)}, f32[192,1152]{1,0:T(8,128)}, u32[]{:S(2)}) copy-start(f32[192,1152]{1,0:T(8,128)} %get-tuple-element.65) | copy-start | bytes 2654212
  339.6 8.4 %copy-start.3 = (f32[192,1536]{1,0:T(8,128)S(1)}, f32[192,1536]{1,0:T(8,128)}, u32[]{:S(2)}) copy-start(f32[192,1536]{1,0:T(8,128)} %get-tuple-element.64) | copy-start | bytes 3538948
  348.1 2.9 copy-start.2
  351.0 1.7 copy-start.5

commit v4 on v3

--- a/solution.py
+++ b/solution.py
@@ -58,26 +58,107 @@
     return pl.ds(pl.multiple_of(start, 16), size)
 
 
-class _Reduction:
-    def __init__(self, outer_n, partial, grads, resid, block_sum, owned, resid_buf, own_tokens, near_buf, far_src, far_buf,
-                 own_grads, in_buf, out_src, out_buf, near_sem, far_sem, in_sem, out_sem, local_sem):
+class _RowSums:
+    def __init__(self, outer_n, block, source, mine, owned, in_buf, pair_src, pair_buf, cross_src, cross_buf,
+                 in_sem, pair_sem, cross_sem):
         self.__dict__.update(locals())
         self.z, self.y, self.x, self.c = _place()
-        self.me = _peer(self.z, self.y, self.x, self.c)
+        self.h, self.l = self.z // 2, self.z % 2
+        self.pairs = outer_n // 2
+        self.parts = _parts(block)
+        self.size = block // self.parts
+        self.order = list(range(1, self.pairs)) + [0]
+
+    def outer_of(self, r, m):
+        low = self.l if m else 1 - self.l
+        return lax.rem(self.h + r, self.pairs) * 2 + low
+
+    def slot_of(self, outer):
+        r = lax.rem(outer // 2 - self.h + self.pairs, self.pairs)
+        low = outer % 2
+        return r * 2 + 1 - (low + self.l - 2 * low * self.l)
+
+    def at(self, part):
+        return pl.ds(part * self.size, self.size)
+
+    def in_copy(self, slot, outer, part):
+        return _remote(self.source(slot, outer, 1 - self.y, part), self.in_buf.at[slot, self.at(part), :],
+                       self.in_sem.at[0, slot, part], self.in_sem.at[1, slot, part],
+                       _peer(self.z, 1 - self.y, self.x, self.c))
+
+    def pair_copy(self, r, part):
+        return _remote(self.pair_src.at[r, self.at(part), :], self.pair_buf.at[r, self.at(part), :],
+                       self.pair_sem.at[0, r, part], self.pair_sem.at[1, r, part],
+                       _peer(self.h * 2 + 1 - self.l, self.y, self.x, self.c))
+
+    def cross_copy(self, r, part):
+        return _remote(self.cross_src.at[r - 1, self.at(part), :], self.cross_buf.at[r - 1, self.at(part), :],
+                       self.cross_sem.at[0, r - 1, part], self.cross_sem.at[1, r - 1, part],
+                       _peer(lax.rem(self.h + r, self.pairs) * 2 + self.l, self.y, self.x, self.c))
+
+    def todo(self):
+        return [(r, m, part) for r in self.order for m in (0, 1) for part in range(self.parts)]
+
+    def step(self, r, m, part):
+        at = self.at(part)
+        outer = self.outer_of(r, m)
+        self.in_copy(r * 2 + m, outer, part).wait_recv()
+        both = self.mine(r * 2 + m, outer, part) + self.in_buf[r * 2 + m, at, :].astype(F32)
+        if m == 0:
+            self.pair_src[r, at, :] = both.astype(BF)
+            self.pair_copy(r, part).start()
+            return
+        self.pair_copy(r, part).wait_recv()
+        both = both + self.pair_buf[r, at, :].astype(F32)
+        if r:
+            self.cross_src[r - 1, at, :] = both.astype(BF)
+            self.cross_copy(r, part).start()
+        else:
+            self.owned[at, :] = both
+
+    def finish(self):
+        for part in range(self.parts):
+            at = self.at(part)
+            total = self.owned[at, :]
+            for r in self.order[:-1]:
+                self.cross_copy(r, part).wait_recv()
+                total = total + self.cross_buf[r - 1, at, :].astype(F32)
+            self.owned[at, :] = total
+
+    def wait_sends(self):
+        for r, m, part in self.todo():
+            self.in_copy(r * 2 + m, self.outer_of(r, m), part).wait_send()
+            if m == 0:
+                self.pair_copy(r, part).wait_send()
+            elif r:
+                self.cross_copy(r, part).wait_send()
+
+
+def row_sums_scratch(outer_n, shape):
+    dma = pltpu.SemaphoreType.DMA
+    parts, pairs = _parts(shape[0]), outer_n // 2
+    return [pltpu.VMEM((outer_n,) + shape, BF), pltpu.VMEM((pairs,) + shape, BF), pltpu.VMEM((pairs,) + shape, BF),
+            pltpu.VMEM((pairs - 1,) + shape, BF), pltpu.VMEM((pairs - 1,) + shape, BF),
+            dma((2, outer_n, parts)), dma((2, pairs, parts)), dma((2, pairs - 1, parts))]
+
+
+class _Reduction:
+    def __init__(self, outer_n, partial, grads, resid, block_sum, owned, resid_buf, own_tokens, near_buf, far_src,
+                 far_buf, own_grads, send_grads, near_sem, far_sem, local_sem, *row_sums):
+        self.__dict__.update(locals())
+        self.z, self.y, self.x, self.c = _place()
         self.own_rows = block_sum.shape[0]
         self.block = owned.shape[0]
-        self.wparts = _parts(self.block)
         self.size = self.own_rows // PARTS
-        self.bsize = self.block // self.wparts
-        order = list(range(1, outer_n))
-        order.sort(key=lambda k: -min(k, outer_n - k))
-        self.order = order + [0]
+        block, size = self.block, self.block // _parts(self.block)
+        self.sums = _RowSums(
+            outer_n, block,
+            lambda slot, outer, inner, part: send_grads.at[slot, pl.ds(part * size, size), :],
+            lambda slot, outer, part: own_grads[slot, pl.ds(part * size, size), :].astype(F32),
+            owned, *row_sums)
 
     def token_rows(self, far, near, part):
         return _rows((far * 2 + near) * self.own_rows + part * self.size, self.size)
-
-    def grad_rows(self, outer, inner, part):
-        return _rows((outer * 2 + inner) * self.block + part * self.bsize, self.bsize)
 
     def near_copy(self, i, part):
         far = (1 - self.x, self.x)[i]
@@ -91,34 +172,38 @@
         return _remote(self.far_src.at[at, :], self.far_buf.at[at, :], self.far_sem.at[0, part],
                        self.far_sem.at[1, part], _peer(self.z, self.y, 1 - self.x, self.c))
 
-    def in_copy(self, k, part):
-        at = pl.ds(part * self.bsize, self.bsize)
-        rows = self.grad_rows((self.z + k) % self.outer_n, 1 - self.y, part)
-        return _remote(self.grads.at[rows, :], self.in_buf.at[k, at, :], self.in_sem.at[0, k, part],
-                       self.in_sem.at[1, k, part], _peer(self.z, 1 - self.y, self.x, self.c))
-
-    def out_copy(self, k, part):
-        at = pl.ds(part * self.bsize, self.bsize)
-        return _remote(self.out_src.at[k - 1, at, :], self.out_buf.at[k - 1, at, :], self.out_sem.at[0, k - 1, part],
-                       self.out_sem.at[1, k - 1, part], _peer((self.z + k) % self.outer_n, self.y, self.x, self.c))
-
     def local_copies(self):
-        copies = [pltpu.make_async_copy(self.resid, self.resid_buf, self.local_sem.at[2 + self.outer_n])]
+        copies = [pltpu.make_async_copy(self.resid, self.resid_buf, self.local_sem.at[0])]
         for i, far in enumerate((1 - self.x, self.x)):
             rows = _rows((far * 2 + self.c) * self.own_rows, self.own_rows)
-            copies.append(pltpu.make_async_copy(self.partial.at[rows, :], self.own_tokens.at[i], self.local_sem.at[i]))
-        for k in range(self.outer_n):
-            rows = _rows((((self.z + k) % self.outer_n) * 2 + self.y) * self.block, self.block)
-            copies.append(pltpu.make_async_copy(self.grads.at[rows, :], self.own_grads.at[k], self.local_sem.at[2 + k]))
+            copies.append(pltpu.make_async_copy(self.partial.at[rows, :], self.own_tokens.at[i], self.local_sem.at[1 + i]))
+        for r in range(self.outer_n // 2):
+            for m in (0, 1):
+                rows = _rows((self.sums.outer_of(r, m) * 2 + self.y) * self.block, self.block)
+                copies.append(pltpu.make_async_copy(self.grads.at[rows, :], self.own_grads.at[r * 2 + m],
+                                                    self.local_sem.at[3 + r * 2 + m]))
         return copies
 
+    def send_loads(self):
+        copies = []
+        for r in self.sums.order:
+            for m in (0, 1):
+                rows = _rows((self.sums.outer_of(r, m) * 2 + 1 - self.y) * self.block, self.block)
+                copies.append(pltpu.make_async_copy(self.grads.at[rows, :], self.send_grads.at[r * 2 + m],
+                                                    self.local_sem.at[3 + self.outer_n + r * 2 + m]))
+        return copies
+
     def begin(self):
+        loads = self.send_loads()
+        for copy in loads:
+            copy.start()
         _greet(self.outer_n)
         for part in range(PARTS):
             self.near_copy(0, part).start()
-        for k in self.order:
-            for part in range(self.wparts):
-                self.in_copy(k, part).start()
+        for i, (r, m, part) in enumerate(self.sums.todo()):
+            if part == 0:
+                loads[i // self.sums.parts].wait()
+            self.sums.in_copy(r * 2 + m, self.sums.outer_of(r, m), part).start()
         for part in range(PARTS):
             self.near_copy(1, part).start()
         for copy in self.local_copies():
@@ -134,65 +219,39 @@
         self.far_src[at, :] = (self.own_tokens[0, at, :].astype(F32) + self.near_buf[0, at, :].astype(F32)).astype(BF)
         self.far_copy(part).start()
 
-    def grad_step(self, k, part):
-        at = pl.ds(part * self.bsize, self.bsize)
-        self.in_copy(k, part).wait_recv()
-        both = self.own_grads[k, at, :].astype(F32) + self.in_buf[k, at, :].astype(F32)
-        if k:
-            self.out_src[k - 1, at, :] = both.astype(BF)
-            self.out_copy(k, part).start()
-        else:
-            self.owned[at, :] = both
-
-    def grad_steps(self):
-        return [(k, part) for k in self.order for part in range(self.wparts)]
-
     def plan(self, steps):
         pieces = [(1, self.ready)]
         for part in range(PARTS):
             pieces.append((min(1 + part, steps - 1), functools.partial(self.token_step, part)))
-        todo = self.grad_steps()
+        todo = self.sums.todo()
         self.late = len(todo) // 8
-        for i, (k, part) in enumerate(todo[: len(todo) - self.late]):
-            pieces.append((min(1 + (i + 2) * (steps - 1) // len(todo), steps - 1),
-                           functools.partial(self.grad_step, k, part)))
+        for i, item in enumerate(todo[: len(todo) - self.late]):
+            pieces.append((min(1 + (i + 3) * (steps - 1) // len(todo), steps - 1),
+                           functools.partial(self.sums.step, *item)))
         return pieces
 
     def end(self):
-        for k, part in self.grad_steps()[-self.late :]:
-            self.grad_step(k, part)
         for part in range(PARTS):
             at = pl.ds(part * self.size, self.size)
             self.near_copy(1, part).wait_recv()
             self.far_copy(part).wait_recv()
             self.block_sum[at, :] = (self.own_tokens[1, at, :].astype(F32) + self.near_buf[1, at, :].astype(F32)
                                      + self.far_buf[at, :].astype(F32)) + self.resid_buf[at, :]
-        for part in range(self.wparts):
-            at = pl.ds(part * self.bsize, self.bsize)
-            total = self.owned[at, :]
-            for k in self.order[:-1]:
-                self.out_copy(k, part).wait_recv()
-                total = total + self.out_buf[k - 1, at, :].astype(F32)
-            self.owned[at, :] = total
+        for item in self.sums.todo()[-self.late :]:
+            self.sums.step(*item)
+        self.sums.finish()
         for part in range(PARTS):
             self.near_copy(0, part).wait_send()
             self.near_copy(1, part).wait_send()
             self.far_copy(part).wait_send()
-        for part in range(self.wparts):
-            for k in self.order:
-                self.in_copy(k, part).wait_send()
-                if k:
-                    self.out_copy(k, part).wait_send()
+        self.sums.wait_sends()
 
 
 def reduction_scratch(outer_n, tokens, grads):
     dma = pltpu.SemaphoreType.DMA
-    parts = _parts(grads[0])
-    return [pltpu.VMEM(tokens, F32), pltpu.VMEM((2,) + tokens, BF), pltpu.VMEM((2,) + tokens, BF), pltpu.VMEM(tokens, BF),
-            pltpu.VMEM(tokens, BF), pltpu.VMEM((outer_n,) + grads, BF), pltpu.VMEM((outer_n,) + grads, BF),
-            pltpu.VMEM((outer_n - 1,) + grads, BF), pltpu.VMEM((outer_n - 1,) + grads, BF),
-            dma((2, 2, PARTS)), dma((2, PARTS)), dma((2, outer_n, parts)), dma((2, outer_n - 1, parts)),
-            dma((3 + outer_n,))]
+    return [pltpu.VMEM(tokens, F32), pltpu.VMEM((2,) + tokens, BF), pltpu.VMEM((2,) + tokens, BF),
+            pltpu.VMEM(tokens, BF), pltpu.VMEM(tokens, BF), pltpu.VMEM((outer_n,) + grads, BF), pltpu.VMEM((outer_n,) + grads, BF),
+            dma((2, 2, PARTS)), dma((2, PARTS)), dma((3 + 2 * outer_n,))] + row_sums_scratch(outer_n, grads)
 
 
 def _sigmoid(v):
@@ -694,8 +753,6 @@
     _greet(outer_n)
     dp_peers = [(k, j) for k in range(outer_n) for j in (0, 1) if k or j]
     tensor_peers = [(k, j) for k in (0, 1) for j in (0, 1) if k or j]
-    order = list(range(1, outer_n))
-    order.sort(key=lambda k: -min(k, outer_n - k))
     at_dp = lambda k, j: _peer((z + k) % outer_n, (y + j) % 2, x, c)
     at_tensor = lambda k, j: _peer(z, y, (x + k) % 2, (c + j) % 2)
 
@@ -708,43 +765,70 @@
     for copy in small_first + bc_first + dt_first:
         copy.start()
 
-    def rows_of(outer, inner, part):
-        return _rows((outer * 2 + inner) * block + part * bsize, bsize)
-
-    def across(src, dst, cols, sem, k, part):
-        return _remote(src.at[pl.ds(part * bsize, bsize), :], dst.at[rows_of(z, y, part), cols],
-                       sem.at[0, k, part], sem.at[1, k, part], _peer(lax.rem(z + k, outer_n), y, x, c))
-
-    def beside(src, dst, cols, sem, part):
-        return _remote(src.at[pl.ds(part * bsize, bsize), :], dst.at[rows_of(z, y, part), cols],
-                       sem.at[2, 0, part], sem.at[3, 0, part], _peer(z, 1 - y, x, c))
-
-    def onward(dst, cols, sem, k, part):
-        view = dst.at[rows_of(lax.rem(z - k + outer_n, outer_n), y, part), cols]
-        return _remote(view, view, sem.at[2, k, part], sem.at[3, k, part], _peer(z, 1 - y, x, c))
+    h, low = z // 2, z % 2
+    pairs = outer_n // 2
+
+    def view_of(dst, cols, r, m, inner, part):
+        outer = lax.rem(h + r, pairs) * 2 + (low if m else 1 - low)
+        return dst.at[_rows((outer * 2 + inner) * block + part * bsize, bsize), cols]
+
+    def piece_of(src, part):
+        return src.at[pl.ds(part * bsize, bsize), :]
+
+    def cross(src, dst, cols, sem, k, part):
+        return _remote(piece_of(src, part), view_of(dst, cols, 0, 1, y, part), sem.at[0, k * 2 + 1, part],
+                       sem.at[1, (pairs - k) * 2 + 1, part], _peer(lax.rem(h + k, pairs) * 2 + low, y, x, c))
+
+    def pair(src, dst, cols, sem, r, part):
+        view = view_of(dst, cols, r, 1, y, part)
+        return _remote(view if r else piece_of(src, part), view, sem.at[0, r * 2, part], sem.at[1, r * 2, part],
+                       _peer(h * 2 + 1 - low, y, x, c))
+
+    def onward(src, dst, cols, sem, r, m, part):
+        view = view_of(dst, cols, r, m, y, part)
+        slot = r * 2 + m
+        return _remote(piece_of(src, part) if slot == 1 else view, view, sem.at[2, slot, part], sem.at[3, slot, part],
+                       _peer(z, 1 - y, x, c))
+
+    def arrived(dst, cols, sem, r, m, part):
+        view = view_of(dst, cols, r, m, y, part)
+        _remote(view, view, sem.at[0, r * 2 + m, part], sem.at[1, r * 2 + m, part], me).wait_recv()
 
     def send_out(src, dst, cols, sem):
         for part in range(wparts):
-            for k in order:
-                across(src, dst, cols, sem, k, part).start()
-            beside(src, dst, cols, sem, part).start()
-
-    def pass_on(src, dst, cols, sem, part):
-        for k in order:
-            across(src, dst, cols, sem, k, part).wait_recv()
-            onward(dst, cols, sem, k, part).start()
+            for k in range(1, pairs):
+                cross(src, dst, cols, sem, k, part).start()
+            pair(src, dst, cols, sem, 0, part).start()
+            onward(src, dst, cols, sem, 0, 1, part).start()
+
+    def pass_first(src, dst, cols, sem, part):
+        for r in range(1, pairs):
+            arrived(dst, cols, sem, r, 1, part)
+            pair(src, dst, cols, sem, r, part).start()
+            onward(src, dst, cols, sem, r, 1, part).start()
+        arrived(dst, cols, sem, 0, 0, part)
+        onward(src, dst, cols, sem, 0, 0, part).start()
+
+    def pass_second(src, dst, cols, sem, part):
+        for r in range(1, pairs):
+            arrived(dst, cols, sem, r, 0, part)
+            onward(src, dst, cols, sem, r, 0, part).start()
 
     def finish(src, dst, cols, sem):
         for part in range(wparts):
-            for k in range(outer_n):
-                onward(dst, cols, sem, k, part).wait_recv()
+            for r in range(pairs):
+                for m in (0, 1):
+                    view = view_of(dst, cols, r, m, 1 - y, part)
+                    _remote(view, view, sem.at[2, r * 2 + m, part], sem.at[3, r * 2 + m, part], me).wait_recv()
 
     def finish_sends(src, dst, cols, sem):
         for part in range(wparts):
-            beside(src, dst, cols, sem, part).wait_send()
-            for k in order:
-                across(src, dst, cols, sem, k, part).wait_send()
-                onward(dst, cols, sem, k, part).wait_send()
+            for r in range(pairs):
+                if r:
+                    cross(src, dst, cols, sem, r, part).wait_send()
+                pair(src, dst, cols, sem, r, part).wait_send()
+                for m in (0, 1):
+                    onward(src, dst, cols, sem, r, m, part).wait_send()
 
     zx = (wzx, weight, pl.ds(0, zx_cols), zx_sem)
     wo = (wout, w_out, pl.ds(0, wout.shape[1]), wo_sem)
@@ -824,9 +908,12 @@
         weight[i * block : (i + 1) * block, zx_cols + bc_cols :] = columns.T[:block, :].astype(BF)
     for part in range(max(PARTS, wparts)):
         if part < wparts:
-            pass_on(*zx, part)
+            pass_first(*zx, part)
+        if 1 <= part < wparts:
+            pass_second(*zx, part - 1)
         if part < PARTS:
             pass_tokens(normed, norm_sem, part)
+    pass_second(*zx, wparts - 1)
     for copy in bc_second:
         copy.wait_recv()
     for i in range(outer_n * 2):
@@ -858,14 +945,20 @@
 
         @pl.when(i < wparts)
         def _():
-            pass_on(*wo, i)
+            pass_first(*wo, i)
+
+        @pl.when((i >= 1) & (i < wparts + 1))
+        def _():
+            pass_second(*wo, i - 1)
 
         @pl.when(i < PARTS)
         def _():
             pass_tokens(cot, cot_sem, i)
 
     for i in range(steps, wparts):
-        pass_on(*wo, i)
+        pass_first(*wo, i)
+    for i in range(steps - 1, wparts):
+        pass_second(*wo, i)
     for i in range(steps, PARTS):
         pass_tokens(cot, cot_sem, i)
     finish_tokens(cot, cot_sem)
@@ -938,11 +1031,10 @@
 
 def final_kernel(outer_n, both_rows, gain_rows, dz_in, rest_in, weight_in, normed_in, small, gain,
                  d_local, owned, small_out, bc_out,
-                 dz, rest, weight, normed, g_all, tok, near_buf, far_src, far_buf, in_buf, out_src, out_buf,
+                 dz, rest, weight, normed, g_all, tok, near_buf, far_src, far_buf,
                  small_d, small_t, gain_d, gain_t, gain_acc, bc_src, bc_buf,
-                 load_sem, near_sem, far_sem, in_sem, out_sem, small_sem_d, small_sem_t, gain_sem_d, gain_sem_t, bc_sem):
+                 load_sem, near_sem, far_sem, small_sem_d, small_sem_t, gain_sem_d, gain_sem_t, bc_sem, *row_sums):
     z, y, x, c = _place()
-    me = _peer(z, y, x, c)
     t = x * 2 + c
     own_rows, model = d_local.shape
     block, cols = owned.shape
@@ -987,15 +1079,11 @@
         return _remote(far_src.at[at, :], far_buf.at[at, :], far_sem.at[0, part], far_sem.at[1, part],
                        _peer(z, y, 1 - x, c))
 
-    def in_copy(k, zz, part):
-        at = pl.ds(part * bsize, bsize)
-        return _remote(g_all.at[zz, 1 - y, at, :], in_buf.at[k, at, :], in_sem.at[0, k, part], in_sem.at[1, k, part],
-                       _peer(z, 1 - y, x, c))
-
-    def out_copy(k, part):
-        at = pl.ds(part * bsize, bsize)
-        return _remote(out_src.at[k - 1, at, :], out_buf.at[k - 1, at, :], out_sem.at[0, k - 1, part],
-                       out_sem.at[1, k - 1, part], _peer((z + k) % outer_n, y, x, c))
+    sums = _RowSums(
+        outer_n, block,
+        lambda slot, outer, inner, part: g_all.at[outer, inner, pl.ds(part * bsize, bsize), :],
+        lambda slot, outer, part: g_all[outer, y, pl.ds(part * bsize, bsize), :].astype(F32),
+        owned, *row_sums)
 
     def token_product(i, part):
         a, b = i // 2, i % 2
@@ -1014,7 +1102,11 @@
             d_local[at, :] = value
 
     def group(i):
-        grp = lax.rem(z // per_group + 1 + i, groups)
+        if per_group == 1:
+            r = lax.rem(1 + i // 2, sums.pairs)
+            grp = lax.rem(sums.h + r, sums.pairs) * 2 + (1 - sums.l) * (1 - i % 2) + sums.l * (i % 2)
+        else:
+            grp = lax.rem(z // per_group + 1 + i, groups)
         at = pl.ds(pl.multiple_of(grp * (2 * per_group * block), LANES), 2 * per_group * block)
         value = lax.dot_general(normed[:, at], rest[...], (((0,), (0,)), ((), ())), preferred_element_type=F32)
         for j in range(per_group):
@@ -1022,26 +1114,14 @@
             for yy in (0, 1):
                 first = (2 * j + yy) * block
                 g_all[zz, yy] = value[first : first + block, :].astype(BF)
-            k = lax.rem(zz - z + outer_n, outer_n)
             for part in range(wparts):
-                in_copy(k, zz, part).start()
+                sums.in_copy(sums.slot_of(zz), zz, part).start()
 
     def token_step(part):
         at = pl.ds(part * size, size)
         near_copy(0, part).wait_recv()
         far_src[at, :] = (tok[1, at, :].astype(F32) + near_buf[0, at, :].astype(F32)).astype(BF)
         far_copy(part).start()
-
-    def grad_step(k, part):
-        at = pl.ds(part * bsize, bsize)
-        zz = lax.rem(z + k, outer_n)
-        in_copy(k, zz, part).wait_recv()
-        both = g_all[zz, y, at, :].astype(F32) + in_buf[k, at, :].astype(F32)
-        if k:
-            out_src[k - 1, at, :] = both.astype(BF)
-            out_copy(k, part).start()
-        else:
-            owned[at, :] = both
 
     small_d[0] = small[...]
     first = dp_copies(small, small_d, small_sem_d)
@@ -1051,9 +1131,8 @@
         copy.wait()
     gain_acc[...] = jnp.zeros_like(gain_acc)
     parts_half = PARTS // 2
-    order = list(range(1, outer_n)) + [0]
-    todo = [(k, part) for k in order for part in range(wparts)]
-    cut = lambda eighths: todo[: eighths * len(todo) // 8]
+    todo = sums.todo()
+    cut = lambda eighths: todo[: eighths * len(todo) // 8] if per_group == 1 or eighths == 8 else []
     per_slot = -(-groups // 4)
     second = tensor_copies(small_t.at[0], small_t, small_sem_t)
 
@@ -1066,8 +1145,8 @@
             token_step(part)
 
     def grads_between(low, high):
-        for k, part in cut(high)[len(cut(low)) :]:
-            grad_step(k, part)
+        for item in cut(high)[len(cut(low)) :]:
+            sums.step(*item)
 
     def small_second():
         for copy in first:
@@ -1132,13 +1211,7 @@
     grads_between(7, 8)
     for part in range(parts_half, PARTS):
         token_finish(part)
-    for part in range(wparts):
-        at = pl.ds(part * bsize, bsize)
-        total = owned[at, :]
-        for k in order[:-1]:
-            out_copy(k, part).wait_recv()
-            total = total + out_buf[k - 1, at, :].astype(F32)
-        owned[at, :] = total
+    sums.finish()
     bc_rows = block // 4
     for i in range(4):
         bc_src[i] = owned[i * bc_rows : (i + 1) * bc_rows, width : width + 2 * LANES]
@@ -1163,12 +1236,7 @@
         near_copy(0, part).wait_send()
         near_copy(1, part).wait_send()
         far_copy(part).wait_send()
-    for k in range(outer_n):
-        zz = lax.rem(z + k, outer_n)
-        for part in range(wparts):
-            in_copy(k, zz, part).wait_send()
-            if k:
-                out_copy(k, part).wait_send()
+    sums.wait_sends()
     for copy in first + second + gain_first + gain_second + bc_copies:
         copy.wait_send()
 
@@ -1199,14 +1267,12 @@
                         pltpu.VMEM((outer_n, 2, block, cols), BF),
                         pltpu.VMEM((3,) + tokens, BF), pltpu.VMEM((2,) + tokens, BF),
                         pltpu.VMEM(tokens, BF), pltpu.VMEM(tokens, BF),
-                        pltpu.VMEM((outer_n, block, cols), BF),
-                        pltpu.VMEM((outer_n - 1, block, cols), BF), pltpu.VMEM((outer_n - 1, block, cols), BF),
                         pltpu.VMEM((dp,) + small.shape, F32), pltpu.VMEM((4, both_rows, LANES), F32),
                         pltpu.VMEM((dp, gain_pad, LANES), F32), pltpu.VMEM((4, gain_pad, LANES), F32),
                         pltpu.VMEM((8, model), F32), pltpu.VMEM(bc, F32), pltpu.VMEM((3,) + bc[1:], F32),
-                        dma((4,)), dma((2, 2, PARTS)), dma((2, PARTS)), dma((2, outer_n, wparts)),
-                        dma((2, outer_n - 1, wparts)), dma((2, dp - 1)), dma((2, 3)), dma((2, dp - 1)), dma((2, 3)),
-                        dma((2, 3))],
+                        dma((4,)), dma((2, 2, PARTS)), dma((2, PARTS)),
+                        dma((2, dp - 1)), dma((2, 3)), dma((2, dp - 1)), dma((2, 3)),
+                        dma((2, 3))] + row_sums_scratch(outer_n, (block, cols)),
         compiler_params=pltpu.CompilerParams(collective_id=1, has_side_effects=True, vmem_limit_bytes=63 * 2**20),
         cost_estimate=pl.CostEstimate(flops=20 * 10**9, bytes_accessed=40 * 2**20, transcendentals=0),
         name="final_sums",

time: 354 us -> 344 us (0.972)
  Pallas kernels: 314 us -> 303 us
    pallas_call x1, Pallas kernels: 66.3 us -> 59.6 us  [final_sums(): pl.pallas_call(functools.partial(final_kernel, outer_n, both_rows, gain_r...]
where the time goes in v4:
time: 344 us; the launch traced here: 343 us
  Pallas kernels  303 us (88%)
  local copies, waits for them, and re-layouts  23.8 us (7%)
  other arithmetic  15.1 us (4%)
    pallas_call x1, Pallas kernels, gather_all(): pl.pallas_call(functools.partial(gather_kernel, outer_n, heads), in_specs...  122 us
    pallas_call x1, Pallas kernels, ssd_backward(): pl.pallas_call(functools.partial(backward_kernel, width, dp // 2), grid=(...  63.6 us
    pallas_call x1, Pallas kernels, final_sums(): pl.pallas_call(functools.partial(final_kernel, outer_n, both_rows, gain_r...  59.6 us
    pallas_call x1, Pallas kernels, middle(): pl.pallas_call(functools.partial(middle_kernel, width, inner_channels), g...  29.4 us
    pallas_call x1, Pallas kernels, ssd_forward(): pl.pallas_call(functools.partial(forward_kernel, width), grid=(length //...  28.6 us
    unnamed x21, local copies, waits for them, and re-layouts  8.03 us

profile of v4, /device:TPU:0, one launch (start us, length us, event | category | flops | bytes accessed | tf_op | source)
XLA Modules:
  0.0 342.8 jit_solution(4864531555024123551)
XLA Ops:
  0.7 0.9 dynamic_update_slice.11
  1.5 0.7 broadcast_in_dim.29
  2.2 0.7 stack.27
  2.9 1.3 select_maximum_fusion.6.head_ref
  4.2 0.8 dynamic_update_slice.10
  5.0 1.3 pad.33.wdt
  6.3 0.7 broadcast_in_dim.30
  7.1 0.8 dynamic_update_slice.9
  8.5 1.3 select_maximum_fusion.1
  9.9 1.9 copy.34
  11.8 121.9 %gather_all.1 = (f32[24,128]{1,0:T(8,128)}, f32[512,128]{1,0:T(8,128)}, bf16[2048,1536]{1,0:T(8,128)(2,1)}, bf16[2048,1536]{1,0:T(8,128)(2,1)}, bf16[1536,1920]{...) custom-call(f32[24,128]{1,0:T(8,128)} %select_maximum_fusion.3.small, ...), custom_call_target="tpu_custom_call" | custom-call | flops 16999999488 | bytes 62914560 | tf_op jit(solution)/shard_map/gather_all/pallas_call | solution.py:1010
  133.7 0.7 slice.66
  134.4 1.1 slice_reduce_fusion
  135.5 0.7 slice.65
  136.8 0.7 slice_bitcast_fusion.4
  137.5 28.6 %scan_forward.1 = (f32[2048,768]{1,0:T(8,128)}, f32[16,128,768]{2,1,0:T(8,128)}, f32[32,128]{1,0:T(8,128)}) custom-call(f32[2048,1920]{1,0:T(8,128)} %get-tuple-element.41.p_ref.z_ref.prev_ref, f32[2048,768]{1,0:T(8,128)} %get-tuple-element.42.dg_ref, f32[8,768]{1,0:T(8,128)} %get-tuple-element.105.convx_ref, f32[8,256]{1,0:T(8,128)} %select_maximum_fusion.5.convbc_ref, ...), custom_call_target="tpu_custom_call" | custom-call | flops 4000000000 | bytes 31457280 | tf_op jit(solution)/shard_map/scan_forward/pallas_call | solution.py:581
  166.1 29.4 %middle.1 = (bf16[2048,768]{1,0:T(8,128)(2,1)}, bf16[2048,768]{1,0:T(8,128)(2,1)}, bf16[2048,1536]{1,0:T(8,128)(2,1)}, bf16[1536,1536]{1,0:T(8,128)(2,1)}, f32[8,768]{1,0:T(8,128)}) custom-call(f32[2048,1920]{1,0:T(8,128)} %get-tuple-element.41.p_ref.z_ref.prev_ref, f32[2048,768]{1,0:T(8,128)} %get-tuple-element.44.y_ref, ...), custom_call_target="tpu_custom_call" | custom-call | flops 15000000512 | bytes 52428800 | tf_op jit(solution)/shard_map/middle/pallas_call | solution.py:699
  195.5 63.6 %scan_backward.1 = (bf16[2048,1152]{1,0:T(8,128)(2,1)}, f32[6,8,768]{2,1,0:T(8,128)}, f32[5,8,256]{2,1,0:T(8,128)}, f32[2,8,128]{2,1,0:T(8,128)}, f32[512,1536]{1,0:T(8,128)}, /*index=5*/f32[192,1536]{1,0:T(8,128)}) custom-call(f32[2048,1920]{1,0:T(8,128)} %get-tuple-element.41.p_ref.z_ref.prev_ref, f32[2048,1920]{1,0:T(8,128)} %get-tuple-element.41.p_ref.z_ref.prev_ref, ...), custom_call_target="tpu_custom_call" | custom-call | flops 12000000000 | bytes 52428800 | tf_op jit(solution)/shard_map/scan_backward/pallas_call | solution.py:618
  259.1 0.7 reduce_sum.57
  259.9 0.8 reduce_sum.54
  260.7 1.0 reduce_sum.55
  262.3 59.6 %final_sums.1 = (f32[512,1536]{1,0:T(8,128)}, f32[192,1152]{1,0:T(8,128)}, f32[72,128]{1,0:T(8,128)}, f32[48,256]{1,0:T(8,128)}) custom-call(bf16[2048,768]{1,0:T(8,128)(2,1)} %get-tuple-element.55.dz_in, bf16[2048,1152]{1,0:T(8,128)(2,1)} %get-tuple-element.56.rest_in, bf16[1536,1920]{1,0:T(8,128)(2,1)} %get-tuple-element.57.weight_in, ...), custom_call_target="tpu_custom_call" | custom-call | flops 20000000000 | bytes 41943040 | tf_op jit(solution)/shard_map/final_sums/pallas_call | solution.py:1257
  322.0 0.7 slice_bitcast_fusion.7
  323.2 1.3 slice_bitcast_fusion.8
  324.5 3.5 %multiply_reduce_fusion = f32[512]{0:T(512)S(1)} fusion(f32[512,1536]{1,0:T(8,128)} %get-tuple-element.62, f32[1536]{0:T(1024)S(1)} %slice_bitcast_fusion.4, f32[512]{0:T(512)S(1)} %slice_reduce_fusion, f32[1,512,1536]{2,1,0:T(8,128)} %param.15), kind=kLoop, calls=%fused_computation.1 | loop fusion | flops 3145216 | bytes 6301696 | tf_op jit(solution)/shard_map/reduce_sum | solution.py:1333
  328.2 1.0 copy-done.1
  329.2 4.5 %add_bitcast_fusion = f32[1,512,1536]{2,1,0:T(8,128)} fusion(f32[512,1536]{1,0:T(8,128)S(1)} %copy-done.1, f32[512]{0:T(512)S(1)} %broadcast_multiply_fusion, f32[1536]{0:T(1024)S(1)} %slice_bitcast_fusion.4, f32[512]{0:T(512)S(1)} %slice_reduce_fusion, f32[1,512,1536]{2,1,0:T(8,128)} %param.29, f32[1,512,1536]{2,1,0:T(8,128)S(1)} %copy-done), kind=kLoop, calls=%fused_computation | loop fusion | flops 4718592 | bytes 12593152 | tf_op jit(solution)/shard_map/broadcast_in_dim | solution.py:1345
  333.7 0.7 constant_dynamic-slice_fusion
  337.0 0.7 copy.33
  337.6 0.9 slice_bitcast_fusion
  338.6 1.9 copy.32
  340.5 1.7 copy.40
  (45 shorter events, 6.1 us)
Async XLA Ops:
  195.5 64.3 %copy-start.7 = (f32[8,768]{1,0:T(8,128)S(1)}, f32[8,768]{1,0:T(8,128)}, u32[]{:S(2)}) copy-start(f32[8,768]{1,0:T(8,128)} %get-tuple-element.60) | copy-start | bytes 73732
  324.5 3.7 %copy-start = (f32[1,512,1536]{2,1,0:T(8,128)S(1)}, f32[1,512,1536]{2,1,0:T(8,128)}, u32[]{:S(2)}) copy-start(f32[1,512,1536]{2,1,0:T(8,128)} %param.15) | copy-start | bytes 9437188
  324.5 4.7 %copy-start.1 = (f32[512,1536]{1,0:T(8,128)S(1)}, f32[512,1536]{1,0:T(8,128)}, u32[]{:S(2)}) copy-start(f32[512,1536]{1,0:T(8,128)} %get-tuple-element.62) | copy-start | bytes 9437188
  329.2 4.5 %copy-start.6 = (f32[72,128]{1,0:T(8,128)S(1)}, f32[72,128]{1,0:T(8,128)}, u32[]{:S(2)}) copy-start(f32[72,128]{1,0:T(8,128)} %get-tuple-element.63) | copy-start | bytes 110596
  329.2 7.7 %copy-start.4 = (f32[192,1152]{1,0:T(8,128)S(1)}, f32[192,1152]{1,0:T(8,128)}, u32[]{:S(2)}) copy-start(f32[192,1152]{1,0:T(8,128)} %get-tuple-element.65) | copy-start | bytes 2654212
  329.2 8.4 %copy-start.3 = (f32[192,1536]{1,0:T(8,128)S(1)}, f32[192,1536]{1,0:T(8,128)}, u32[]{:S(2)}) copy-start(f32[192,1536]{1,0:T(8,128)} %get-tuple-element.64) | copy-start | bytes 3538948
  337.6 2.9 copy-start.2
  340.5 1.7 copy-start.5
